TPU v7x, 128 devices: a whole 4x4x4 slice. The times are simulated.
128 devices in a mesh: op: 32 (over z_lo, x, y), sector: 4 (over z_hi, core).
Axes of the slice: x: 4, y: 4, z: 4 (z_hi: 2, z_lo: 2; z = z_hi * 2 + z_lo), core: 2. Of those that a mesh axis runs over, the one named last changes fastest.
Arguments:
- wavefunction: bfloat16 [8, 512, 512], P('sector'), may hold values from -10 to 10
- left_blocks: bfloat16 [128, 8, 512, 512], P('op', 'sector'), may hold values from -1 to 1
- right_blocks: bfloat16 [128, 8, 512, 512], P('op', 'sector'), may hold values from -1 to 1
- target_sector: int32 [128, 8], P('op', 'sector'), may hold values from 0 to 7, as said below
- preconditioner: float32 [8, 512, 512], P('sector', 'op'), may hold values from 1 to 10
Outputs:
- sigma_first: float32 [8, 512, 512], P('sector', 'op')
- sigma_second: float32 [8, 512, 512], P('sector', 'op')
Inputs may be any that keep to these rules, and one draw needn't show every extreme that they name: `target_sector`: sector t belongs to index t // 2 of sector. Among the 4 x 2 pairs (k, s) that one device holds, at most 3 have targets belonging to one index of sector, and on every device some index of sector gets exactly 3.
All inputs are finite; a program needn't handle non-finite values.
Results may differ from a plain program's by a relative error of at most 0.0034.
Values may be sent and summed in bfloat16 or wider, within the bound.
No kernel may reach another device: no remote copies, remote signals or barrier semaphores. Data moves between devices by JAX's collectives and lax.ppermute only.
A program may use at most 64 MiB of HBM per device.

v0:
```python
import functools

import jax
import jax.numpy as jnp
from jax import lax
from jax.sharding import Mesh
from jax.sharding import PartitionSpec as P

SECTOR = ("sector_0", "sector_1")
OP = ("op_0", "op_1", "op_2")
OP_SECTOR = ("op_0", "op_1", "op_2", "sector_0", "sector_1")


def split_up(value, dim, count):
    before, after = (value.shape[:dim], value.shape[dim + 1 :])
    return jnp.moveaxis(value.reshape(*before, count, -1, *after), dim, 0)


def sum_at_owner(value, axis, dim):
    pieces = split_up(value, dim, lax.axis_size(axis))
    arrived = lax.all_to_all(pieces, axis, split_axis=0, concat_axis=0, tiled=True)
    return arrived.sum(axis=0)


def one_axis_at_a_time(value, axes):
    return functools.reduce(lax.psum, axes, value)


def laid_out(pieces, dim):
    dims = list(pieces.shape[1:])
    dims[dim] *= pieces.shape[0]
    return jnp.moveaxis(pieces, 0, dim).reshape(dims)


def sent_to_all(value, axis):
    copies = jnp.broadcast_to(value, (lax.axis_size(axis), *value.shape))
    return lax.all_to_all(copies, axis, split_axis=0, concat_axis=0, tiled=True)


def gathered_copies(value, axis, dim):
    return laid_out(sent_to_all(value, axis), dim)


def apply_terms(left_blocks, right_blocks, target_sector, vector, sector_count):
    term_count, local_sectors = target_sector.shape
    block_width = vector.shape[1]

    def one_task(task_index, totals):
        term_index = task_index // local_sectors
        sector_index = task_index % local_sectors
        middle = jnp.dot(
            left_blocks[term_index, sector_index],
            vector[sector_index],
            preferred_element_type=jnp.float32,
        ).astype(jnp.bfloat16)
        contribution = lax.dot_general(
            middle,
            right_blocks[term_index, sector_index],
            (((1,), (1,)), ((), ())),
            preferred_element_type=jnp.float32,
        )
        target = target_sector[term_index, sector_index]
        current = lax.dynamic_index_in_dim(totals, target, 0, keepdims=False)
        return lax.dynamic_update_index_in_dim(totals, current + contribution, target, 0)

    initial = jnp.zeros((sector_count, block_width, block_width), jnp.float32)
    return lax.fori_loop(0, term_count * local_sectors, one_task, initial)


def reduce_terms(partial_sums):
    across = lax.psum_scatter(partial_sums, SECTOR, scatter_dimension=0, tiled=True)
    return sum_at_owner(across, OP, 1)


def on_device(wavefunction, left_blocks, right_blocks, target_sector, preconditioner):
    local_sectors = wavefunction.shape[0]
    sector_count = local_sectors * lax.axis_size(SECTOR)
    row_count = preconditioner.shape[1]
    offset = lax.axis_index(OP) * row_count
    sigma_first = reduce_terms(
        apply_terms(left_blocks, right_blocks, target_sector, wavefunction, sector_count)
    )
    own_rows = lax.dynamic_slice_in_dim(wavefunction, offset, row_count, 1).astype(jnp.float32)
    norm_sq, correlation = (
        one_axis_at_a_time(jnp.sum(own_rows * own_rows), OP_SECTOR),
        one_axis_at_a_time(jnp.sum(own_rows * sigma_first), OP_SECTOR),
    )
    rayleigh = correlation / norm_sq
    correction = (sigma_first - (rayleigh - 1.0) * own_rows) / preconditioner
    projected, correction_sq = (
        one_axis_at_a_time(jnp.sum(own_rows * correction), OP_SECTOR),
        one_axis_at_a_time(jnp.sum(correction * correction), OP_SECTOR),
    )
    update = correction - projected / norm_sq * own_rows
    update_sq = correction_sq - projected * projected / norm_sq
    new_rows = (update * jnp.sqrt(norm_sq) * lax.rsqrt(update_sq + 1e-06)).astype(jnp.bfloat16)
    new_vector = gathered_copies(new_rows, OP, 1)
    sigma_second = reduce_terms(
        apply_terms(left_blocks, right_blocks, target_sector, new_vector, sector_count)
    )
    return (sigma_first, sigma_second)


def solution(mesh):
    torus = Mesh(
        mesh.devices.reshape(2, 4, 4, 2, 2), ("op_0", "op_1", "op_2", "sector_0", "sector_1")
    )
    placed = (
        P(SECTOR, None, None),
        P(OP, SECTOR, None, None),
        P(OP, SECTOR, None, None),
        P(OP, SECTOR),
        P(SECTOR, OP, None),
    )
    return jax.shard_map(
        on_device,
        mesh=torus,
        in_specs=placed,
        out_specs=(P(SECTOR, OP, None), P(SECTOR, OP, None)),
        check_vma=False,
    )
```

profile of v0, /device:TPU:0, one launch (start us, length us, event | category | flops | bytes accessed | tf_op | source)
XLA Modules:
  0.0 462.6 jit_solution(14131422853348740566)
XLA Ops:
  7.2 4.3 broadcast.7.clone
  11.5 54.0 %while.30 = (s32[]{:T(128)}, f32[8,512,512]{2,1,0:T(8,128)}, s32[4,2]{0,1:T(2,128)S(1)}, bf16[4,2,512,512]{3,2,1,0:T(8,128)(2,1)}, bf16[2,512,512]{2,1,0:T(8,128...) while((s32[]{:T(128)}, f32[8,512,512]{2,1,0:T(8,128)}, ...), condition=%wide.region_1.2_spmd, body=%wide.region_0.1_spmd.sunk | while | flops 537395200 | bytes 5770590 | solution.py:67
  11.5 0.6 dynamic_slice.155
  14.1 1.3 constant_dynamic-slice_fusion.4
  15.4 2.9 fusion.49
  18.3 0.6 dynamic_slice.155
  20.8 1.3 constant_dynamic-slice_fusion.4
  22.1 3.0 fusion.49
  27.6 1.3 constant_dynamic-slice_fusion.4
  28.9 2.9 fusion.49
  34.3 1.3 constant_dynamic-slice_fusion.4
  35.6 2.9 fusion.49
  41.0 1.3 constant_dynamic-slice_fusion.4
  42.3 2.9 fusion.49
  45.3 0.6 dynamic_slice.155
  47.8 1.3 constant_dynamic-slice_fusion.4
  49.1 2.9 fusion.49
  52.0 0.6 dynamic_slice.155
  54.6 1.3 constant_dynamic-slice_fusion.4
  55.9 2.9 fusion.49
  58.8 0.6 dynamic_slice.155
  61.3 1.3 constant_dynamic-slice_fusion.4
  62.6 2.9 fusion.49
  65.6 81.0 %reduce-scatter.3.cloned.1.call-done = f32[2,512,512]{2,1,0:T(8,128)} async-done(((f32[8,512,512]{2,1,0:T(8,128)}), f32[2,512,512]{2,1,0:T(8,128)}) %reduce-scatter.3.cloned.1.call-update) | async-done | bytes 2097168 | tf_op jit(solution)/shard_map/reduce_scatter | solution.py:71
  146.6 3.3 copy.7
  149.9 7.3 %all-to-all-start = ((f32[32,2,16,512]{3,2,1,0:T(8,128)}), f32[32,2,16,512]{3,2,1,0:T(8,128)S(1)}, u32[]{:S(2)}, u32[]{:S(2)}) async-start(f32[32,2,16,512]{3,2,1,0:T(8,128)} %copy.7), calls=%async_computation.1 | async-start | bytes 4194304 | tf_op jit(solution)/shard_map/all_to_all | solution.py:21
  157.2 28.0 %all-to-all-done = f32[32,2,16,512]{3,2,1,0:T(8,128)S(1)} async-done(((f32[32,2,16,512]{3,2,1,0:T(8,128)}), f32[32,2,16,512]{3,2,1,0:T(8,128)S(1)}, u32[]{:S(2)}, u32[]{:S(2)}) %all-to-all-start) | async-done | bytes 2097184 | tf_op jit(solution)/shard_map/all_to_all | solution.py:21
  185.3 0.6 fusion.29
  185.9 5.6 %all-reduce.9 = (f32[]{:T(128)}, f32[]{:T(128)}) all-reduce(f32[]{:T(128)} %get-tuple-element.319, f32[]{:T(128)} %get-tuple-element.318), channel_id=1, replica_groups=mesh['op_0'=2,'op_1'=4,'op_2'=4,'sector_0'=2,'sector_1'=2] {'op_0'}, use_global_device_ids=true, to_apply=%region_5.6 | all-reduce | flops 2 | bytes 16 | tf_op jit(solution)/shard_map/psum | solution.py:26
  191.6 11.0 %all-reduce.3 = (f32[]{:T(128)}, f32[]{:T(128)}) all-reduce(f32[]{:T(128)} %get-tuple-element.364, f32[]{:T(128)} %get-tuple-element.365), channel_id=1, replica_groups=mesh['op_0'=2,'op_1'=4,'op_2'=4,'sector_0'=2,'sector_1'=2] {'op_1'}, use_global_device_ids=true, to_apply=%region_6.7 | all-reduce | flops 2 | bytes 16 | tf_op jit(solution)/shard_map/psum | solution.py:26
  202.5 10.5 %all-reduce.1 = (f32[]{:T(128)}, f32[]{:T(128)}) all-reduce(f32[]{:T(128)} %get-tuple-element.352, f32[]{:T(128)} %get-tuple-element.353), channel_id=1, replica_groups=mesh['op_0'=2,'op_1'=4,'op_2'=4,'sector_0'=2,'sector_1'=2] {'op_2'}, use_global_device_ids=true, to_apply=%region_7.8 | all-reduce | flops 2 | bytes 16 | tf_op jit(solution)/shard_map/psum | solution.py:26
  213.0 7.0 %all-reduce.7 = (f32[]{:T(128)}, f32[]{:T(128)}) all-reduce(f32[]{:T(128)} %get-tuple-element.348, f32[]{:T(128)} %get-tuple-element.349), channel_id=1, replica_groups=mesh['op_0'=2,'op_1'=4,'op_2'=4,'sector_0'=2,'sector_1'=2] {'sector_0'}, use_global_device_ids=true, to_apply=%region_8.9 | all-reduce | flops 2 | bytes 16 | tf_op jit(solution)/shard_map/psum | solution.py:26
  220.0 3.2 all-reduce.5
  224.6 0.7 fusion.32
  225.3 5.6 %all-reduce.8 = (f32[]{:T(128)}, f32[]{:T(128)}) all-reduce(f32[]{:T(128)} %get-tuple-element.321, f32[]{:T(128)} %get-tuple-element.320), channel_id=1, replica_groups=mesh['op_0'=2,'op_1'=4,'op_2'=4,'sector_0'=2,'sector_1'=2] {'op_0'}, use_global_device_ids=true, to_apply=%region_23.24 | all-reduce | flops 2 | bytes 16 | tf_op jit(solution)/shard_map/psum | solution.py:26
  230.9 8.4 %all-reduce.2 = (f32[]{:T(128)}, f32[]{:T(128)}) all-reduce(f32[]{:T(128)} %get-tuple-element.362, f32[]{:T(128)} %get-tuple-element.363), channel_id=1, replica_groups=mesh['op_0'=2,'op_1'=4,'op_2'=4,'sector_0'=2,'sector_1'=2] {'op_1'}, use_global_device_ids=true, to_apply=%region_24.25 | all-reduce | flops 2 | bytes 16 | tf_op jit(solution)/shard_map/psum | solution.py:26
  239.3 8.4 %all-reduce = (f32[]{:T(128)}, f32[]{:T(128)}) all-reduce(f32[]{:T(128)} %get-tuple-element.350, f32[]{:T(128)} %get-tuple-element.351), channel_id=1, replica_groups=mesh['op_0'=2,'op_1'=4,'op_2'=4,'sector_0'=2,'sector_1'=2] {'op_2'}, use_global_device_ids=true, to_apply=%region_25.26 | all-reduce | flops 2 | bytes 16 | tf_op jit(solution)/shard_map/psum | solution.py:26
  247.8 7.1 %all-reduce.6 = (f32[]{:T(128)}, f32[]{:T(128)}) all-reduce(f32[]{:T(128)} %get-tuple-element.346, f32[]{:T(128)} %get-tuple-element.347), channel_id=1, replica_groups=mesh['op_0'=2,'op_1'=4,'op_2'=4,'sector_0'=2,'sector_1'=2] {'sector_0'}, use_global_device_ids=true, to_apply=%region_26.27 | all-reduce | flops 2 | bytes 16 | tf_op jit(solution)/shard_map/psum | solution.py:26
  254.9 3.2 all-reduce.4
  262.5 1.1 broadcast_in_dim.24
  263.7 5.1 %all-to-all-start.1 = ((bf16[32,2,16,512]{3,2,1,0:T(8,128)(2,1)}), bf16[32,2,16,512]{3,2,1,0:T(8,128)(2,1)S(1)}, u32[]{:S(2)}, u32[]{:S(2)}) async-start(bf16[32,2,16,512]{3,2,1,0:T(8,128)(2,1)} %broadcast_in_dim.24), calls=%async_computation.2 | async-start | bytes 2097152 | tf_op jit(solution)/shard_map/all_to_all | solution.py:37
  268.8 17.0 %all-to-all-done.1 = bf16[32,2,16,512]{3,2,1,0:T(8,128)(2,1)S(1)} async-done(((bf16[32,2,16,512]{3,2,1,0:T(8,128)(2,1)}), bf16[32,2,16,512]{3,2,1,0:T(8,128)(2,1)S(1)}, u32[]{:S(2)}, u32[]{:S(2)}) %all-to-all-start.1) | async-done | bytes 1048608 | tf_op jit(solution)/shard_map/all_to_all | solution.py:37
  285.9 4.3 broadcast.7
  290.2 51.9 %while.31 = (s32[]{:T(128)}, f32[8,512,512]{2,1,0:T(8,128)}, s32[4,2]{0,1:T(2,128)S(1)}, bf16[4,2,512,512]{3,2,1,0:T(8,128)(2,1)}, bf16[2,512,512]{2,1,0:T(8,128...) while((s32[]{:T(128)}, f32[8,512,512]{2,1,0:T(8,128)}, ...), condition=%wide.region_29.30_spmd, body=%wide.region_28.29_spmd.sunk | while | flops 537395200 | bytes 5770590 | solution.py:67
  292.4 1.3 constant_dynamic-slice_fusion.5
  293.7 2.9 fusion.53
  298.9 1.3 constant_dynamic-slice_fusion.5
  300.2 3.0 fusion.53
  305.4 1.3 constant_dynamic-slice_fusion.5
  306.7 2.9 fusion.53
  311.9 1.3 constant_dynamic-slice_fusion.5
  313.2 2.9 fusion.53
  318.4 1.3 constant_dynamic-slice_fusion.5
  319.7 2.9 fusion.53
  324.9 1.3 constant_dynamic-slice_fusion.5
  326.2 2.9 fusion.53
  331.4 1.3 constant_dynamic-slice_fusion.5
  332.7 2.9 fusion.53
  337.9 1.3 constant_dynamic-slice_fusion.5
  339.2 2.9 fusion.53
  342.1 76.2 %reduce-scatter.5.cloned.1.call-done = f32[2,512,512]{2,1,0:T(8,128)} async-done(((f32[8,512,512]{2,1,0:T(8,128)}), f32[2,512,512]{2,1,0:T(8,128)}) %reduce-scatter.5.cloned.1.call-update) | async-done | bytes 2097168 | tf_op jit(solution)/shard_map/reduce_scatter | solution.py:71
  418.3 1.8 copy.9
  420.1 34.8 %all_to_all.15 = f32[32,2,16,512]{3,2,1,0:T(8,128)S(1)} all-to-all(f32[32,2,16,512]{3,2,1,0:T(8,128)S(1)} %copy.9), channel_id=1, replica_groups=mesh['op_0'=2,'op_1'=4,'op_2'=4,'sector_0'=2,'sector_1'=2] {'op_0','op_1..., dimensions={0} | all-to-all | bytes 4194304 | tf_op jit(solution)/shard_map/all_to_all | solution.py:21
  455.0 0.8 reduce_sum.59
  (26 shorter events, 6.6 us)
Async XLA Ops:
  7.2 139.4 %reduce-scatter.3.cloned.1.call-start = ((), (), s32[]{:S(2)}) async-start(), calls=%async_computation.5 | async-start | bytes 10485760 | tf_op jit(solution)/shard_map/reduce_scatter | solution.py:71
  7.2 4.3 copy-start
  7.2 4.3 copy-start.3
  149.8 74.7 %copy-start.2 = (f32[2,16,512]{2,1,0:T(8,128)S(1)}, f32[2,16,512]{2,1,0:T(8,128)}, u32[]{:S(2)}) copy-start(f32[2,16,512]{2,1,0:T(8,128)} %param.13) | copy-start | bytes 196612
  149.9 35.3 %all-to-all-start = ((f32[32,2,16,512]{3,2,1,0:T(8,128)}), f32[32,2,16,512]{3,2,1,0:T(8,128)S(1)}, u32[]{:S(2)}, u32[]{:S(2)}) async-start(f32[32,2,16,512]{3,2,1,0:T(8,128)} %copy.7), calls=%async_computation.1 | async-start | bytes 4194304 | tf_op jit(solution)/shard_map/all_to_all | solution.py:21
  185.3 104.9 %copy-start.1 = (f32[2,16,512]{2,1,0:T(8,128)}, f32[2,16,512]{2,1,0:T(8,128)S(1)}, u32[]{:S(2)}) copy-start(f32[2,16,512]{2,1,0:T(8,128)S(1)} %reduce_sum.54) | copy-start | bytes 196612
  263.7 22.1 %all-to-all-start.1 = ((bf16[32,2,16,512]{3,2,1,0:T(8,128)(2,1)}), bf16[32,2,16,512]{3,2,1,0:T(8,128)(2,1)S(1)}, u32[]{:S(2)}, u32[]{:S(2)}) async-start(bf16[32,2,16,512]{3,2,1,0:T(8,128)(2,1)} %broadcast_in_dim.24), calls=%async_computation.2 | async-start | bytes 2097152 | tf_op jit(solution)/shard_map/all_to_all | solution.py:37
  268.8 149.5 %reduce-scatter.5.cloned.1.call-start = ((), (), s32[]{:S(2)}) async-start(), calls=%async_computation.6 | async-start | bytes 10485760 | tf_op jit(solution)/shard_map/reduce_scatter | solution.py:71
Sparse Core Ops, SparseCore 0:
  65.7 80.8 reduce-scatter.2
  342.2 76.0 reduce-scatter.4
where the time goes:
time: 465 us; the launch traced here: 463 us
  waiting for transfers between devices  202 us (43%)
  blocking collectives  105 us (23%)
  matrix products  46.7 us (10%)
  local copies, waits for them, and re-layouts  44.8 us (10%)
  loops' own time  29.3 us (6%)
  between operations  20 us (4%)
  starting transfers between devices  12.5 us (3%)
    reduce_scatter x2, waiting for transfers between devices, reduce_terms(): lax.psum_scatter(partial_sums, SECTOR, scatter_dimension=0, tiled=True)  157 us
    psum x10, blocking collectives, one_axis_at_a_time(): return functools.reduce(lax.psum, axes, value)  70 us
    dot_general x16, matrix products, one_task(): lax.dot_general(middle, right_blocks[term_index, sector_index], (((1,), (...  46.7 us
    all_to_all x1, blocking collectives, sum_at_owner(): lax.all_to_all(pieces, axis, split_axis=0, concat_axis=0, tiled=True)  34.8 us
    another operation x2, loops' own time, apply_terms(): return lax.fori_loop(0, term_count * local_sectors, one_task, initial)  29.3 us
    all_to_all x1, waiting for transfers between devices, sum_at_owner(): lax.all_to_all(pieces, axis, split_axis=0, concat_axis=0, tiled=True)  28 us
    dynamic_slice x16, local copies, waits for them, and re-layouts, one_task(): current = lax.dynamic_index_in_dim(totals, target, 0, keepdims=False)  20.8 us
    all_to_all x1, waiting for transfers between devices, sent_to_all(): return lax.all_to_all(copies, axis, split_axis=0, concat_axis=0, tiled=True)  17 us
  transfers between devices with their start and end apart: 4, of which 4 were waited for; matrix products, arithmetic and copies ran while one was open for 0% of the time, Pallas kernels for 0%

commit v1 on v0

v1 whole, which is shorter than its diff:
```python
import functools

import jax
import jax.numpy as jnp
from jax import lax
from jax.experimental import pallas as pl
from jax.experimental.pallas import tpu as pltpu
from jax.sharding import Mesh
from jax.sharding import PartitionSpec as P

SECTOR = ("sector_0", "sector_1")
OP = ("op_0", "op_1", "op_2")
CHIPS = ("op_0", "op_1", "op_2", "sector_0")
EVERY = ("op_0", "op_1", "op_2", "sector_0", "sector_1")
CORE = "sector_1"
F32 = jnp.float32
BF16 = jnp.bfloat16
VMEM = pl.BlockSpec(memory_space=pltpu.VMEM)
SMEM = pl.BlockSpec(memory_space=pltpu.SMEM)
HBM = pl.BlockSpec(memory_space=pltpu.HBM)


def room(mebibytes):
    return pltpu.CompilerParams(vmem_limit_bytes=mebibytes * 2**20)


def exchange(pieces, axis):
    return lax.all_to_all(pieces, axis, split_axis=0, concat_axis=0, tiled=True)


def wanted(targets, core, local_sectors, task):
    return lax.rem(targets[task] // local_sectors, 2) == core[0]


def all_tasks(targets, core, local_sectors, vector, lefts, rights, totals, arrive):
    tasks, width, _ = lefts.shape
    totals[...] = jnp.zeros_like(totals)

    def one_task(task, carry):
        @pl.when(wanted(targets, core, local_sectors, task))
        def _():
            arrive(task)
            sector = lax.rem(task, local_sectors)
            source = vector[sector] if vector.shape[1] == width else vector[:, sector]
            source = source.reshape(width, width)
            middle = jnp.dot(lefts[task], source, preferred_element_type=F32).astype(BF16)
            target = targets[task]
            slot = target // (2 * local_sectors) * local_sectors + lax.rem(target, local_sectors)
            totals[slot] += lax.dot_general(
                middle, rights[task], (((1,), (1,)), ((), ())), preferred_element_type=F32
            )

        return carry

    lax.fori_loop(0, tasks, one_task, 0)


def loading_kernel(local_sectors, targets, core, vector, left, right, totals, lefts, rights, sems):

    def copies(task):
        return (
            pltpu.make_async_copy(left.at[task], lefts.at[task], sems.at[0, task]),
            pltpu.make_async_copy(right.at[task], rights.at[task], sems.at[1, task]),
        )

    def start(task, carry):
        @pl.when(wanted(targets, core, local_sectors, task))
        def _():
            for copy in copies(task):
                copy.start()

        return carry

    def arrive(task):
        for copy in copies(task):
            copy.wait()

    lax.fori_loop(0, left.shape[0], start, 0)
    all_tasks(targets, core, local_sectors, vector, lefts, rights, totals, arrive)


def resident_kernel(local_sectors, targets, core, vector, lefts, rights, totals):
    all_tasks(targets, core, local_sectors, vector, lefts, rights, totals, lambda task: None)


def apply_terms(targets, core, vector, left, right, loading):
    tasks, width, _ = left.shape
    slots = tasks // 2
    total = jax.ShapeDtypeStruct((slots, width, width), F32)
    cost = pl.CostEstimate(
        flops=2 * tasks * width**3, bytes_accessed=2 * tasks * width**2, transcendentals=0
    )
    if loading:
        return pl.pallas_call(
            functools.partial(loading_kernel, slots // 2),
            out_shape=total,
            in_specs=[SMEM, SMEM, VMEM, HBM, HBM],
            out_specs=VMEM,
            scratch_shapes=[
                pltpu.VMEM(left.shape, BF16),
                pltpu.VMEM(left.shape, BF16),
                pltpu.SemaphoreType.DMA((2, tasks)),
            ],
            compiler_params=room(47),
            cost_estimate=cost,
            name="loading",
        )(targets, core, vector, left, right)
    return pl.pallas_call(
        functools.partial(resident_kernel, slots // 2),
        out_shape=total,
        in_specs=[SMEM, SMEM, VMEM, VMEM, VMEM],
        out_specs=VMEM,
        compiler_params=room(4),
        cost_estimate=cost,
        name="resident",
    )(targets, core, vector, left, right)


def pack_kernel(kept, arrived, packed):
    slots, width, _ = kept.shape
    owners, halves, local_sectors, rows, _ = packed.shape
    for slot in range(slots):

        def one_owner(owner, carry, slot=slot):
            here = pl.ds(pl.multiple_of(owner * rows, rows), rows)
            total = kept[slot, here, :] + arrived[slot, here, :]
            packed[owner, slot // local_sectors, slot % local_sectors] = total.astype(BF16)
            return carry

        lax.fori_loop(0, owners, one_owner, 0, unroll=4)


def pack(kept, arrived, owners):
    slots, width, _ = kept.shape
    return pl.pallas_call(
        pack_kernel,
        out_shape=jax.ShapeDtypeStruct((owners, 2, slots // 2, width // owners, width), BF16),
        in_specs=[VMEM, VMEM],
        out_specs=VMEM,
        compiler_params=room(4),
        name="pack",
    )(kept, arrived)


def summed(pieces):
    shape = pieces.shape[1:]
    count = pieces.shape[0]

    def add(index, total):
        return total + pieces[index].astype(F32)

    return lax.fori_loop(0, count, add, jnp.zeros(shape, F32), unroll=8)


def lanes(value):
    local_sectors, rows, width = value.shape
    flat = jnp.sum(value.reshape(local_sectors * rows, width), axis=0, keepdims=True)
    return sum(flat[:, at : at + 128] for at in range(0, width, 128))


def first_kernel(offset, pieces, wave, precond, sigma, sums):
    rows = precond.shape[1]
    own = wave[:, pl.ds(pl.multiple_of(offset[0], rows), rows), :].astype(F32)
    total = summed(pieces)
    sigma[...] = total
    ratio, scaled = total / precond[...], own / precond[...]
    terms = (
        own * own,
        own * total,
        own * ratio,
        own * scaled,
        ratio * ratio,
        ratio * scaled,
        scaled * scaled,
    )
    one = jnp.concatenate([lanes(term) for term in terms] + [jnp.zeros((1, 128), F32)], axis=0)
    sums[...] = jnp.broadcast_to(one[None], sums.shape)


def second_kernel(offset, sums, sigma, wave, precond, copies):
    rows = precond.shape[1]
    own = wave[:, pl.ds(pl.multiple_of(offset[0], rows), rows), :].astype(F32)
    whole = jnp.sum(summed(sums), axis=1, keepdims=True)
    norm_sq, w_s, w_r, w_b, r_r, r_b, b_b = (whole[k : k + 1] for k in range(7))
    shift = w_s / norm_sq - 1.0
    projected = w_r - shift * w_b
    correction_sq = r_r - 2.0 * shift * r_b + shift * shift * b_b
    along = projected / norm_sq
    update_sq = correction_sq - projected * along
    scale = jnp.sqrt(norm_sq) * lax.rsqrt(update_sq + 1e-06)
    correction = (sigma[...] - shift[None] * own) / precond[...]
    new = ((correction - along[None] * own) * scale[None]).astype(BF16)
    copies[...] = jnp.broadcast_to(new[None], copies.shape)


def sum_kernel(pieces, sigma):
    sigma[...] = summed(pieces)


def on_device(wavefunction, left_blocks, right_blocks, target_sector, preconditioner):
    local_sectors, width, _ = wavefunction.shape
    rows = preconditioner.shape[1]
    owners = lax.axis_size(OP)
    offset = (lax.axis_index(OP) * rows).reshape(1)
    mine = lax.axis_index(CORE).reshape(1)
    targets = target_sector.reshape(-1)
    row_shape = jax.ShapeDtypeStruct((local_sectors, rows, width), F32)

    def partial_pieces(vector, left, right, loading):
        sent = apply_terms(targets, 1 - mine, vector, left, right, loading)
        arrived = lax.ppermute(sent, CORE, [(0, 1), (1, 0)])
        kept = apply_terms(targets, mine, vector, left, right, loading)
        packed = pack(kept, arrived, owners)
        pieces = packed.reshape(2 * owners, local_sectors, rows, width)
        return exchange(pieces, CHIPS)

    left, right = (
        blocks.reshape(-1, width, width) for blocks in (left_blocks, right_blocks)
    )
    pieces = partial_pieces(wavefunction, left, right, True)
    devices = lax.axis_size(EVERY)
    sigma_first, sums = pl.pallas_call(
        first_kernel,
        out_shape=(row_shape, jax.ShapeDtypeStruct((devices, 8, 128), F32)),
        in_specs=[SMEM, VMEM, VMEM, VMEM],
        out_specs=(VMEM, VMEM),
        compiler_params=room(4),
        name="first",
    )(offset, pieces, wavefunction, preconditioner)
    sums = exchange(sums, EVERY)
    copies = pl.pallas_call(
        second_kernel,
        out_shape=jax.ShapeDtypeStruct((owners, local_sectors, rows, width), BF16),
        in_specs=[SMEM, VMEM, VMEM, VMEM, VMEM],
        out_specs=VMEM,
        compiler_params=room(4),
        name="second",
    )(offset, sums, sigma_first, wavefunction, preconditioner)
    pieces = partial_pieces(exchange(copies, OP), left, right, False)
    sigma_second = pl.pallas_call(
        sum_kernel,
        out_shape=row_shape,
        in_specs=[VMEM],
        out_specs=VMEM,
        compiler_params=room(4),
        name="last",
    )(pieces)
    return (sigma_first, sigma_second)


def solution(mesh):
    torus = Mesh(mesh.devices.reshape(2, 4, 4, 2, 2), EVERY)
    placed = (
        P(SECTOR, None, None),
        P(OP, SECTOR, None, None),
        P(OP, SECTOR, None, None),
        P(OP, SECTOR),
        P(SECTOR, OP, None),
    )
    return jax.shard_map(
        on_device,
        mesh=torus,
        in_specs=placed,
        out_specs=(P(SECTOR, OP, None), P(SECTOR, OP, None)),
        check_vma=False,
    )
```

time: 465 us -> 150 us (0.32)
  waiting for transfers between devices: 202 us -> 35.8 us
  matrix products: 46.7 us -> 0 us
  local copies, waits for them, and re-layouts: 44.8 us -> 2.93 us
  blocking collectives: 105 us -> 75.1 us
  loops' own time: 29.3 us -> 0 us
  Pallas kernels: 0 us -> 22 us
  between operations: 20 us -> 0.73 us
    reduce_scatter x2 -> x0, waiting for transfers between devices: 157 us -> none  [reduce_terms(): lax.psum_scatter(partial_sums, SECTOR, scatter_dimension=0, tiled=True)]
    psum x10 -> x0, blocking collectives: 70 us -> none  [one_axis_at_a_time(): return functools.reduce(lax.psum, axes, value)]
    dot_general x16 -> x0, matrix products: 46.7 us -> none  [one_task(): lax.dot_general(middle, right_blocks[term_index, sector_index], (((1,), (...]
    all_to_all x1 -> x3, blocking collectives: 34.8 us -> 75.1 us  [exchange(): return lax.all_to_all(pieces, axis, split_axis=0, concat_axis=0, tiled=True)]
    dynamic_slice x32 -> x0, local copies, waits for them, and re-layouts: 29.9 us -> none  [the longest x16 20.8 us: one_task(): current = lax.dynamic_index_in_dim(totals, target, 0, keepdims=False)]
    another operation x2 -> x0, loops' own time: 29.3 us -> none  [apply_terms(): return lax.fori_loop(0, term_count * local_sectors, one_task, initial)]
    pallas_call x0 -> x9, Pallas kernels: none -> 22 us  [the longest x2 9.77 us: apply_terms(): pl.pallas_call(functools.partial(loading_kernel, slots // 2), out_shape=t...]
    all_to_all x2 -> x1, waiting for transfers between devices: 44.9 us -> 30.2 us  [exchange(): return lax.all_to_all(pieces, axis, split_axis=0, concat_axis=0, tiled=True)]
  transfers between devices with their start and end apart: 4 -> 3, of which waited for: 4 -> 3; matrix products, arithmetic and copies ran while one was open for 0% -> 0% of each run, Pallas kernels for 0% -> 6%
where the time goes in v1:
time: 150 us
  blocking collectives  75.1 us (50%)
  waiting for transfers between devices  35.8 us (24%)
  Pallas kernels  22 us (15%)
  starting transfers between devices  13.1 us (9%)
  local copies, waits for them, and re-layouts  2.93 us (2%)
    all_to_all x3, blocking collectives, exchange(): return lax.all_to_all(pieces, axis, split_axis=0, concat_axis=0, tiled=True)  75.1 us
    all_to_all x1, waiting for transfers between devices, exchange(): return lax.all_to_all(pieces, axis, split_axis=0, concat_axis=0, tiled=True)  30.2 us
    all_to_all x1, starting transfers between devices, exchange(): return lax.all_to_all(pieces, axis, split_axis=0, concat_axis=0, tiled=True)  12.9 us
    pallas_call x2, Pallas kernels, apply_terms(): pl.pallas_call(functools.partial(loading_kernel, slots // 2), out_shape=t...  9.77 us
    pallas_call x2, Pallas kernels, apply_terms(): pl.pallas_call(functools.partial(resident_kernel, slots // 2), out_shape=...  7.63 us
    ppermute x2, waiting for transfers between devices, partial_pieces(): arrived = lax.ppermute(sent, CORE, [(0, 1), (1, 0)])  5.56 us
  transfers between devices with their start and end apart: 3, of which 3 were waited for; matrix products, arithmetic and copies ran while one was open for 0% of the time, Pallas kernels for 6%

profile of v1, /device:TPU:0, one launch (start us, length us, event | category | flops | bytes accessed | tf_op | source)
XLA Modules:
  0.0 149.6 jit_solution(6556187695771732430)
XLA Ops:
  0.6 0.8 copy.8
  1.4 0.1 reshape.26.targets
  1.5 0.0 copy-start.2
  1.5 1.2 copy-done.2
  2.7 0.0 copy-start.3
  2.7 4.9 %loading.3 = f32[4,512,512]{2,1,0:T(8,128)S(1)} custom-call(s32[8]{0:T(128)S(1)} %reshape.26.targets, s32[1]{0:T(128)S(6)} %sub.4.core, bf16[2,512,512]{2,1,0:T(8,128)(2,1)S(1)} %copy-done.2, bf16[8,512,512]{2,1,0:T(8,128)(2,1)} %bitcast.6, bf16[8,512,512]{2,1,0:T(8,128)(2,1)} %bitcast.10), custom_call_target="tpu_custom_call" | custom-call | flops 2147483648 | bytes 4194304 | tf_op jit(solution)/shard_map/loading/pallas_call | solution.py:94
  7.6 0.1 collective-permute-start
  7.7 0.0 copy-done.3
  7.7 4.9 %loading.2.kept = f32[4,512,512]{2,1,0:T(8,128)S(1)} custom-call(s32[8]{0:T(128)S(1)} %reshape.26.targets, s32[1]{0:T(128)} %bitcast.1.core, bf16[2,512,512]{2,1,0:T(8,128)(2,1)S(1)} %copy-done.3, bf16[8,512,512]{2,1,0:T(8,128)(2,1)} %bitcast.7, bf16[8,512,512]{2,1,0:T(8,128)(2,1)} %bitcast.11), custom_call_target="tpu_custom_call" | custom-call | flops 2147483648 | bytes 4194304 | tf_op jit(solution)/shard_map/loading/pallas_call | solution.py:94
  12.6 2.2 %collective-permute-done.arrived = f32[4,512,512]{2,1,0:T(8,128)S(1)} collective-permute-done((f32[4,512,512]{2,1,0:T(8,128)S(1)}, f32[4,512,512]{2,1,0:T(8,128)S(1)}, u32[]{:S(2)}, u32[]{:S(2)}) %collective-permute-start) | collective-permute-done | bytes 4194336 | tf_op jit(solution)/shard_map/ppermute | solution.py:211
  14.8 1.9 %pack.2 = bf16[32,2,2,16,512]{4,3,2,1,0:T(8,128)(2,1)} custom-call(f32[4,512,512]{2,1,0:T(8,128)S(1)} %loading.2.kept, f32[4,512,512]{2,1,0:T(8,128)S(1)} %collective-permute-done.arrived), custom_call_target="tpu_custom_call" | custom-call | tf_op jit(solution)/shard_map/pack/pallas_call | solution.py:135
  16.7 0.0 copy-start.4
  16.7 12.9 %all-to-all-start = ((bf16[64,2,16,512]{3,2,1,0:T(8,128)(2,1)}), bf16[64,2,16,512]{3,2,1,0:T(8,128)(2,1)S(1)}, u32[]{:S(2)}, u32[]{:S(2)}) async-start(bf16[64,2,16,512]{3,2,1,0:T(8,128)(2,1)} %bitcast.4), calls=%async_computation | async-start | bytes 4194304 | tf_op jit(solution)/shard_map/all_to_all | solution.py:28
  29.6 30.2 %all-to-all-done.pieces = bf16[64,2,16,512]{3,2,1,0:T(8,128)(2,1)S(1)} async-done(((bf16[64,2,16,512]{3,2,1,0:T(8,128)(2,1)}), bf16[64,2,16,512]{3,2,1,0:T(8,128)(2,1)S(1)}, u32[]{:S(2)}, u32[]{:S(2)}) %all-to-all-start) | async-done | bytes 2097184 | tf_op jit(solution)/shard_map/all_to_all | solution.py:28
  59.9 0.0 copy-done.4
  59.9 0.0 copy-start
  59.9 0.0 copy-start.1
  59.9 0.9 first.1
  60.8 17.6 %all_to_all.20.sums = f32[128,8,128]{2,1,0:T(8,128)S(1)} all-to-all(f32[128,8,128]{2,1,0:T(8,128)S(1)} %get-tuple-element.5), channel_id=1, replica_groups=mesh['op_0'=2,'op_1'=4,'op_2'=4,'sector_0'=2,'sector_1'=2] {'op_0','op_1..., dimensions={0} | all-to-all | bytes 1048576 | tf_op jit(solution)/shard_map/all_to_all | solution.py:28
  78.4 0.0 copy-start.5
  78.4 0.8 copy-done.5
  79.3 0.4 second.1
  79.6 21.1 %all_to_all.21.vector = bf16[32,2,16,512]{3,2,1,0:T(8,128)(2,1)S(1)} all-to-all(bf16[32,2,16,512]{3,2,1,0:T(8,128)(2,1)S(1)} %second.1), channel_id=1, replica_groups=mesh['op_0'=2,'op_1'=4,'op_2'=4,'sector_0'=2,'sector_1'=2] {'op_0','op_1..., dimensions={0} | all-to-all | bytes 2097152 | tf_op jit(solution)/shard_map/all_to_all | solution.py:28
  100.7 0.0 copy-done
  100.7 0.0 copy-done.1
  100.7 3.8 %resident.3 = f32[4,512,512]{2,1,0:T(8,128)S(1)} custom-call(s32[8]{0:T(128)S(1)} %reshape.26.targets, s32[1]{0:T(128)S(6)} %sub.4.core, bf16[32,2,16,512]{3,2,1,0:T(8,128)(2,1)S(1)} %all_to_all.21.vector, bf16[8,512,512]{2,1,0:T(8,128)(2,1)S(1)} %bitcast.8, bf16[8,512,512]{2,1,0:T(8,128)(2,1)S(1)} %bitcast.12), custom_call_target="tpu_custom_call" | custom-call | flops 2147483648 | bytes 4194304 | tf_op jit(solution)/shard_map/resident/pallas_call | solution.py:108
  104.5 0.1 collective-permute-start.1
  104.6 3.8 %resident.2.kept = f32[4,512,512]{2,1,0:T(8,128)S(1)} custom-call(s32[8]{0:T(128)S(1)} %reshape.26.targets, s32[1]{0:T(128)} %bitcast.1.core, bf16[32,2,16,512]{3,2,1,0:T(8,128)(2,1)S(1)} %all_to_all.21.vector, bf16[8,512,512]{2,1,0:T(8,128)(2,1)S(1)} %bitcast.9, bf16[8,512,512]{2,1,0:T(8,128)(2,1)S(1)} %bitcast.13), custom_call_target="tpu_custom_call" | custom-call | flops 2147483648 | bytes 4194304 | tf_op jit(solution)/shard_map/resident/pallas_call | solution.py:108
  108.4 3.3 %collective-permute-done.1.arrived = f32[4,512,512]{2,1,0:T(8,128)S(1)} collective-permute-done((f32[4,512,512]{2,1,0:T(8,128)S(1)}, f32[4,512,512]{2,1,0:T(8,128)S(1)}, u32[]{:S(2)}, u32[]{:S(2)}) %collective-permute-start.1) | collective-permute-done | bytes 4194336 | tf_op jit(solution)/shard_map/ppermute | solution.py:211
  111.7 0.5 pack.3
  112.3 36.4 %all_to_all.22.pieces = bf16[64,2,16,512]{3,2,1,0:T(8,128)(2,1)S(1)} all-to-all(bf16[64,2,16,512]{3,2,1,0:T(8,128)(2,1)S(1)} %bitcast.14), channel_id=1, replica_groups=mesh['op_0'=2,'op_1'=4,'op_2'=4,'sector_0'=2,'sector_1'=2] {'op_0','op_1..., dimensions={0} | all-to-all | bytes 4194304 | tf_op jit(solution)/shard_map/all_to_all | solution.py:28
  148.7 0.9 last.1
Async XLA Ops:
  1.5 1.2 copy-start.2
  2.7 5.0 %copy-start.3 = (bf16[2,512,512]{2,1,0:T(8,128)(2,1)S(1)}, bf16[2,512,512]{2,1,0:T(8,128)(2,1)}, u32[]{:S(2)}) copy-start(bf16[2,512,512]{2,1,0:T(8,128)(2,1)} %wave.3) | copy-start | bytes 3145732
  7.6 7.2 %collective-permute-start = (f32[4,512,512]{2,1,0:T(8,128)S(1)}, f32[4,512,512]{2,1,0:T(8,128)S(1)}, u32[]{:S(2)}, u32[]{:S(2)}) collective-permute-start(f32[4,512,512]{2,1,0:T(8,128)S(1)} %loading.3), channel_id=1, source_target_pairs={{0,1},{1,0},{2,3},{3,2},{4,5},{5,4},{6,7},{7,6},{8,9},{9,8},{10,11... | collective-permute-start | bytes 12582920 | tf_op jit(solution)/shard_map/ppermute | solution.py:211
  16.7 43.2 %copy-start.4 = (f32[2,16,512]{2,1,0:T(8,128)S(1)}, f32[2,16,512]{2,1,0:T(8,128)}, u32[]{:S(2)}) copy-start(f32[2,16,512]{2,1,0:T(8,128)} %precond.3) | copy-start | bytes 196612
  16.7 43.1 %all-to-all-start = ((bf16[64,2,16,512]{3,2,1,0:T(8,128)(2,1)}), bf16[64,2,16,512]{3,2,1,0:T(8,128)(2,1)S(1)}, u32[]{:S(2)}, u32[]{:S(2)}) async-start(bf16[64,2,16,512]{3,2,1,0:T(8,128)(2,1)} %bitcast.4), calls=%async_computation | async-start | bytes 4194304 | tf_op jit(solution)/shard_map/all_to_all | solution.py:28
  59.9 40.8 %copy-start = (bf16[4,2,512,512]{3,2,1,0:T(8,128)(2,1)S(1)}, bf16[4,2,512,512]{3,2,1,0:T(8,128)(2,1)}, u32[]{:S(2)}) copy-start(bf16[4,2,512,512]{3,2,1,0:T(8,128)(2,1)} %param.6) | copy-start | bytes 12582916
  59.9 40.8 %copy-start.1 = (bf16[4,2,512,512]{3,2,1,0:T(8,128)(2,1)S(1)}, bf16[4,2,512,512]{3,2,1,0:T(8,128)(2,1)}, u32[]{:S(2)}) copy-start(bf16[4,2,512,512]{3,2,1,0:T(8,128)(2,1)} %param.7) | copy-start | bytes 12582916
  78.4 0.8 copy-start.5
  104.5 7.2 %collective-permute-start.1 = (f32[4,512,512]{2,1,0:T(8,128)S(1)}, f32[4,512,512]{2,1,0:T(8,128)S(1)}, u32[]{:S(2)}, u32[]{:S(2)}) collective-permute-start(f32[4,512,512]{2,1,0:T(8,128)S(1)} %resident.3), channel_id=1, source_target_pairs={{0,1},{1,0},{2,3},{3,2},{4,5},{5,4},{6,7},{7,6},{8,9},{9,8},{10,11... | collective-permute-start | bytes 12582920 | tf_op jit(solution)/shard_map/ppermute | solution.py:211

commit v2 on v1

v2 whole, which is shorter than its diff:
```python
import functools

import jax
import jax.numpy as jnp
from jax import lax
from jax.experimental import pallas as pl
from jax.experimental.pallas import tpu as pltpu
from jax.sharding import Mesh
from jax.sharding import PartitionSpec as P

SECTOR = ("sector_0", "sector_1")
OP = ("op_0", "op_1", "op_2")
CHIPS = ("op_0", "op_1", "op_2", "sector_0")
EVERY = ("op_0", "op_1", "op_2", "sector_0", "sector_1")
CORE = "sector_1"
F32 = jnp.float32
BF16 = jnp.bfloat16
VMEM = pl.BlockSpec(memory_space=pltpu.VMEM)
SMEM = pl.BlockSpec(memory_space=pltpu.SMEM)
HBM = pl.BlockSpec(memory_space=pltpu.HBM)


def room(mebibytes):
    return pltpu.CompilerParams(vmem_limit_bytes=mebibytes * 2**20)


def exchange(pieces, axis):
    return lax.all_to_all(pieces, axis, split_axis=0, concat_axis=0, tiled=True)


def wanted(targets, core, task):
    local_sectors = targets.shape[0]
    target = targets[lax.rem(task, local_sectors), task // local_sectors]
    return target, lax.rem(target // local_sectors, 2) == core[0]


def all_tasks(targets, core, source, lefts, rights, totals, touched, arrive):
    local_sectors = targets.shape[0]
    slots, width, _ = totals.shape
    for slot in range(slots):
        touched[slot] = 0

    def one_task(task, carry):
        target, chosen = wanted(targets, core, task)

        @pl.when(chosen)
        def _():
            slot = target // (2 * local_sectors) * local_sectors + lax.rem(target, local_sectors)
            fresh = touched[slot] == 0
            touched[slot] = 1
            arrive(task)
            middle = jnp.dot(
                lefts[task], source(lax.rem(task, local_sectors)), preferred_element_type=F32
            ).astype(BF16)
            share = lax.dot_general(
                middle, rights[task], (((1,), (1,)), ((), ())), preferred_element_type=F32
            )
            totals[slot] = share + jnp.where(fresh, 0.0, totals[slot])

        return carry

    lax.fori_loop(0, lefts.shape[0], one_task, 0)
    for slot in range(slots):

        @pl.when(touched[slot] == 0)
        def _(slot=slot):
            totals[slot] = jnp.zeros((width, width), F32)


def loading_kernel(
    targets, core, vector, left, right, totals, lefts, rights, touched, sems
):
    def copies(task):
        return (
            pltpu.make_async_copy(left.at[task], lefts.at[task], sems.at[0, task]),
            pltpu.make_async_copy(right.at[task], rights.at[task], sems.at[1, task]),
        )

    def start(task, carry):
        @pl.when(wanted(targets, core, task)[1])
        def _():
            for copy in copies(task):
                copy.start()

        return carry

    def arrive(task):
        for copy in copies(task):
            copy.wait()

    lax.fori_loop(0, left.shape[0], start, 0)
    all_tasks(
        targets, core, lambda sector: vector[sector], lefts, rights, totals, touched, arrive
    )


def resident_kernel(targets, core, vector, lefts, rights, totals, touched):
    width = lefts.shape[1]

    def source(sector):
        return vector[:, sector].reshape(width, width)

    all_tasks(targets, core, source, lefts, rights, totals, touched, lambda task: None)


def apply_terms(targets, core, vector, left, right, loading, grant):
    tasks, width, _ = left.shape
    slots = tasks // 2
    flags = pltpu.SMEM((slots,), jnp.int32)
    scratch = [flags]
    if loading:
        scratch = [
            pltpu.VMEM(left.shape, BF16),
            pltpu.VMEM(left.shape, BF16),
            flags,
            pltpu.SemaphoreType.DMA((2, tasks)),
        ]
    return pl.pallas_call(
        loading_kernel if loading else resident_kernel,
        out_shape=jax.ShapeDtypeStruct((slots, width, width), F32),
        in_specs=[SMEM, SMEM] + [VMEM] + [HBM if loading else VMEM] * 2,
        out_specs=VMEM,
        scratch_shapes=scratch,
        compiler_params=room(grant),
        cost_estimate=pl.CostEstimate(
            flops=2 * tasks * width**3, bytes_accessed=2 * tasks * width**2, transcendentals=0
        ),
        name="loading" if loading else "resident",
    )(targets, core, vector, left, right)


def pack_kernel(kept, arrived, packed):
    slots, width, _ = kept.shape
    owners, halves, local_sectors, rows, _ = packed.shape
    for slot in range(slots):

        def one_owner(owner, carry, slot=slot):
            here = pl.ds(pl.multiple_of(owner * rows, rows), rows)
            total = kept[slot, here, :] + arrived[slot, here, :].astype(F32)
            packed[owner, slot // local_sectors, slot % local_sectors] = total.astype(BF16)
            return carry

        lax.fori_loop(0, owners, one_owner, 0, unroll=4)


def pack(kept, arrived, owners):
    slots, width, _ = kept.shape
    return pl.pallas_call(
        pack_kernel,
        out_shape=jax.ShapeDtypeStruct((owners, 2, slots // 2, width // owners, width), BF16),
        in_specs=[VMEM, VMEM],
        out_specs=VMEM,
        compiler_params=room(4),
        name="pack",
    )(kept, arrived)


def summed(pieces):
    shape = pieces.shape[1:]
    count = pieces.shape[0]

    def add(index, total):
        return total + pieces[index].astype(F32)

    return lax.fori_loop(0, count, add, jnp.zeros(shape, F32), unroll=8)


def lanes(value):
    local_sectors, rows, width = value.shape
    flat = jnp.sum(value.reshape(local_sectors * rows, width), axis=0, keepdims=True)
    return sum(flat[:, at : at + 128] for at in range(0, width, 128))


def first_kernel(offset, pieces, wave, precond, sigma, again, sums):
    rows = precond.shape[1]
    own = wave[:, pl.ds(pl.multiple_of(offset[0], rows), rows), :].astype(F32)
    total = summed(pieces)
    sigma[...] = total
    again[...] = total
    ratio, scaled = total / precond[...], own / precond[...]
    terms = (
        own * own,
        own * total,
        own * ratio,
        own * scaled,
        ratio * ratio,
        ratio * scaled,
        scaled * scaled,
    )
    one = jnp.concatenate([lanes(term) for term in terms] + [jnp.zeros((1, 128), F32)], axis=0)
    one = jnp.sum(one, axis=1, keepdims=True)
    row = lax.broadcasted_iota(jnp.int32, (8, 128), 0)
    lane = lax.broadcasted_iota(jnp.int32, (8, 128), 1)
    one = jnp.sum(jnp.where(row == lane, one, 0.0), axis=0, keepdims=True)
    sums[...] = jnp.broadcast_to(one[None], sums.shape)


def second_kernel(offset, sums, sigma, wave, precond, copies):
    rows = precond.shape[1]
    own = wave[:, pl.ds(pl.multiple_of(offset[0], rows), rows), :].astype(F32)
    whole = summed(sums)
    norm_sq, w_s, w_r, w_b, r_r, r_b, b_b = (whole[:, k : k + 1] for k in range(7))
    shift = w_s / norm_sq - 1.0
    projected = w_r - shift * w_b
    correction_sq = r_r - 2.0 * shift * r_b + shift * shift * b_b
    along = projected / norm_sq
    update_sq = correction_sq - projected * along
    scale = jnp.sqrt(norm_sq) * lax.rsqrt(update_sq + 1e-06)
    correction = (sigma[...] - shift[None] * own) / precond[...]
    new = ((correction - along[None] * own) * scale[None]).astype(BF16)
    copies[...] = jnp.broadcast_to(new[None], copies.shape)


def sum_kernel(pieces, sigma):
    sigma[...] = summed(pieces)


def on_device(wavefunction, left_blocks, right_blocks, target_sector, preconditioner):
    local_sectors, width, _ = wavefunction.shape
    rows = preconditioner.shape[1]
    owners = lax.axis_size(OP)
    offset = (lax.axis_index(OP) * rows).reshape(1)
    mine = lax.axis_index(CORE).reshape(1)
    theirs = 1 - mine
    targets = target_sector.T
    left, right = (
        blocks.reshape(-1, width, width) for blocks in (left_blocks, right_blocks)
    )
    row_shape = jax.ShapeDtypeStruct((local_sectors, rows, width), F32)
    offset, mine, theirs = lax.optimization_barrier((offset, mine, theirs))

    def partial_pieces(vector, loading):
        sent = apply_terms(targets, theirs, vector, left, right, loading, 47 if loading else 4)
        arrived = lax.ppermute(sent, CORE, [(0, 1), (1, 0)])
        kept = apply_terms(targets, mine, vector, left, right, loading, 47 if loading else 4)
        packed = pack(kept, arrived, owners)
        return exchange(packed.reshape(2 * owners, local_sectors, rows, width), CHIPS)

    pieces = partial_pieces(wavefunction, True)
    devices = lax.axis_size(EVERY)
    sigma_first, again, sums = pl.pallas_call(
        first_kernel,
        out_shape=(row_shape, row_shape, jax.ShapeDtypeStruct((devices, 1, 128), F32)),
        in_specs=[SMEM, VMEM, VMEM, VMEM],
        out_specs=(VMEM, VMEM, VMEM),
        compiler_params=room(4),
        name="first",
    )(offset, pieces, wavefunction, preconditioner)
    sums = exchange(sums, EVERY)
    copies = pl.pallas_call(
        second_kernel,
        out_shape=jax.ShapeDtypeStruct((owners, local_sectors, rows, width), BF16),
        in_specs=[SMEM, VMEM, VMEM, VMEM, VMEM],
        out_specs=VMEM,
        compiler_params=room(4),
        name="second",
    )(offset, sums, again, wavefunction, preconditioner)
    pieces = partial_pieces(exchange(copies, OP), False)
    sigma_second = pl.pallas_call(
        sum_kernel,
        out_shape=row_shape,
        in_specs=[VMEM],
        out_specs=VMEM,
        compiler_params=room(4),
        name="last",
    )(pieces)
    return (sigma_first, sigma_second)


def solution(mesh):
    torus = Mesh(mesh.devices.reshape(2, 4, 4, 2, 2), EVERY)
    placed = (
        P(SECTOR, None, None),
        P(OP, SECTOR, None, None),
        P(OP, SECTOR, None, None),
        P(OP, SECTOR),
        P(SECTOR, OP, None),
    )
    return jax.shard_map(
        on_device,
        mesh=torus,
        in_specs=placed,
        out_specs=(P(SECTOR, OP, None), P(SECTOR, OP, None)),
        check_vma=False,
    )
```

time: 150 us -> 143 us (0.953)
  blocking collectives: 75.1 us -> 114 us
  waiting for transfers between devices: 35.8 us -> 5.51 us
  starting transfers between devices: 13.1 us -> 0.17 us
    all_to_all x3 -> x4, blocking collectives: 75.1 us -> 114 us  [exchange(): return lax.all_to_all(pieces, axis, split_axis=0, concat_axis=0, tiled=True)]
    all_to_all x1 -> x0, waiting for transfers between devices: 30.2 us -> none  [exchange(): return lax.all_to_all(pieces, axis, split_axis=0, concat_axis=0, tiled=True)]
    all_to_all x1 -> x0, starting transfers between devices: 12.9 us -> none  [exchange(): return lax.all_to_all(pieces, axis, split_axis=0, concat_axis=0, tiled=True)]
  transfers between devices with their start and end apart: 3 -> 2, of which waited for: 3 -> 2; matrix products, arithmetic and copies ran while one was open for 0% -> 0% of each run, Pallas kernels for 6% -> 6%
where the time goes in v2:
time: 143 us
  blocking collectives  114 us (80%)
  Pallas kernels  21.3 us (15%)
  waiting for transfers between devices  5.51 us (4%)
  local copies, waits for them, and re-layouts  1.92 us (1%)
    all_to_all x4, blocking collectives, exchange(): return lax.all_to_all(pieces, axis, split_axis=0, concat_axis=0, tiled=True)  114 us
    pallas_call x4, Pallas kernels, apply_terms(): pl.pallas_call(loading_kernel if loading else resident_kernel, out_shape=...  17.5 us
    ppermute x2, waiting for transfers between devices, partial_pieces(): arrived = lax.ppermute(sent, CORE, [(0, 1), (1, 0)])  5.51 us
  transfers between devices with their start and end apart: 2, of which 2 were waited for; matrix products, arithmetic and copies ran while one was open for 0% of the time, Pallas kernels for 6%

profile of v2, /device:TPU:0, one launch (start us, length us, event | category | flops | bytes accessed | tf_op | source)
XLA Modules:
  0.0 143.5 jit_solution(3252016839450229409)
XLA Ops:
  0.6 0.0 copy-start.2
  0.6 1.2 copy-done.2
  1.9 0.0 copy-start.5
  1.9 0.7 copy-done.5
  2.5 0.0 copy-start.3
  2.5 5.1 %loading.3 = f32[4,512,512]{2,1,0:T(8,128)S(1)} custom-call(s32[2,4]{1,0:T(2,128)S(1)} %bitcast.17, s32[1]{0:T(128)S(6)} %sub.3.core, bf16[2,512,512]{2,1,0:T(8,128)(2,1)S(1)} %copy-done.2, bf16[8,512,512]{2,1,0:T(8,128)(2,1)} %bitcast.7, bf16[8,512,512]{2,1,0:T(8,128)(2,1)} %bitcast.11), custom_call_target="tpu_custom_call" | custom-call | flops 2147483648 | bytes 4194304 | tf_op jit(solution)/shard_map/loading/pallas_call | solution.py:118
  7.6 0.1 collective-permute-start
  7.7 0.0 copy-done.3
  7.7 5.1 %loading.2.kept = f32[4,512,512]{2,1,0:T(8,128)S(1)} custom-call(s32[2,4]{1,0:T(2,128)S(1)} %bitcast.18, s32[1]{0:T(128)} %bitcast.1.core, bf16[2,512,512]{2,1,0:T(8,128)(2,1)S(1)} %copy-done.3, bf16[8,512,512]{2,1,0:T(8,128)(2,1)} %bitcast.8, bf16[8,512,512]{2,1,0:T(8,128)(2,1)} %bitcast.12), custom_call_target="tpu_custom_call" | custom-call | flops 2147483648 | bytes 4194304 | tf_op jit(solution)/shard_map/loading/pallas_call | solution.py:118
  12.8 2.1 %collective-permute-done.arrived = f32[4,512,512]{2,1,0:T(8,128)S(1)} collective-permute-done((f32[4,512,512]{2,1,0:T(8,128)S(1)}, f32[4,512,512]{2,1,0:T(8,128)S(1)}, u32[]{:S(2)}, u32[]{:S(2)}) %collective-permute-start) | collective-permute-done | bytes 4194336 | tf_op jit(solution)/shard_map/ppermute | solution.py:234
  14.9 0.5 pack.2
  15.4 0.0 copy-start.4
  15.4 0.0 copy-start.1
  15.4 42.4 %all_to_all.20.pieces = bf16[64,2,16,512]{3,2,1,0:T(8,128)(2,1)S(1)} all-to-all(bf16[64,2,16,512]{3,2,1,0:T(8,128)(2,1)S(1)} %bitcast.15), channel_id=1, replica_groups=mesh['op_0'=2,'op_1'=4,'op_2'=4,'sector_0'=2,'sector_1'=2] {'op_0','op_1..., dimensions={0} | all-to-all | bytes 4194304 | tf_op jit(solution)/shard_map/all_to_all | solution.py:28
  57.8 0.0 copy-done.4
  57.8 0.0 copy-start
  57.8 1.0 first.1
  58.8 14.1 %all_to_all.21.sums = f32[128,1,128]{2,1,0:T(1,128)S(1)} all-to-all(f32[128,1,128]{2,1,0:T(1,128)S(1)} %get-tuple-element.12), channel_id=1, replica_groups=mesh['op_0'=2,'op_1'=4,'op_2'=4,'sector_0'=2,'sector_1'=2] {'op_0','op_1..., dimensions={0} | all-to-all | bytes 131072 | tf_op jit(solution)/shard_map/all_to_all | solution.py:28
  72.8 0.6 second.1
  73.4 20.6 %all_to_all.22.vector = bf16[32,2,16,512]{3,2,1,0:T(8,128)(2,1)S(1)} all-to-all(bf16[32,2,16,512]{3,2,1,0:T(8,128)(2,1)S(1)} %second.1), channel_id=1, replica_groups=mesh['op_0'=2,'op_1'=4,'op_2'=4,'sector_0'=2,'sector_1'=2] {'op_0','op_1..., dimensions={0} | all-to-all | bytes 2097152 | tf_op jit(solution)/shard_map/all_to_all | solution.py:28
  94.1 0.0 copy-done.1
  94.1 0.0 copy-done
  94.1 3.7 %resident.3 = f32[4,512,512]{2,1,0:T(8,128)S(1)} custom-call(s32[2,4]{1,0:T(2,128)S(1)} %bitcast.19, s32[1]{0:T(128)S(6)} %sub.3.core, bf16[32,2,16,512]{3,2,1,0:T(8,128)(2,1)S(1)} %all_to_all.22.vector, bf16[8,512,512]{2,1,0:T(8,128)(2,1)S(1)} %bitcast.9, bf16[8,512,512]{2,1,0:T(8,128)(2,1)S(1)} %bitcast.13), custom_call_target="tpu_custom_call" | custom-call | flops 2147483648 | bytes 4194304 | tf_op jit(solution)/shard_map/resident/pallas_call | solution.py:118
  97.8 0.1 collective-permute-start.1
  97.9 3.7 %resident.2.kept = f32[4,512,512]{2,1,0:T(8,128)S(1)} custom-call(s32[2,4]{1,0:T(2,128)S(1)} %bitcast.20, s32[1]{0:T(128)} %bitcast.1.core, bf16[32,2,16,512]{3,2,1,0:T(8,128)(2,1)S(1)} %all_to_all.22.vector, bf16[8,512,512]{2,1,0:T(8,128)(2,1)S(1)} %bitcast.10, bf16[8,512,512]{2,1,0:T(8,128)(2,1)S(1)} %bitcast.14), custom_call_target="tpu_custom_call" | custom-call | flops 2147483648 | bytes 4194304 | tf_op jit(solution)/shard_map/resident/pallas_call | solution.py:118
  101.6 3.4 %collective-permute-done.1.arrived = f32[4,512,512]{2,1,0:T(8,128)S(1)} collective-permute-done((f32[4,512,512]{2,1,0:T(8,128)S(1)}, f32[4,512,512]{2,1,0:T(8,128)S(1)}, u32[]{:S(2)}, u32[]{:S(2)}) %collective-permute-start.1) | collective-permute-done | bytes 4194336 | tf_op jit(solution)/shard_map/ppermute | solution.py:234
  105.0 0.8 pack.3
  105.8 36.7 %all_to_all.23.pieces = bf16[64,2,16,512]{3,2,1,0:T(8,128)(2,1)S(1)} all-to-all(bf16[64,2,16,512]{3,2,1,0:T(8,128)(2,1)S(1)} %bitcast.16), channel_id=1, replica_groups=mesh['op_0'=2,'op_1'=4,'op_2'=4,'sector_0'=2,'sector_1'=2] {'op_0','op_1..., dimensions={0} | all-to-all | bytes 4194304 | tf_op jit(solution)/shard_map/all_to_all | solution.py:28
  142.5 0.9 last.1
Async XLA Ops:
  0.6 1.2 copy-start.2
  1.9 0.7 copy-start.5
  2.5 5.2 %copy-start.3 = (bf16[2,512,512]{2,1,0:T(8,128)(2,1)S(1)}, bf16[2,512,512]{2,1,0:T(8,128)(2,1)}, u32[]{:S(2)}) copy-start(bf16[2,512,512]{2,1,0:T(8,128)(2,1)} %wave.3) | copy-start | bytes 3145732
  7.6 7.2 %collective-permute-start = (f32[4,512,512]{2,1,0:T(8,128)S(1)}, f32[4,512,512]{2,1,0:T(8,128)S(1)}, u32[]{:S(2)}, u32[]{:S(2)}) collective-permute-start(f32[4,512,512]{2,1,0:T(8,128)S(1)} %loading.3), channel_id=1, source_target_pairs={{0,1},{1,0},{2,3},{3,2},{4,5},{5,4},{6,7},{7,6},{8,9},{9,8},{10,11... | collective-permute-start | bytes 12582920 | tf_op jit(solution)/shard_map/ppermute | solution.py:234
  15.4 42.4 %copy-start.4 = (f32[2,16,512]{2,1,0:T(8,128)S(1)}, f32[2,16,512]{2,1,0:T(8,128)}, u32[]{:S(2)}) copy-start(f32[2,16,512]{2,1,0:T(8,128)} %precond.3) | copy-start | bytes 196612
  15.4 78.7 %copy-start.1 = (bf16[4,2,512,512]{3,2,1,0:T(8,128)(2,1)S(1)}, bf16[4,2,512,512]{3,2,1,0:T(8,128)(2,1)}, u32[]{:S(2)}) copy-start(bf16[4,2,512,512]{3,2,1,0:T(8,128)(2,1)} %param.7) | copy-start | bytes 12582916
  57.8 36.3 %copy-start = (bf16[4,2,512,512]{3,2,1,0:T(8,128)(2,1)S(1)}, bf16[4,2,512,512]{3,2,1,0:T(8,128)(2,1)}, u32[]{:S(2)}) copy-start(bf16[4,2,512,512]{3,2,1,0:T(8,128)(2,1)} %param.6) | copy-start | bytes 12582916
  97.8 7.2 %collective-permute-start.1 = (f32[4,512,512]{2,1,0:T(8,128)S(1)}, f32[4,512,512]{2,1,0:T(8,128)S(1)}, u32[]{:S(2)}, u32[]{:S(2)}) collective-permute-start(f32[4,512,512]{2,1,0:T(8,128)S(1)} %resident.3), channel_id=1, source_target_pairs={{0,1},{1,0},{2,3},{3,2},{4,5},{5,4},{6,7},{7,6},{8,9},{9,8},{10,11... | collective-permute-start | bytes 12582920 | tf_op jit(solution)/shard_map/ppermute | solution.py:234

commit v3 on v2

--- a/solution.py
+++ b/solution.py
@@ -28,38 +28,53 @@
     return lax.all_to_all(pieces, axis, split_axis=0, concat_axis=0, tiled=True)
 
 
-def wanted(targets, core, task):
-    local_sectors = targets.shape[0]
-    target = targets[lax.rem(task, local_sectors), task // local_sectors]
-    return target, lax.rem(target // local_sectors, 2) == core[0]
-
-
-def all_tasks(targets, core, source, lefts, rights, totals, touched, arrive):
+def chosen_tasks(targets, core, order):
+    local_sectors, terms = targets.shape
+
+    def scan(task, count):
+        target = targets[lax.rem(task, local_sectors), task // local_sectors]
+        order[count] = task
+        return count + (lax.rem(target // local_sectors, 2) == core[0]).astype(jnp.int32)
+
+    return lax.fori_loop(0, local_sectors * terms, scan, jnp.int32(0))
+
+
+def run_tasks(targets, order, count, source, lefts, rights, totals, touched, arrive):
     local_sectors = targets.shape[0]
     slots, width, _ = totals.shape
     for slot in range(slots):
         touched[slot] = 0
 
-    def one_task(task, carry):
-        target, chosen = wanted(targets, core, task)
-
-        @pl.when(chosen)
-        def _():
-            slot = target // (2 * local_sectors) * local_sectors + lax.rem(target, local_sectors)
-            fresh = touched[slot] == 0
-            touched[slot] = 1
+    def middle_of(task):
+        vector = source(lax.rem(task, local_sectors))
+        return jnp.dot(lefts[task], vector, preferred_element_type=F32).astype(BF16)
+
+    def add(task, middle):
+        target = targets[lax.rem(task, local_sectors), task // local_sectors]
+        slot = target // (2 * local_sectors) * local_sectors + lax.rem(target, local_sectors)
+        fresh = touched[slot] == 0
+        touched[slot] = 1
+        share = lax.dot_general(
+            middle, rights[task], (((1,), (1,)), ((), ())), preferred_element_type=F32
+        )
+        totals[slot] = share + jnp.where(fresh, 0.0, totals[slot])
+
+    def pair(index, carry):
+        tasks = order[2 * index], order[2 * index + 1]
+        for task in tasks:
             arrive(task)
-            middle = jnp.dot(
-                lefts[task], source(lax.rem(task, local_sectors)), preferred_element_type=F32
-            ).astype(BF16)
-            share = lax.dot_general(
-                middle, rights[task], (((1,), (1,)), ((), ())), preferred_element_type=F32
-            )
-            totals[slot] = share + jnp.where(fresh, 0.0, totals[slot])
-
+        for task, middle in zip(tasks, [middle_of(task) for task in tasks]):
+            add(task, middle)
         return carry
 
-    lax.fori_loop(0, lefts.shape[0], one_task, 0)
+    lax.fori_loop(0, count // 2, pair, 0)
+
+    @pl.when(lax.rem(count, 2) == 1)
+    def _():
+        task = order[count - 1]
+        arrive(task)
+        add(task, middle_of(task))
+
     for slot in range(slots):
 
         @pl.when(touched[slot] == 0)
@@ -67,65 +82,71 @@
             totals[slot] = jnp.zeros((width, width), F32)
 
 
-def loading_kernel(
-    targets, core, vector, left, right, totals, lefts, rights, touched, sems
-):
-    def copies(task):
-        return (
-            pltpu.make_async_copy(left.at[task], lefts.at[task], sems.at[0, task]),
-            pltpu.make_async_copy(right.at[task], rights.at[task], sems.at[1, task]),
-        )
-
-    def start(task, carry):
-        @pl.when(wanted(targets, core, task)[1])
-        def _():
+def apply_kernel(loading, sending, *refs):
+    targets, core, vector, left, right, out, touched, order = refs[:8]
+    rest = list(refs[8:])
+    totals = rest.pop(0) if sending else out
+    count = chosen_tasks(targets, core, order)
+    if loading:
+        lefts, rights, sems = rest
+
+        def copies(task):
+            return (
+                pltpu.make_async_copy(left.at[task], lefts.at[task], sems.at[0, task]),
+                pltpu.make_async_copy(right.at[task], rights.at[task], sems.at[1, task]),
+            )
+
+        def start(index, carry):
+            for copy in copies(order[index]):
+                copy.start()
+            return carry
+
+        def arrive(task):
             for copy in copies(task):
-                copy.start()
-
-        return carry
-
-    def arrive(task):
-        for copy in copies(task):
-            copy.wait()
-
-    lax.fori_loop(0, left.shape[0], start, 0)
-    all_tasks(
-        targets, core, lambda sector: vector[sector], lefts, rights, totals, touched, arrive
-    )
-
-
-def resident_kernel(targets, core, vector, lefts, rights, totals, touched):
+                copy.wait()
+
+        lax.fori_loop(0, count, start, 0)
+    else:
+        lefts, rights = left, right
+
+        def arrive(task):
+            del task
+
     width = lefts.shape[1]
 
     def source(sector):
+        if loading:
+            return vector[sector]
         return vector[:, sector].reshape(width, width)
 
-    all_tasks(targets, core, source, lefts, rights, totals, touched, lambda task: None)
-
-
-def apply_terms(targets, core, vector, left, right, loading, grant):
+    run_tasks(targets, order, count, source, lefts, rights, totals, touched, arrive)
+    if sending:
+        out[...] = totals[...].astype(BF16)
+
+
+def apply_terms(targets, core, vector, left, right, loading, sending):
     tasks, width, _ = left.shape
     slots = tasks // 2
-    flags = pltpu.SMEM((slots,), jnp.int32)
-    scratch = [flags]
+    scratch = [pltpu.SMEM((slots,), jnp.int32), pltpu.SMEM((tasks + 1,), jnp.int32)]
+    if sending:
+        scratch += [pltpu.VMEM((slots, width, width), F32)]
     if loading:
-        scratch = [
+        scratch += [
             pltpu.VMEM(left.shape, BF16),
             pltpu.VMEM(left.shape, BF16),
-            flags,
             pltpu.SemaphoreType.DMA((2, tasks)),
         ]
     return pl.pallas_call(
-        loading_kernel if loading else resident_kernel,
-        out_shape=jax.ShapeDtypeStruct((slots, width, width), F32),
-        in_specs=[SMEM, SMEM] + [VMEM] + [HBM if loading else VMEM] * 2,
+        functools.partial(apply_kernel, loading, sending),
+        out_shape=jax.ShapeDtypeStruct((slots, width, width), BF16 if sending else F32),
+        in_specs=[SMEM, SMEM, VMEM] + [HBM if loading else VMEM] * 2,
         out_specs=VMEM,
         scratch_shapes=scratch,
-        compiler_params=room(grant),
+        compiler_params=room((50 if sending else 46) if loading else 8),
         cost_estimate=pl.CostEstimate(
             flops=2 * tasks * width**3, bytes_accessed=2 * tasks * width**2, transcendentals=0
         ),
-        name="loading" if loading else "resident",
+        name=("load_" if loading else "") + ("send" if sending else "keep"),
     )(targets, core, vector, left, right)
 
 
@@ -230,9 +251,9 @@
     offset, mine, theirs = lax.optimization_barrier((offset, mine, theirs))
 
     def partial_pieces(vector, loading):
-        sent = apply_terms(targets, theirs, vector, left, right, loading, 47 if loading else 4)
+        sent = apply_terms(targets, theirs, vector, left, right, loading, True)
         arrived = lax.ppermute(sent, CORE, [(0, 1), (1, 0)])
-        kept = apply_terms(targets, mine, vector, left, right, loading, 47 if loading else 4)
+        kept = apply_terms(targets, mine, vector, left, right, loading, False)
         packed = pack(kept, arrived, owners)
         return exchange(packed.reshape(2 * owners, local_sectors, rows, width), CHIPS)
 

time: 143 us -> 139 us (0.972)
  waiting for transfers between devices: 5.51 us -> 1.25 us
    ppermute x2, waiting for transfers between devices: 5.51 us -> 1.25 us  [partial_pieces(): arrived = lax.ppermute(sent, CORE, [(0, 1), (1, 0)])]
  transfers between devices with their start and end apart: 2 -> 2, of which waited for: 2 -> 1; matrix products, arithmetic and copies ran while one was open for 0% -> 0% of each run, Pallas kernels for 6% -> 5%
where the time goes in v3:
time: 139 us; the launch traced here: 138 us
  blocking collectives  113 us (81%)
  Pallas kernels  21.2 us (15%)
  local copies, waits for them, and re-layouts  1.92 us (1%)
    all_to_all x4, blocking collectives, exchange(): return lax.all_to_all(pieces, axis, split_axis=0, concat_axis=0, tiled=True)  113 us
    pallas_call x4, Pallas kernels, apply_terms(): pl.pallas_call(functools.partial(apply_kernel, loading, sending), out_sha...  17.7 us
  transfers between devices with their start and end apart: 2, of which 1 were waited for; matrix products, arithmetic and copies ran while one was open for 0% of the time, Pallas kernels for 5%

profile of v3, /device:TPU:0, one launch (start us, length us, event | category | flops | bytes accessed | tf_op | source)
XLA Modules:
  0.0 138.3 jit_solution(17970017342024693040)
XLA Ops:
  0.6 0.0 copy-start.2
  0.7 1.2 copy-done.2
  1.9 0.0 copy-start.5
  1.9 0.7 copy-done.5
  2.5 0.0 copy-start.3
  2.5 0.0 copy-start.6
  2.5 5.9 %load_send.1 = bf16[4,512,512]{2,1,0:T(8,128)(2,1)S(1)} custom-call(s32[2,4]{1,0:T(2,128)S(1)} %bitcast.17, s32[1]{0:T(128)S(6)} %sub.3.refs_1_, bf16[2,512,512]{2,1,0:T(8,128)(2,1)S(1)} %copy-done.2, bf16[8,512,512]{2,1,0:T(8,128)(2,1)} %bitcast.7, bf16[8,512,512]{2,1,0:T(8,128)(2,1)} %bitcast.11), custom_call_target="tpu_custom_call" | custom-call | flops 2147483648 | bytes 4194304 | tf_op jit(solution)/shard_map/load_send/pallas_call | solution.py:139
  8.5 0.1 collective-permute-start
  8.6 0.0 copy-done.3
  8.6 0.0 copy-done.6
  8.6 4.5 %load_keep.1.kept = f32[4,512,512]{2,1,0:T(8,128)S(1)} custom-call(s32[2,4]{1,0:T(2,128)S(1)} %bitcast.18, s32[1]{0:T(128)} %bitcast.1.refs_1_, bf16[2,512,512]{2,1,0:T(8,128)(2,1)S(1)} %copy-done.3, bf16[8,512,512]{2,1,0:T(8,128)(2,1)} %bitcast.8, bf16[8,512,512]{2,1,0:T(8,128)(2,1)} %bitcast.12), custom_call_target="tpu_custom_call" | custom-call | flops 2147483648 | bytes 4194304 | tf_op jit(solution)/shard_map/load_keep/pallas_call | solution.py:139
  13.2 0.0 collective-permute-done.arrived
  13.2 0.0 copy-start.4
  13.2 0.5 pack.2
  13.7 0.0 copy-start.1
  13.7 42.3 %all_to_all.20.pieces = bf16[64,2,16,512]{3,2,1,0:T(8,128)(2,1)S(1)} all-to-all(bf16[64,2,16,512]{3,2,1,0:T(8,128)(2,1)S(1)} %bitcast.15), channel_id=1, replica_groups=mesh['op_0'=2,'op_1'=4,'op_2'=4,'sector_0'=2,'sector_1'=2] {'op_0','op_1..., dimensions={0} | all-to-all | bytes 4194304 | tf_op jit(solution)/shard_map/all_to_all | solution.py:28
  56.0 0.0 copy-done.4
  56.0 1.0 first.1
  57.0 14.0 %all_to_all.21.sums = f32[128,1,128]{2,1,0:T(1,128)S(1)} all-to-all(f32[128,1,128]{2,1,0:T(1,128)S(1)} %get-tuple-element.12), channel_id=1, replica_groups=mesh['op_0'=2,'op_1'=4,'op_2'=4,'sector_0'=2,'sector_1'=2] {'op_0','op_1..., dimensions={0} | all-to-all | bytes 131072 | tf_op jit(solution)/shard_map/all_to_all | solution.py:28
  71.0 0.0 copy-start
  71.0 0.6 second.1
  71.6 20.8 %all_to_all.22.refs_2_ = bf16[32,2,16,512]{3,2,1,0:T(8,128)(2,1)S(1)} all-to-all(bf16[32,2,16,512]{3,2,1,0:T(8,128)(2,1)S(1)} %second.1), channel_id=1, replica_groups=mesh['op_0'=2,'op_1'=4,'op_2'=4,'sector_0'=2,'sector_1'=2] {'op_0','op_1..., dimensions={0} | all-to-all | bytes 2097152 | tf_op jit(solution)/shard_map/all_to_all | solution.py:28
  92.4 0.0 copy-done.1
  92.4 0.0 copy-done
  92.4 4.3 %send.1 = bf16[4,512,512]{2,1,0:T(8,128)(2,1)S(1)} custom-call(s32[2,4]{1,0:T(2,128)S(1)} %bitcast.19, s32[1]{0:T(128)S(6)} %sub.3.refs_1_, bf16[32,2,16,512]{3,2,1,0:T(8,128)(2,1)S(1)} %all_to_all.22.refs_2_, bf16[8,512,512]{2,1,0:T(8,128)(2,1)S(1)} %bitcast.9, bf16[8,512,512]{2,1,0:T(8,128)(2,1)S(1)} %bitcast.13), custom_call_target="tpu_custom_call" | custom-call | flops 2147483648 | bytes 4194304 | tf_op jit(solution)/shard_map/send/pallas_call | solution.py:139
  96.7 0.1 collective-permute-start.1
  96.8 2.9 %keep.1.kept = f32[4,512,512]{2,1,0:T(8,128)S(1)} custom-call(s32[2,4]{1,0:T(2,128)S(1)} %bitcast.20, s32[1]{0:T(128)} %bitcast.1.refs_1_, bf16[32,2,16,512]{3,2,1,0:T(8,128)(2,1)S(1)} %all_to_all.22.refs_2_, bf16[8,512,512]{2,1,0:T(8,128)(2,1)S(1)} %bitcast.10, bf16[8,512,512]{2,1,0:T(8,128)(2,1)S(1)} %bitcast.14), custom_call_target="tpu_custom_call" | custom-call | flops 2147483648 | bytes 4194304 | tf_op jit(solution)/shard_map/keep/pallas_call | solution.py:139
  99.7 1.2 collective-permute-done.1.arrived
  100.9 0.5 pack.3
  101.4 36.0 %all_to_all.23.pieces = bf16[64,2,16,512]{3,2,1,0:T(8,128)(2,1)S(1)} all-to-all(bf16[64,2,16,512]{3,2,1,0:T(8,128)(2,1)S(1)} %bitcast.16), channel_id=1, replica_groups=mesh['op_0'=2,'op_1'=4,'op_2'=4,'sector_0'=2,'sector_1'=2] {'op_0','op_1..., dimensions={0} | all-to-all | bytes 4194304 | tf_op jit(solution)/shard_map/all_to_all | solution.py:28
  137.4 0.9 last.1
Async XLA Ops:
  0.6 1.2 copy-start.2
  1.9 0.7 copy-start.5
  2.5 6.1 %copy-start.3 = (bf16[2,512,512]{2,1,0:T(8,128)(2,1)S(1)}, bf16[2,512,512]{2,1,0:T(8,128)(2,1)}, u32[]{:S(2)}) copy-start(bf16[2,512,512]{2,1,0:T(8,128)(2,1)} %wave.3) | copy-start | bytes 3145732
  2.5 6.1 %copy-start.6 = (s32[4,2]{0,1:T(2,128)S(1)}, s32[4,2]{0,1:T(2,128)}, u32[]{:S(2)}) copy-start(s32[4,2]{0,1:T(2,128)} %param.8) | copy-start | bytes 100
  8.5 4.7 %collective-permute-start = (bf16[4,512,512]{2,1,0:T(8,128)(2,1)S(1)}, bf16[4,512,512]{2,1,0:T(8,128)(2,1)S(1)}, u32[]{:S(2)}, u32[]{:S(2)}) collective-permute-start(bf16[4,512,512]{2,1,0:T(8,128)(2,1)S(1)} %load_send.1), channel_id=1, source_target_pairs={{0,1},{1,0},{2,3},{3,2},{4,5},{5,4},{6,7},{7,6},{8,9},{9,8},{10,11... | collective-permute-start | bytes 6291464 | tf_op jit(solution)/shard_map/ppermute | solution.py:255
  13.2 42.9 %copy-start.4 = (f32[2,16,512]{2,1,0:T(8,128)S(1)}, f32[2,16,512]{2,1,0:T(8,128)}, u32[]{:S(2)}) copy-start(f32[2,16,512]{2,1,0:T(8,128)} %precond.3) | copy-start | bytes 196612
  13.7 78.7 %copy-start.1 = (bf16[4,2,512,512]{3,2,1,0:T(8,128)(2,1)S(1)}, bf16[4,2,512,512]{3,2,1,0:T(8,128)(2,1)}, u32[]{:S(2)}) copy-start(bf16[4,2,512,512]{3,2,1,0:T(8,128)(2,1)} %param.7) | copy-start | bytes 12582916
  71.0 21.4 %copy-start = (bf16[4,2,512,512]{3,2,1,0:T(8,128)(2,1)S(1)}, bf16[4,2,512,512]{3,2,1,0:T(8,128)(2,1)}, u32[]{:S(2)}) copy-start(bf16[4,2,512,512]{3,2,1,0:T(8,128)(2,1)} %param.6) | copy-start | bytes 12582916
  96.7 4.2 %collective-permute-start.1 = (bf16[4,512,512]{2,1,0:T(8,128)(2,1)S(1)}, bf16[4,512,512]{2,1,0:T(8,128)(2,1)S(1)}, u32[]{:S(2)}, u32[]{:S(2)}) collective-permute-start(bf16[4,512,512]{2,1,0:T(8,128)(2,1)S(1)} %send.1), channel_id=1, source_target_pairs={{0,1},{1,0},{2,3},{3,2},{4,5},{5,4},{6,7},{7,6},{8,9},{9,8},{10,11... | collective-permute-start | bytes 6291464 | tf_op jit(solution)/shard_map/ppermute | solution.py:255

commit v4 on v3

--- a/solution.py
+++ b/solution.py
@@ -1,4 +1,5 @@
 import functools
+import itertools
 
 import jax
 import jax.numpy as jnp
@@ -10,7 +11,6 @@
 
 SECTOR = ("sector_0", "sector_1")
 OP = ("op_0", "op_1", "op_2")
-CHIPS = ("op_0", "op_1", "op_2", "sector_0")
 EVERY = ("op_0", "op_1", "op_2", "sector_0", "sector_1")
 CORE = "sector_1"
 F32 = jnp.float32
@@ -150,30 +150,79 @@
     )(targets, core, vector, left, right)
 
 
-def pack_kernel(kept, arrived, packed):
-    slots, width, _ = kept.shape
-    owners, halves, local_sectors, rows, _ = packed.shape
-    for slot in range(slots):
-
-        def one_owner(owner, carry, slot=slot):
-            here = pl.ds(pl.multiple_of(owner * rows, rows), rows)
+def place(op_0, op_1, op_2, half, core):
+    return (((op_0 * 4 + op_1) * 4 + op_2) * 2 + half) * 2 + core
+
+
+def along_ring(value, step):
+    pairs = []
+    for op_0, op_1, op_2, half in itertools.product(range(2), range(4), range(4), range(2)):
+        first, second = (op_1 + step) % 4, (op_2 + step) % 4
+        pairs.append((place(op_0, op_1, op_2, half, 0), place(op_0, first, op_2, half, 0)))
+        pairs.append((place(op_0, op_1, op_2, half, 1), place(op_0, op_1, second, half, 1)))
+    return lax.ppermute(value, EVERY, pairs)
+
+
+def across_rings(pieces):
+    rest = list(itertools.product(range(2), range(4), range(2)))
+    groups = [[place(low, ring, at, half, 0) for low, at, half in rest] for ring in range(4)]
+    groups += [[place(low, at, ring, half, 1) for low, at, half in rest] for ring in range(4)]
+    return lax.all_to_all(
+        pieces, EVERY, split_axis=0, concat_axis=0, axis_index_groups=groups, tiled=True
+    )
+
+
+def pack_kernel(ring, core, kept, arrived, own, *sent):
+    others, local_sectors, rows, _ = own.shape
+
+    def one_block(index, carry):
+        other, sector = index // local_sectors, lax.rem(index, local_sectors)
+        low, at, half = other // 8, lax.rem(other // 2, 4), lax.rem(other, 2)
+        slot = half * local_sectors + sector
+        for step in range(4):
+            to = lax.rem(ring[0] + step, 4)
+            block = low * 16 + jnp.where(core[0] == 0, to * 4 + at, at * 4 + to)
+            here = pl.ds(pl.multiple_of(block * rows, rows), rows)
             total = kept[slot, here, :] + arrived[slot, here, :].astype(F32)
-            packed[owner, slot // local_sectors, slot % local_sectors] = total.astype(BF16)
-            return carry
-
-        lax.fori_loop(0, owners, one_owner, 0, unroll=4)
-
-
-def pack(kept, arrived, owners):
-    slots, width, _ = kept.shape
+            if step == 0:
+                own[other, sector] = total
+            else:
+                sent[step - 1][other, sector] = total.astype(BF16)
+        return carry
+
+    lax.fori_loop(0, others * local_sectors, one_block, 0, unroll=2)
+
+
+def pack(ring, core, kept, arrived, shape):
     return pl.pallas_call(
         pack_kernel,
-        out_shape=jax.ShapeDtypeStruct((owners, 2, slots // 2, width // owners, width), BF16),
-        in_specs=[VMEM, VMEM],
+        out_shape=[jax.ShapeDtypeStruct(shape, F32)] + [jax.ShapeDtypeStruct(shape, BF16)] * 3,
+        in_specs=[SMEM, SMEM, VMEM, VMEM],
+        out_specs=[VMEM] * 4,
+        compiler_params=room(4),
+        name="pack",
+    )(ring, core, kept, arrived)
+
+
+def meet_kernel(own, first, second, third, out):
+    def one(index, carry):
+        total = own[index] + first[index].astype(F32)
+        total += second[index].astype(F32) + third[index].astype(F32)
+        out[index] = total.astype(BF16)
+        return carry
+
+    lax.fori_loop(0, own.shape[0], one, 0, unroll=4)
+
+
+def meet(own, arrived):
+    return pl.pallas_call(
+        meet_kernel,
+        out_shape=jax.ShapeDtypeStruct(own.shape, BF16),
+        in_specs=[VMEM] * 4,
         out_specs=VMEM,
         compiler_params=room(4),
-        name="pack",
-    )(kept, arrived)
+        name="meet",
+    )(own, *arrived)
 
 
 def summed(pieces):
@@ -243,19 +292,22 @@
     offset = (lax.axis_index(OP) * rows).reshape(1)
     mine = lax.axis_index(CORE).reshape(1)
     theirs = 1 - mine
+    ring = jnp.where(mine == 0, lax.axis_index("op_1"), lax.axis_index("op_2"))
     targets = target_sector.T
     left, right = (
         blocks.reshape(-1, width, width) for blocks in (left_blocks, right_blocks)
     )
     row_shape = jax.ShapeDtypeStruct((local_sectors, rows, width), F32)
-    offset, mine, theirs = lax.optimization_barrier((offset, mine, theirs))
+    offset, mine, theirs, ring = lax.optimization_barrier((offset, mine, theirs, ring))
 
     def partial_pieces(vector, loading):
         sent = apply_terms(targets, theirs, vector, left, right, loading, True)
         arrived = lax.ppermute(sent, CORE, [(0, 1), (1, 0)])
         kept = apply_terms(targets, mine, vector, left, right, loading, False)
-        packed = pack(kept, arrived, owners)
-        return exchange(packed.reshape(2 * owners, local_sectors, rows, width), CHIPS)
+        shape = (owners // 2, local_sectors, rows, width)
+        own, *sent = pack(ring, mine, kept, arrived, shape)
+        arrived = [along_ring(piece, step) for step, piece in enumerate(sent, 1)]
+        return across_rings(meet(own, arrived))
 
     pieces = partial_pieces(wavefunction, True)
     devices = lax.axis_size(EVERY)

time: 139 us -> 130 us (0.935)
  blocking collectives: 113 us -> 68.9 us
  waiting for transfers between devices: 1.25 us -> 24.3 us
  starting transfers between devices: 0.17 us -> 11.5 us
  Pallas kernels: 21.2 us -> 22.6 us
    all_to_all x4 -> x2, blocking collectives: 113 us -> 35.6 us  [exchange(): return lax.all_to_all(pieces, axis, split_axis=0, concat_axis=0, tiled=True)]
    all_to_all x0 -> x2, blocking collectives: none -> 33.3 us  [across_rings(): lax.all_to_all(pieces, EVERY, split_axis=0, concat_axis=0, axis_index_gro...]
    ppermute x0 -> x6, waiting for transfers between devices: none -> 23.6 us  [along_ring(): return lax.ppermute(value, EVERY, pairs)]
    ppermute x0 -> x6, starting transfers between devices: none -> 11.4 us  [along_ring(): return lax.ppermute(value, EVERY, pairs)]
    pallas_call x2 -> x4, Pallas kernels: 1.04 us -> 3.11 us  [the longest x2 2.52 us: pack(): pl.pallas_call(pack_kernel, out_shape=[jax.ShapeDtypeStruct(shape, F32)]...]
  transfers between devices with their start and end apart: 2 -> 8, of which waited for: 1 -> 5; matrix products, arithmetic and copies ran while one was open for 0% -> 0% of each run, Pallas kernels for 5% -> 7%
where the time goes in v4:
time: 130 us
  blocking collectives  68.9 us (53%)
  waiting for transfers between devices  24.3 us (19%)
  Pallas kernels  22.6 us (17%)
  starting transfers between devices  11.5 us (9%)
  local copies, waits for them, and re-layouts  1.92 us (1%)
    all_to_all x2, blocking collectives, exchange(): return lax.all_to_all(pieces, axis, split_axis=0, concat_axis=0, tiled=True)  35.6 us
    all_to_all x2, blocking collectives, across_rings(): lax.all_to_all(pieces, EVERY, split_axis=0, concat_axis=0, axis_index_gro...  33.3 us
    ppermute x6, waiting for transfers between devices, along_ring(): return lax.ppermute(value, EVERY, pairs)  23.6 us
    pallas_call x4, Pallas kernels, apply_terms(): pl.pallas_call(functools.partial(apply_kernel, loading, sending), out_sha...  17.5 us
    ppermute x6, starting transfers between devices, along_ring(): return lax.ppermute(value, EVERY, pairs)  11.4 us
  transfers between devices with their start and end apart: 8, of which 5 were waited for; matrix products, arithmetic and copies ran while one was open for 0% of the time, Pallas kernels for 7%

profile of v4, /device:TPU:0, one launch (start us, length us, event | category | flops | bytes accessed | tf_op | source)
XLA Modules:
  0.0 130.0 jit_solution(16805705119046690091)
XLA Ops:
  0.6 0.0 copy-start.2
  0.7 1.2 copy-done.2
  1.9 0.0 copy-start.5
  1.9 0.7 copy-done.5
  2.5 0.0 copy-start.3
  2.6 0.0 copy-start.6
  2.6 5.3 %load_send.1 = bf16[4,512,512]{2,1,0:T(8,128)(2,1)S(1)} custom-call(s32[2,4]{1,0:T(2,128)S(1)} %bitcast.15, s32[1]{0:T(128)S(6)} %sub.3.refs_1_, bf16[2,512,512]{2,1,0:T(8,128)(2,1)S(1)} %copy-done.2, bf16[8,512,512]{2,1,0:T(8,128)(2,1)} %bitcast.7, bf16[8,512,512]{2,1,0:T(8,128)(2,1)} %bitcast.11), custom_call_target="tpu_custom_call" | custom-call | flops 2147483648 | bytes 4194304 | tf_op jit(solution)/shard_map/load_send/pallas_call | solution.py:139
  7.9 0.1 collective-permute-start
  7.9 0.0 copy-done.3
  8.0 0.0 copy-done.6
  8.0 5.1 %load_keep.1.kept = f32[4,512,512]{2,1,0:T(8,128)S(1)} custom-call(s32[2,4]{1,0:T(2,128)S(1)} %bitcast.16, s32[1]{0:T(128)} %bitcast.1.refs_1_.core, bf16[2,512,512]{2,1,0:T(8,128)(2,1)S(1)} %copy-done.3, bf16[8,512,512]{2,1,0:T(8,128)(2,1)} %bitcast.8, bf16[8,512,512]{2,1,0:T(8,128)(2,1)} %bitcast.12), custom_call_target="tpu_custom_call" | custom-call | flops 2147483648 | bytes 4194304 | tf_op jit(solution)/shard_map/load_keep/pallas_call | solution.py:139
  13.1 0.0 copy-start.4
  13.1 0.0 collective-permute-done.arrived
  13.1 1.3 pack.2
  14.4 1.8 %collective-permute-start.1 = (bf16[16,2,16,512]{3,2,1,0:T(8,128)(2,1)S(1)}, bf16[16,2,16,512]{3,2,1,0:T(8,128)(2,1)S(1)}, u32[]{:S(2)}, u32[]{:S(2)}) collective-permute-start(bf16[16,2,16,512]{3,2,1,0:T(8,128)(2,1)S(1)} %get-tuple-element.22), channel_id=1, source_target_pairs={{0,16},{1,5},{2,18},{3,7},{4,20},{5,9},{6,22},{7,11},{8,24},{9,13}... | collective-permute-start | bytes 1572872 | tf_op jit(solution)/shard_map/ppermute | solution.py:163
  16.1 2.7 %collective-permute-start.2 = (bf16[16,2,16,512]{3,2,1,0:T(8,128)(2,1)S(1)}, bf16[16,2,16,512]{3,2,1,0:T(8,128)(2,1)S(1)}, u32[]{:S(2)}, u32[]{:S(2)}) collective-permute-start(bf16[16,2,16,512]{3,2,1,0:T(8,128)(2,1)S(1)} %get-tuple-element.23), channel_id=1, source_target_pairs={{0,32},{1,9},{2,34},{3,11},{4,36},{5,13},{6,38},{7,15},{8,40},{9,1... | collective-permute-start | bytes 1572872 | tf_op jit(solution)/shard_map/ppermute | solution.py:163
  18.9 1.4 %collective-permute-start.3 = (bf16[16,2,16,512]{3,2,1,0:T(8,128)(2,1)S(1)}, bf16[16,2,16,512]{3,2,1,0:T(8,128)(2,1)S(1)}, u32[]{:S(2)}, u32[]{:S(2)}) collective-permute-start(bf16[16,2,16,512]{3,2,1,0:T(8,128)(2,1)S(1)} %get-tuple-element.24), channel_id=1, source_target_pairs={{0,48},{1,13},{2,50},{3,15},{4,52},{5,1},{6,54},{7,3},{8,56},{9,5}... | collective-permute-start | bytes 1572872 | tf_op jit(solution)/shard_map/ppermute | solution.py:163
  20.3 4.5 %collective-permute-done.1.first = bf16[16,2,16,512]{3,2,1,0:T(8,128)(2,1)S(1)} collective-permute-done((bf16[16,2,16,512]{3,2,1,0:T(8,128)(2,1)S(1)}, bf16[16,2,16,512]{3,2,1,0:T(8,128)(2,1)S(1)}, u32[]{:S(2)}, u32[]{:S(2)}) %collective-permute-start.1) | collective-permute-done | bytes 524320 | tf_op jit(solution)/shard_map/ppermute | solution.py:163
  24.8 6.8 %collective-permute-done.2.second = bf16[16,2,16,512]{3,2,1,0:T(8,128)(2,1)S(1)} collective-permute-done((bf16[16,2,16,512]{3,2,1,0:T(8,128)(2,1)S(1)}, bf16[16,2,16,512]{3,2,1,0:T(8,128)(2,1)S(1)}, u32[]{:S(2)}, u32[]{:S(2)}) %collective-permute-start.2) | collective-permute-done | bytes 524320 | tf_op jit(solution)/shard_map/ppermute | solution.py:163
  31.7 0.0 collective-permute-done.3.third
  31.7 0.0 copy-start.1
  31.7 0.3 meet.2
  32.0 0.0 copy-start
  32.0 19.4 %all_to_all.20.pieces = bf16[16,2,16,512]{3,2,1,0:T(8,128)(2,1)S(1)} all-to-all(bf16[16,2,16,512]{3,2,1,0:T(8,128)(2,1)S(1)} %meet.2), channel_id=1, replica_groups={{0,2,4,6,8,10,12,14,64,66,68,70,72,74,76,78},{16,18,20,22,24,26,28,30,8..., dimensions={0} | all-to-all | bytes 1048576 | tf_op jit(solution)/shard_map/all_to_all | solution.py:170
  51.3 0.0 copy-done.4
  51.3 0.7 first.1
  52.1 15.0 %all_to_all.21.sums = f32[128,1,128]{2,1,0:T(1,128)S(1)} all-to-all(f32[128,1,128]{2,1,0:T(1,128)S(1)} %get-tuple-element.26), channel_id=1, replica_groups=mesh['op_0'=2,'op_1'=4,'op_2'=4,'sector_0'=2,'sector_1'=2] {'op_0','op_1..., dimensions={0} | all-to-all | bytes 131072 | tf_op jit(solution)/shard_map/all_to_all | solution.py:28
  67.0 0.6 second.1
  67.6 20.6 %all_to_all.22.refs_2_ = bf16[32,2,16,512]{3,2,1,0:T(8,128)(2,1)S(1)} all-to-all(bf16[32,2,16,512]{3,2,1,0:T(8,128)(2,1)S(1)} %second.1), channel_id=1, replica_groups=mesh['op_0'=2,'op_1'=4,'op_2'=4,'sector_0'=2,'sector_1'=2] {'op_0','op_1..., dimensions={0} | all-to-all | bytes 2097152 | tf_op jit(solution)/shard_map/all_to_all | solution.py:28
  88.3 0.0 copy-done.1
  88.3 0.0 copy-done
  88.3 3.6 %send.1 = bf16[4,512,512]{2,1,0:T(8,128)(2,1)S(1)} custom-call(s32[2,4]{1,0:T(2,128)S(1)} %bitcast.17, s32[1]{0:T(128)S(6)} %sub.3.refs_1_, bf16[32,2,16,512]{3,2,1,0:T(8,128)(2,1)S(1)} %all_to_all.22.refs_2_, bf16[8,512,512]{2,1,0:T(8,128)(2,1)S(1)} %bitcast.9, bf16[8,512,512]{2,1,0:T(8,128)(2,1)S(1)} %bitcast.13), custom_call_target="tpu_custom_call" | custom-call | flops 2147483648 | bytes 4194304 | tf_op jit(solution)/shard_map/send/pallas_call | solution.py:139
  91.9 0.1 collective-permute-start.4
  92.0 3.4 %keep.1.kept = f32[4,512,512]{2,1,0:T(8,128)S(1)} custom-call(s32[2,4]{1,0:T(2,128)S(1)} %bitcast.18, s32[1]{0:T(128)} %bitcast.1.refs_1_.core, bf16[32,2,16,512]{3,2,1,0:T(8,128)(2,1)S(1)} %all_to_all.22.refs_2_, bf16[8,512,512]{2,1,0:T(8,128)(2,1)S(1)} %bitcast.10, bf16[8,512,512]{2,1,0:T(8,128)(2,1)S(1)} %bitcast.14), custom_call_target="tpu_custom_call" | custom-call | flops 2147483648 | bytes 4194304 | tf_op jit(solution)/shard_map/keep/pallas_call | solution.py:139
  95.4 0.7 collective-permute-done.4.arrived
  96.1 1.2 pack.3
  97.4 0.4 collective-permute-start.5
  97.8 4.5 %collective-permute-start.6 = (bf16[16,2,16,512]{3,2,1,0:T(8,128)(2,1)S(1)}, bf16[16,2,16,512]{3,2,1,0:T(8,128)(2,1)S(1)}, u32[]{:S(2)}, u32[]{:S(2)}) collective-permute-start(bf16[16,2,16,512]{3,2,1,0:T(8,128)(2,1)S(1)} %get-tuple-element.30), channel_id=1, source_target_pairs={{0,32},{1,9},{2,34},{3,11},{4,36},{5,13},{6,38},{7,15},{8,40},{9,1... | collective-permute-start | bytes 1572872 | tf_op jit(solution)/shard_map/ppermute | solution.py:163
  102.3 0.5 collective-permute-start.7
  102.8 5.2 %collective-permute-done.5.first = bf16[16,2,16,512]{3,2,1,0:T(8,128)(2,1)S(1)} collective-permute-done((bf16[16,2,16,512]{3,2,1,0:T(8,128)(2,1)S(1)}, bf16[16,2,16,512]{3,2,1,0:T(8,128)(2,1)S(1)}, u32[]{:S(2)}, u32[]{:S(2)}) %collective-permute-start.5) | collective-permute-done | bytes 524320 | tf_op jit(solution)/shard_map/ppermute | solution.py:163
  108.0 7.1 %collective-permute-done.6.second = bf16[16,2,16,512]{3,2,1,0:T(8,128)(2,1)S(1)} collective-permute-done((bf16[16,2,16,512]{3,2,1,0:T(8,128)(2,1)S(1)}, bf16[16,2,16,512]{3,2,1,0:T(8,128)(2,1)S(1)}, u32[]{:S(2)}, u32[]{:S(2)}) %collective-permute-start.6) | collective-permute-done | bytes 524320 | tf_op jit(solution)/shard_map/ppermute | solution.py:163
  115.1 0.0 collective-permute-done.7.third
  115.1 0.3 meet.3
  115.4 13.9 %all_to_all.23.pieces = bf16[16,2,16,512]{3,2,1,0:T(8,128)(2,1)S(1)} all-to-all(bf16[16,2,16,512]{3,2,1,0:T(8,128)(2,1)S(1)} %meet.3), channel_id=1, replica_groups={{0,2,4,6,8,10,12,14,64,66,68,70,72,74,76,78},{16,18,20,22,24,26,28,30,8..., dimensions={0} | all-to-all | bytes 1048576 | tf_op jit(solution)/shard_map/all_to_all | solution.py:170
  129.3 0.7 last.1
Async XLA Ops:
  0.6 1.2 copy-start.2
  1.9 0.7 copy-start.5
  2.5 5.4 %copy-start.3 = (bf16[2,512,512]{2,1,0:T(8,128)(2,1)S(1)}, bf16[2,512,512]{2,1,0:T(8,128)(2,1)}, u32[]{:S(2)}) copy-start(bf16[2,512,512]{2,1,0:T(8,128)(2,1)} %wave.3) | copy-start | bytes 3145732
  2.6 5.4 %copy-start.6 = (s32[4,2]{0,1:T(2,128)S(1)}, s32[4,2]{0,1:T(2,128)}, u32[]{:S(2)}) copy-start(s32[4,2]{0,1:T(2,128)} %param.8) | copy-start | bytes 100
  7.9 5.2 %collective-permute-start = (bf16[4,512,512]{2,1,0:T(8,128)(2,1)S(1)}, bf16[4,512,512]{2,1,0:T(8,128)(2,1)S(1)}, u32[]{:S(2)}, u32[]{:S(2)}) collective-permute-start(bf16[4,512,512]{2,1,0:T(8,128)(2,1)S(1)} %load_send.1), channel_id=1, source_target_pairs={{0,1},{1,0},{2,3},{3,2},{4,5},{5,4},{6,7},{7,6},{8,9},{9,8},{10,11... | collective-permute-start | bytes 6291464 | tf_op jit(solution)/shard_map/ppermute | solution.py:305
  13.1 38.3 %copy-start.4 = (f32[2,16,512]{2,1,0:T(8,128)S(1)}, f32[2,16,512]{2,1,0:T(8,128)}, u32[]{:S(2)}) copy-start(f32[2,16,512]{2,1,0:T(8,128)} %precond.3) | copy-start | bytes 196612
  14.4 10.5 %collective-permute-start.1 = (bf16[16,2,16,512]{3,2,1,0:T(8,128)(2,1)S(1)}, bf16[16,2,16,512]{3,2,1,0:T(8,128)(2,1)S(1)}, u32[]{:S(2)}, u32[]{:S(2)}) collective-permute-start(bf16[16,2,16,512]{3,2,1,0:T(8,128)(2,1)S(1)} %get-tuple-element.22), channel_id=1, source_target_pairs={{0,16},{1,5},{2,18},{3,7},{4,20},{5,9},{6,22},{7,11},{8,24},{9,13}... | collective-permute-start | bytes 1572872 | tf_op jit(solution)/shard_map/ppermute | solution.py:163
  16.1 15.5 %collective-permute-start.2 = (bf16[16,2,16,512]{3,2,1,0:T(8,128)(2,1)S(1)}, bf16[16,2,16,512]{3,2,1,0:T(8,128)(2,1)S(1)}, u32[]{:S(2)}, u32[]{:S(2)}) collective-permute-start(bf16[16,2,16,512]{3,2,1,0:T(8,128)(2,1)S(1)} %get-tuple-element.23), channel_id=1, source_target_pairs={{0,32},{1,9},{2,34},{3,11},{4,36},{5,13},{6,38},{7,15},{8,40},{9,1... | collective-permute-start | bytes 1572872 | tf_op jit(solution)/shard_map/ppermute | solution.py:163
  18.9 12.8 %collective-permute-start.3 = (bf16[16,2,16,512]{3,2,1,0:T(8,128)(2,1)S(1)}, bf16[16,2,16,512]{3,2,1,0:T(8,128)(2,1)S(1)}, u32[]{:S(2)}, u32[]{:S(2)}) collective-permute-start(bf16[16,2,16,512]{3,2,1,0:T(8,128)(2,1)S(1)} %get-tuple-element.24), channel_id=1, source_target_pairs={{0,48},{1,13},{2,50},{3,15},{4,52},{5,1},{6,54},{7,3},{8,56},{9,5}... | collective-permute-start | bytes 1572872 | tf_op jit(solution)/shard_map/ppermute | solution.py:163
  31.7 56.6 %copy-start.1 = (bf16[4,2,512,512]{3,2,1,0:T(8,128)(2,1)S(1)}, bf16[4,2,512,512]{3,2,1,0:T(8,128)(2,1)}, u32[]{:S(2)}) copy-start(bf16[4,2,512,512]{3,2,1,0:T(8,128)(2,1)} %param.7) | copy-start | bytes 12582916
  32.0 56.3 %copy-start = (bf16[4,2,512,512]{3,2,1,0:T(8,128)(2,1)S(1)}, bf16[4,2,512,512]{3,2,1,0:T(8,128)(2,1)}, u32[]{:S(2)}) copy-start(bf16[4,2,512,512]{3,2,1,0:T(8,128)(2,1)} %param.6) | copy-start | bytes 12582916
  91.9 4.2 %collective-permute-start.4 = (bf16[4,512,512]{2,1,0:T(8,128)(2,1)S(1)}, bf16[4,512,512]{2,1,0:T(8,128)(2,1)S(1)}, u32[]{:S(2)}, u32[]{:S(2)}) collective-permute-start(bf16[4,512,512]{2,1,0:T(8,128)(2,1)S(1)} %send.1), channel_id=1, source_target_pairs={{0,1},{1,0},{2,3},{3,2},{4,5},{5,4},{6,7},{7,6},{8,9},{9,8},{10,11... | collective-permute-start | bytes 6291464 | tf_op jit(solution)/shard_map/ppermute | solution.py:305
  97.4 10.6 %collective-permute-start.5 = (bf16[16,2,16,512]{3,2,1,0:T(8,128)(2,1)S(1)}, bf16[16,2,16,512]{3,2,1,0:T(8,128)(2,1)S(1)}, u32[]{:S(2)}, u32[]{:S(2)}) collective-permute-start(bf16[16,2,16,512]{3,2,1,0:T(8,128)(2,1)S(1)} %get-tuple-element.29), channel_id=1, source_target_pairs={{0,16},{1,5},{2,18},{3,7},{4,20},{5,9},{6,22},{7,11},{8,24},{9,13}... | collective-permute-start | bytes 1572872 | tf_op jit(solution)/shard_map/ppermute | solution.py:163
  97.8 17.2 %collective-permute-start.6 = (bf16[16,2,16,512]{3,2,1,0:T(8,128)(2,1)S(1)}, bf16[16,2,16,512]{3,2,1,0:T(8,128)(2,1)S(1)}, u32[]{:S(2)}, u32[]{:S(2)}) collective-permute-start(bf16[16,2,16,512]{3,2,1,0:T(8,128)(2,1)S(1)} %get-tuple-element.30), channel_id=1, source_target_pairs={{0,32},{1,9},{2,34},{3,11},{4,36},{5,13},{6,38},{7,15},{8,40},{9,1... | collective-permute-start | bytes 1572872 | tf_op jit(solution)/shard_map/ppermute | solution.py:163
  102.3 12.8 %collective-permute-start.7 = (bf16[16,2,16,512]{3,2,1,0:T(8,128)(2,1)S(1)}, bf16[16,2,16,512]{3,2,1,0:T(8,128)(2,1)S(1)}, u32[]{:S(2)}, u32[]{:S(2)}) collective-permute-start(bf16[16,2,16,512]{3,2,1,0:T(8,128)(2,1)S(1)} %get-tuple-element.31), channel_id=1, source_target_pairs={{0,48},{1,13},{2,50},{3,15},{4,52},{5,1},{6,54},{7,3},{8,56},{9,5}... | collective-permute-start | bytes 1572872 | tf_op jit(solution)/shard_map/ppermute | solution.py:163

commit v5 on v4

--- a/solution.py
+++ b/solution.py
@@ -62,8 +62,11 @@
     def pair(index, carry):
         tasks = order[2 * index], order[2 * index + 1]
         for task in tasks:
-            arrive(task)
-        for task, middle in zip(tasks, [middle_of(task) for task in tasks]):
+            arrive(0, task)
+        middles = [middle_of(task) for task in tasks]
+        for task in tasks:
+            arrive(1, task)
+        for task, middle in zip(tasks, middles):
             add(task, middle)
         return carry
 
@@ -72,7 +75,8 @@
     @pl.when(lax.rem(count, 2) == 1)
     def _():
         task = order[count - 1]
-        arrive(task)
+        arrive(0, task)
+        arrive(1, task)
         add(task, middle_of(task))
 
     for slot in range(slots):
@@ -90,27 +94,27 @@
     if loading:
         lefts, rights, sems = rest
 
-        def copies(task):
-            return (
-                pltpu.make_async_copy(left.at[task], lefts.at[task], sems.at[0, task]),
-                pltpu.make_async_copy(right.at[task], rights.at[task], sems.at[1, task]),
-            )
-
-        def start(index, carry):
-            for copy in copies(order[index]):
-                copy.start()
+        def copy(side, task):
+            source, buffer = ((left, lefts), (right, rights))[side]
+            return pltpu.make_async_copy(source.at[task], buffer.at[task], sems.at[side, task])
+
+        def start(sides, index, carry):
+            for side in sides:
+                copy(side, order[index]).start()
             return carry
 
-        def arrive(task):
-            for copy in copies(task):
-                copy.wait()
-
-        lax.fori_loop(0, count, start, 0)
+        def arrive(side, task):
+            copy(side, task).wait()
+
+        early = jnp.minimum(count, 2)
+        lax.fori_loop(0, early, functools.partial(start, (0,)), 0)
+        lax.fori_loop(0, early, functools.partial(start, (1,)), 0)
+        lax.fori_loop(early, count, functools.partial(start, (0, 1)), 0)
     else:
         lefts, rights = left, right
 
-        def arrive(task):
-            del task
+        def arrive(side, task):
+            del side, task
 
     width = lefts.shape[1]
 
@@ -190,7 +194,7 @@
                 sent[step - 1][other, sector] = total.astype(BF16)
         return carry
 
-    lax.fori_loop(0, others * local_sectors, one_block, 0, unroll=2)
+    lax.fori_loop(0, others * local_sectors, one_block, 0, unroll=8)
 
 
 def pack(ring, core, kept, arrived, shape):
@@ -306,7 +310,7 @@
         kept = apply_terms(targets, mine, vector, left, right, loading, False)
         shape = (owners // 2, local_sectors, rows, width)
         own, *sent = pack(ring, mine, kept, arrived, shape)
-        arrived = [along_ring(piece, step) for step, piece in enumerate(sent, 1)]
+        arrived = [along_ring(sent[step - 1], step) for step in (2, 1, 3)]
         return across_rings(meet(own, arrived))
 
     pieces = partial_pieces(wavefunction, True)

time: 130 us -> 129 us (level)
  waiting for transfers between devices: 24.3 us -> 21.9 us
    ppermute x6, waiting for transfers between devices: 23.6 us -> 21.1 us  [along_ring(): return lax.ppermute(value, EVERY, pairs)]
  transfers between devices with their start and end apart: 8 -> 8, of which waited for: 5 -> 6; matrix products, arithmetic and copies ran while one was open for 0% -> 0% of each run, Pallas kernels for 7% -> 7%
where the time goes in v5:
time: 129 us; the launch traced here: 128 us
  blocking collectives  69.1 us (54%)
  Pallas kernels  22.6 us (18%)
  waiting for transfers between devices  21.9 us (17%)
  starting transfers between devices  12.1 us (9%)
  local copies, waits for them, and re-layouts  1.92 us (1%)
    all_to_all x2, blocking collectives, across_rings(): lax.all_to_all(pieces, EVERY, split_axis=0, concat_axis=0, axis_index_gro...  34.5 us
    all_to_all x2, blocking collectives, exchange(): return lax.all_to_all(pieces, axis, split_axis=0, concat_axis=0, tiled=True)  34.5 us
    ppermute x6, waiting for transfers between devices, along_ring(): return lax.ppermute(value, EVERY, pairs)  21.1 us
    pallas_call x4, Pallas kernels, apply_terms(): pl.pallas_call(functools.partial(apply_kernel, loading, sending), out_sha...  17.4 us
    ppermute x6, starting transfers between devices, along_ring(): return lax.ppermute(value, EVERY, pairs)  11.9 us
    pallas_call x2, Pallas kernels, pack(): pl.pallas_call(pack_kernel, out_shape=[jax.ShapeDtypeStruct(shape, F32)]...  2.59 us
  transfers between devices with their start and end apart: 8, of which 6 were waited for; matrix products, arithmetic and copies ran while one was open for 0% of the time, Pallas kernels for 7%

profile of v5, /device:TPU:0, one launch (start us, length us, event | category | flops | bytes accessed | tf_op | source)
XLA Modules:
  0.0 128.3 jit_solution(3177550062924229059)
XLA Ops:
  0.6 0.0 copy-start.2
  0.7 1.2 copy-done.2
  1.9 0.0 copy-start.5
  1.9 0.7 copy-done.5
  2.5 0.0 copy-start.3
  2.6 0.0 copy-start.6
  2.6 5.3 %load_send.1 = bf16[4,512,512]{2,1,0:T(8,128)(2,1)S(1)} custom-call(s32[2,4]{1,0:T(2,128)S(1)} %bitcast.15, s32[1]{0:T(128)S(6)} %sub.3.refs_1_, bf16[2,512,512]{2,1,0:T(8,128)(2,1)S(1)} %copy-done.2, bf16[8,512,512]{2,1,0:T(8,128)(2,1)} %bitcast.7, bf16[8,512,512]{2,1,0:T(8,128)(2,1)} %bitcast.11), custom_call_target="tpu_custom_call" | custom-call | flops 2147483648 | bytes 4194304 | tf_op jit(solution)/shard_map/load_send/pallas_call | solution.py:143
  7.9 0.1 collective-permute-start
  8.0 0.0 copy-done.3
  8.0 0.0 copy-done.6
  8.0 5.1 %load_keep.1.kept = f32[4,512,512]{2,1,0:T(8,128)S(1)} custom-call(s32[2,4]{1,0:T(2,128)S(1)} %bitcast.16, s32[1]{0:T(128)} %bitcast.1.refs_1_.core, bf16[2,512,512]{2,1,0:T(8,128)(2,1)S(1)} %copy-done.3, bf16[8,512,512]{2,1,0:T(8,128)(2,1)} %bitcast.8, bf16[8,512,512]{2,1,0:T(8,128)(2,1)} %bitcast.12), custom_call_target="tpu_custom_call" | custom-call | flops 2147483648 | bytes 4194304 | tf_op jit(solution)/shard_map/load_keep/pallas_call | solution.py:143
  13.1 0.0 copy-start.4
  13.1 0.0 collective-permute-done.arrived
  13.1 1.4 %pack.2 = (f32[16,2,16,512]{3,2,1,0:T(8,128)S(1)}, bf16[16,2,16,512]{3,2,1,0:T(8,128)(2,1)S(1)}, bf16[16,2,16,512]{3,2,1,0:T(8,128)(2,1)S(1)}, bf16[16,2,16,512]{3,2,1,0:T(8,128)(2,1)S(1)}) custom-call(s32[1]{0:T(128)S(6)} %select_n.4.ring, s32[1]{0:T(128)} %bitcast.1.refs_1_.core, f32[4,512,512]{2,1,0:T(8,128)S(1)} %load_keep.1.kept, ...), custom_call_target="tpu_custom_call" | custom-call | tf_op jit(solution)/shard_map/pack/pallas_call | solution.py:201
  14.5 3.7 %collective-permute-start.1 = (bf16[16,2,16,512]{3,2,1,0:T(8,128)(2,1)S(1)}, bf16[16,2,16,512]{3,2,1,0:T(8,128)(2,1)S(1)}, u32[]{:S(2)}, u32[]{:S(2)}) collective-permute-start(bf16[16,2,16,512]{3,2,1,0:T(8,128)(2,1)S(1)} %get-tuple-element.22), channel_id=1, source_target_pairs={{0,32},{1,9},{2,34},{3,11},{4,36},{5,13},{6,38},{7,15},{8,40},{9,1... | collective-permute-start | bytes 1572872 | tf_op jit(solution)/shard_map/ppermute | solution.py:167
  18.2 0.1 collective-permute-start.2
  18.3 3.2 %collective-permute-start.3 = (bf16[16,2,16,512]{3,2,1,0:T(8,128)(2,1)S(1)}, bf16[16,2,16,512]{3,2,1,0:T(8,128)(2,1)S(1)}, u32[]{:S(2)}, u32[]{:S(2)}) collective-permute-start(bf16[16,2,16,512]{3,2,1,0:T(8,128)(2,1)S(1)} %get-tuple-element.24), channel_id=1, source_target_pairs={{0,48},{1,13},{2,50},{3,15},{4,52},{5,1},{6,54},{7,3},{8,56},{9,5}... | collective-permute-start | bytes 1572872 | tf_op jit(solution)/shard_map/ppermute | solution.py:167
  21.5 4.0 %collective-permute-done.1.first = bf16[16,2,16,512]{3,2,1,0:T(8,128)(2,1)S(1)} collective-permute-done((bf16[16,2,16,512]{3,2,1,0:T(8,128)(2,1)S(1)}, bf16[16,2,16,512]{3,2,1,0:T(8,128)(2,1)S(1)}, u32[]{:S(2)}, u32[]{:S(2)}) %collective-permute-start.1) | collective-permute-done | bytes 524320 | tf_op jit(solution)/shard_map/ppermute | solution.py:167
  25.5 5.5 %collective-permute-done.2.second = bf16[16,2,16,512]{3,2,1,0:T(8,128)(2,1)S(1)} collective-permute-done((bf16[16,2,16,512]{3,2,1,0:T(8,128)(2,1)S(1)}, bf16[16,2,16,512]{3,2,1,0:T(8,128)(2,1)S(1)}, u32[]{:S(2)}, u32[]{:S(2)}) %collective-permute-start.2) | collective-permute-done | bytes 524320 | tf_op jit(solution)/shard_map/ppermute | solution.py:167
  31.0 0.1 collective-permute-done.3.third
  31.1 0.0 copy-start.1
  31.1 0.3 meet.2
  31.4 0.0 copy-start
  31.4 20.4 %all_to_all.20.pieces = bf16[16,2,16,512]{3,2,1,0:T(8,128)(2,1)S(1)} all-to-all(bf16[16,2,16,512]{3,2,1,0:T(8,128)(2,1)S(1)} %meet.2), channel_id=1, replica_groups={{0,2,4,6,8,10,12,14,64,66,68,70,72,74,76,78},{16,18,20,22,24,26,28,30,8..., dimensions={0} | all-to-all | bytes 1048576 | tf_op jit(solution)/shard_map/all_to_all | solution.py:174
  51.9 0.0 copy-done.4
  51.9 0.7 first.1
  52.6 13.9 %all_to_all.21.sums = f32[128,1,128]{2,1,0:T(1,128)S(1)} all-to-all(f32[128,1,128]{2,1,0:T(1,128)S(1)} %get-tuple-element.26), channel_id=1, replica_groups=mesh['op_0'=2,'op_1'=4,'op_2'=4,'sector_0'=2,'sector_1'=2] {'op_0','op_1..., dimensions={0} | all-to-all | bytes 131072 | tf_op jit(solution)/shard_map/all_to_all | solution.py:28
  66.5 0.6 second.1
  67.1 20.6 %all_to_all.22.refs_2_ = bf16[32,2,16,512]{3,2,1,0:T(8,128)(2,1)S(1)} all-to-all(bf16[32,2,16,512]{3,2,1,0:T(8,128)(2,1)S(1)} %second.1), channel_id=1, replica_groups=mesh['op_0'=2,'op_1'=4,'op_2'=4,'sector_0'=2,'sector_1'=2] {'op_0','op_1..., dimensions={0} | all-to-all | bytes 2097152 | tf_op jit(solution)/shard_map/all_to_all | solution.py:28
  87.7 0.0 copy-done.1
  87.7 0.0 copy-done
  87.7 3.6 %send.1 = bf16[4,512,512]{2,1,0:T(8,128)(2,1)S(1)} custom-call(s32[2,4]{1,0:T(2,128)S(1)} %bitcast.17, s32[1]{0:T(128)S(6)} %sub.3.refs_1_, bf16[32,2,16,512]{3,2,1,0:T(8,128)(2,1)S(1)} %all_to_all.22.refs_2_, bf16[8,512,512]{2,1,0:T(8,128)(2,1)S(1)} %bitcast.9, bf16[8,512,512]{2,1,0:T(8,128)(2,1)S(1)} %bitcast.13), custom_call_target="tpu_custom_call" | custom-call | flops 2147483648 | bytes 4194304 | tf_op jit(solution)/shard_map/send/pallas_call | solution.py:143
  91.3 0.1 collective-permute-start.4
  91.4 3.4 %keep.1.kept = f32[4,512,512]{2,1,0:T(8,128)S(1)} custom-call(s32[2,4]{1,0:T(2,128)S(1)} %bitcast.18, s32[1]{0:T(128)} %bitcast.1.refs_1_.core, bf16[32,2,16,512]{3,2,1,0:T(8,128)(2,1)S(1)} %all_to_all.22.refs_2_, bf16[8,512,512]{2,1,0:T(8,128)(2,1)S(1)} %bitcast.10, bf16[8,512,512]{2,1,0:T(8,128)(2,1)S(1)} %bitcast.14), custom_call_target="tpu_custom_call" | custom-call | flops 2147483648 | bytes 4194304 | tf_op jit(solution)/shard_map/keep/pallas_call | solution.py:143
  94.8 0.8 collective-permute-done.4.arrived
  95.5 1.2 pack.3
  96.8 1.7 %collective-permute-start.5 = (bf16[16,2,16,512]{3,2,1,0:T(8,128)(2,1)S(1)}, bf16[16,2,16,512]{3,2,1,0:T(8,128)(2,1)S(1)}, u32[]{:S(2)}, u32[]{:S(2)}) collective-permute-start(bf16[16,2,16,512]{3,2,1,0:T(8,128)(2,1)S(1)} %get-tuple-element.29), channel_id=1, source_target_pairs={{0,32},{1,9},{2,34},{3,11},{4,36},{5,13},{6,38},{7,15},{8,40},{9,1... | collective-permute-start | bytes 1572872 | tf_op jit(solution)/shard_map/ppermute | solution.py:167
  98.4 1.5 %collective-permute-start.6 = (bf16[16,2,16,512]{3,2,1,0:T(8,128)(2,1)S(1)}, bf16[16,2,16,512]{3,2,1,0:T(8,128)(2,1)S(1)}, u32[]{:S(2)}, u32[]{:S(2)}) collective-permute-start(bf16[16,2,16,512]{3,2,1,0:T(8,128)(2,1)S(1)} %get-tuple-element.30), channel_id=1, source_target_pairs={{0,16},{1,5},{2,18},{3,7},{4,20},{5,9},{6,22},{7,11},{8,24},{9,13}... | collective-permute-start | bytes 1572872 | tf_op jit(solution)/shard_map/ppermute | solution.py:167
  99.9 1.7 %collective-permute-start.7 = (bf16[16,2,16,512]{3,2,1,0:T(8,128)(2,1)S(1)}, bf16[16,2,16,512]{3,2,1,0:T(8,128)(2,1)S(1)}, u32[]{:S(2)}, u32[]{:S(2)}) collective-permute-start(bf16[16,2,16,512]{3,2,1,0:T(8,128)(2,1)S(1)} %get-tuple-element.31), channel_id=1, source_target_pairs={{0,48},{1,13},{2,50},{3,15},{4,52},{5,1},{6,54},{7,3},{8,56},{9,5}... | collective-permute-start | bytes 1572872 | tf_op jit(solution)/shard_map/ppermute | solution.py:167
  101.7 6.0 %collective-permute-done.5.first = bf16[16,2,16,512]{3,2,1,0:T(8,128)(2,1)S(1)} collective-permute-done((bf16[16,2,16,512]{3,2,1,0:T(8,128)(2,1)S(1)}, bf16[16,2,16,512]{3,2,1,0:T(8,128)(2,1)S(1)}, u32[]{:S(2)}, u32[]{:S(2)}) %collective-permute-start.5) | collective-permute-done | bytes 524320 | tf_op jit(solution)/shard_map/ppermute | solution.py:167
  107.6 5.5 %collective-permute-done.6.second = bf16[16,2,16,512]{3,2,1,0:T(8,128)(2,1)S(1)} collective-permute-done((bf16[16,2,16,512]{3,2,1,0:T(8,128)(2,1)S(1)}, bf16[16,2,16,512]{3,2,1,0:T(8,128)(2,1)S(1)}, u32[]{:S(2)}, u32[]{:S(2)}) %collective-permute-start.6) | collective-permute-done | bytes 524320 | tf_op jit(solution)/shard_map/ppermute | solution.py:167
  113.1 0.0 collective-permute-done.7.third
  113.1 0.3 meet.3
  113.4 14.1 %all_to_all.23.pieces = bf16[16,2,16,512]{3,2,1,0:T(8,128)(2,1)S(1)} all-to-all(bf16[16,2,16,512]{3,2,1,0:T(8,128)(2,1)S(1)} %meet.3), channel_id=1, replica_groups={{0,2,4,6,8,10,12,14,64,66,68,70,72,74,76,78},{16,18,20,22,24,26,28,30,8..., dimensions={0} | all-to-all | bytes 1048576 | tf_op jit(solution)/shard_map/all_to_all | solution.py:174
  127.6 0.7 last.1
Async XLA Ops:
  0.6 1.2 copy-start.2
  1.9 0.7 copy-start.5
  2.5 5.4 %copy-start.3 = (bf16[2,512,512]{2,1,0:T(8,128)(2,1)S(1)}, bf16[2,512,512]{2,1,0:T(8,128)(2,1)}, u32[]{:S(2)}) copy-start(bf16[2,512,512]{2,1,0:T(8,128)(2,1)} %wave.3) | copy-start | bytes 3145732
  2.6 5.4 %copy-start.6 = (s32[4,2]{0,1:T(2,128)S(1)}, s32[4,2]{0,1:T(2,128)}, u32[]{:S(2)}) copy-start(s32[4,2]{0,1:T(2,128)} %param.8) | copy-start | bytes 100
  7.9 5.2 %collective-permute-start = (bf16[4,512,512]{2,1,0:T(8,128)(2,1)S(1)}, bf16[4,512,512]{2,1,0:T(8,128)(2,1)S(1)}, u32[]{:S(2)}, u32[]{:S(2)}) collective-permute-start(bf16[4,512,512]{2,1,0:T(8,128)(2,1)S(1)} %load_send.1), channel_id=1, source_target_pairs={{0,1},{1,0},{2,3},{3,2},{4,5},{5,4},{6,7},{7,6},{8,9},{9,8},{10,11... | collective-permute-start | bytes 6291464 | tf_op jit(solution)/shard_map/ppermute | solution.py:309
  13.1 38.8 %copy-start.4 = (f32[2,16,512]{2,1,0:T(8,128)S(1)}, f32[2,16,512]{2,1,0:T(8,128)}, u32[]{:S(2)}) copy-start(f32[2,16,512]{2,1,0:T(8,128)} %precond.3) | copy-start | bytes 196612
  14.5 11.0 %collective-permute-start.1 = (bf16[16,2,16,512]{3,2,1,0:T(8,128)(2,1)S(1)}, bf16[16,2,16,512]{3,2,1,0:T(8,128)(2,1)S(1)}, u32[]{:S(2)}, u32[]{:S(2)}) collective-permute-start(bf16[16,2,16,512]{3,2,1,0:T(8,128)(2,1)S(1)} %get-tuple-element.22), channel_id=1, source_target_pairs={{0,32},{1,9},{2,34},{3,11},{4,36},{5,13},{6,38},{7,15},{8,40},{9,1... | collective-permute-start | bytes 1572872 | tf_op jit(solution)/shard_map/ppermute | solution.py:167
  18.2 12.8 %collective-permute-start.2 = (bf16[16,2,16,512]{3,2,1,0:T(8,128)(2,1)S(1)}, bf16[16,2,16,512]{3,2,1,0:T(8,128)(2,1)S(1)}, u32[]{:S(2)}, u32[]{:S(2)}) collective-permute-start(bf16[16,2,16,512]{3,2,1,0:T(8,128)(2,1)S(1)} %get-tuple-element.23), channel_id=1, source_target_pairs={{0,16},{1,5},{2,18},{3,7},{4,20},{5,9},{6,22},{7,11},{8,24},{9,13}... | collective-permute-start | bytes 1572872 | tf_op jit(solution)/shard_map/ppermute | solution.py:167
  18.3 12.8 %collective-permute-start.3 = (bf16[16,2,16,512]{3,2,1,0:T(8,128)(2,1)S(1)}, bf16[16,2,16,512]{3,2,1,0:T(8,128)(2,1)S(1)}, u32[]{:S(2)}, u32[]{:S(2)}) collective-permute-start(bf16[16,2,16,512]{3,2,1,0:T(8,128)(2,1)S(1)} %get-tuple-element.24), channel_id=1, source_target_pairs={{0,48},{1,13},{2,50},{3,15},{4,52},{5,1},{6,54},{7,3},{8,56},{9,5}... | collective-permute-start | bytes 1572872 | tf_op jit(solution)/shard_map/ppermute | solution.py:167
  31.1 56.6 %copy-start.1 = (bf16[4,2,512,512]{3,2,1,0:T(8,128)(2,1)S(1)}, bf16[4,2,512,512]{3,2,1,0:T(8,128)(2,1)}, u32[]{:S(2)}) copy-start(bf16[4,2,512,512]{3,2,1,0:T(8,128)(2,1)} %param.7) | copy-start | bytes 12582916
  31.4 56.3 %copy-start = (bf16[4,2,512,512]{3,2,1,0:T(8,128)(2,1)S(1)}, bf16[4,2,512,512]{3,2,1,0:T(8,128)(2,1)}, u32[]{:S(2)}) copy-start(bf16[4,2,512,512]{3,2,1,0:T(8,128)(2,1)} %param.6) | copy-start | bytes 12582916
  91.3 4.2 %collective-permute-start.4 = (bf16[4,512,512]{2,1,0:T(8,128)(2,1)S(1)}, bf16[4,512,512]{2,1,0:T(8,128)(2,1)S(1)}, u32[]{:S(2)}, u32[]{:S(2)}) collective-permute-start(bf16[4,512,512]{2,1,0:T(8,128)(2,1)S(1)} %send.1), channel_id=1, source_target_pairs={{0,1},{1,0},{2,3},{3,2},{4,5},{5,4},{6,7},{7,6},{8,9},{9,8},{10,11... | collective-permute-start | bytes 6291464 | tf_op jit(solution)/shard_map/ppermute | solution.py:309
  96.8 10.9 %collective-permute-start.5 = (bf16[16,2,16,512]{3,2,1,0:T(8,128)(2,1)S(1)}, bf16[16,2,16,512]{3,2,1,0:T(8,128)(2,1)S(1)}, u32[]{:S(2)}, u32[]{:S(2)}) collective-permute-start(bf16[16,2,16,512]{3,2,1,0:T(8,128)(2,1)S(1)} %get-tuple-element.29), channel_id=1, source_target_pairs={{0,32},{1,9},{2,34},{3,11},{4,36},{5,13},{6,38},{7,15},{8,40},{9,1... | collective-permute-start | bytes 1572872 | tf_op jit(solution)/shard_map/ppermute | solution.py:167
  98.4 14.7 %collective-permute-start.6 = (bf16[16,2,16,512]{3,2,1,0:T(8,128)(2,1)S(1)}, bf16[16,2,16,512]{3,2,1,0:T(8,128)(2,1)S(1)}, u32[]{:S(2)}, u32[]{:S(2)}) collective-permute-start(bf16[16,2,16,512]{3,2,1,0:T(8,128)(2,1)S(1)} %get-tuple-element.30), channel_id=1, source_target_pairs={{0,16},{1,5},{2,18},{3,7},{4,20},{5,9},{6,22},{7,11},{8,24},{9,13}... | collective-permute-start | bytes 1572872 | tf_op jit(solution)/shard_map/ppermute | solution.py:167
  99.9 13.2 %collective-permute-start.7 = (bf16[16,2,16,512]{3,2,1,0:T(8,128)(2,1)S(1)}, bf16[16,2,16,512]{3,2,1,0:T(8,128)(2,1)S(1)}, u32[]{:S(2)}, u32[]{:S(2)}) collective-permute-start(bf16[16,2,16,512]{3,2,1,0:T(8,128)(2,1)S(1)} %get-tuple-element.31), channel_id=1, source_target_pairs={{0,48},{1,13},{2,50},{3,15},{4,52},{5,1},{6,54},{7,3},{8,56},{9,5}... | collective-permute-start | bytes 1572872 | tf_op jit(solution)/shard_map/ppermute | solution.py:167

commit v6 on v5

--- a/solution.py
+++ b/solution.py
@@ -28,15 +28,15 @@
     return lax.all_to_all(pieces, axis, split_axis=0, concat_axis=0, tiled=True)
 
 
-def chosen_tasks(targets, core, order):
+def chosen_tasks(targets, core, order, at):
     local_sectors, terms = targets.shape
 
     def scan(task, count):
         target = targets[lax.rem(task, local_sectors), task // local_sectors]
         order[count] = task
-        return count + (lax.rem(target // local_sectors, 2) == core[0]).astype(jnp.int32)
-
-    return lax.fori_loop(0, local_sectors * terms, scan, jnp.int32(0))
+        return count + (lax.rem(target // local_sectors, 2) == core).astype(jnp.int32)
+
+    return lax.fori_loop(0, local_sectors * terms, scan, jnp.int32(at))
 
 
 def run_tasks(targets, order, count, source, lefts, rights, totals, touched, arrive):
@@ -86,71 +86,90 @@
             totals[slot] = jnp.zeros((width, width), F32)
 
 
-def apply_kernel(loading, sending, *refs):
-    targets, core, vector, left, right, out, touched, order = refs[:8]
-    rest = list(refs[8:])
-    totals = rest.pop(0) if sending else out
-    count = chosen_tasks(targets, core, order)
-    if loading:
-        lefts, rights, sems = rest
-
-        def copy(side, task):
-            source, buffer = ((left, lefts), (right, rights))[side]
-            return pltpu.make_async_copy(source.at[task], buffer.at[task], sems.at[side, task])
-
-        def start(sides, index, carry):
-            for side in sides:
-                copy(side, order[index]).start()
-            return carry
-
-        def arrive(side, task):
-            copy(side, task).wait()
-
-        early = jnp.minimum(count, 2)
-        lax.fori_loop(0, early, functools.partial(start, (0,)), 0)
-        lax.fori_loop(0, early, functools.partial(start, (1,)), 0)
-        lax.fori_loop(early, count, functools.partial(start, (0, 1)), 0)
-    else:
-        lefts, rights = left, right
-
-        def arrive(side, task):
-            del side, task
-
+def send_first_kernel(
+    targets, core, vector, left, right, out, lefts, rights, touched, order, totals, wave, sems, wave_sem
+):
+    tasks = left.shape[0]
+
+    def copy(side, task):
+        source, buffer = ((left, lefts), (right, rights))[side]
+        return pltpu.make_async_copy(source.at[task], buffer.at[task], sems.at[side, task])
+
+    def start(sides, index, carry):
+        for side in sides:
+            copy(side, order[index]).start()
+        return carry
+
+    def arrive(side, task):
+        copy(side, task).wait()
+
+    def rest(index, carry):
+        for side in (0, 1):
+            arrive(side, order[index])
+        return carry
+
+    whole = pltpu.make_async_copy(vector, wave, wave_sem)
+    whole.start()
+    count = chosen_tasks(targets, core[0], order, 0)
+    chosen_tasks(targets, 1 - core[0], order, count)
+    early = jnp.minimum(count, 2)
+    lax.fori_loop(0, early, functools.partial(start, (0,)), 0)
+    lax.fori_loop(0, early, functools.partial(start, (1,)), 0)
+    lax.fori_loop(early, tasks, functools.partial(start, (0, 1)), 0)
+    whole.wait()
+    run_tasks(
+        targets, order, count, lambda sector: wave[sector], lefts, rights, totals, touched, arrive
+    )
+    lax.fori_loop(count, tasks, rest, 0)
+    out[...] = totals[...].astype(BF16)
+
+
+def apply_kernel(sending, targets, core, vector, lefts, rights, out, touched, order, *totals):
     width = lefts.shape[1]
+    count = chosen_tasks(targets, core[0], order, 0)
 
     def source(sector):
-        if loading:
-            return vector[sector]
-        return vector[:, sector].reshape(width, width)
-
-    run_tasks(targets, order, count, source, lefts, rights, totals, touched, arrive)
+        return (vector[sector] if vector.shape[1] == width else vector[:, sector]).reshape(
+            width, width
+        )
+
+    def arrive(side, task):
+        del side, task
+
+    total = totals[0] if sending else out
+    run_tasks(targets, order, count, source, lefts, rights, total, touched, arrive)
     if sending:
-        out[...] = totals[...].astype(BF16)
-
-
-def apply_terms(targets, core, vector, left, right, loading, sending):
+        out[...] = total[...].astype(BF16)
+
+
+def apply_terms(targets, core, vector, left, right, first, sending):
     tasks, width, _ = left.shape
     slots = tasks // 2
     scratch = [pltpu.SMEM((slots,), jnp.int32), pltpu.SMEM((tasks + 1,), jnp.int32)]
     if sending:
         scratch += [pltpu.VMEM((slots, width, width), F32)]
-    if loading:
+    out = jax.ShapeDtypeStruct((slots, width, width), BF16 if sending else F32)
+    if first:
         scratch += [
-            pltpu.VMEM(left.shape, BF16),
-            pltpu.VMEM(left.shape, BF16),
+            pltpu.VMEM(vector.shape, BF16),
             pltpu.SemaphoreType.DMA((2, tasks)),
+            pltpu.SemaphoreType.DMA,
         ]
+        vector, left, right = (
+            pltpu.with_memory_space_constraint(value, pltpu.HBM) for value in (vector, left, right)
+        )
+        out = (out, jax.ShapeDtypeStruct(left.shape, BF16), jax.ShapeDtypeStruct(left.shape, BF16))
     return pl.pallas_call(
-        functools.partial(apply_kernel, loading, sending),
-        out_shape=jax.ShapeDtypeStruct((slots, width, width), BF16 if sending else F32),
-        in_specs=[SMEM, SMEM, VMEM] + [HBM if loading else VMEM] * 2,
-        out_specs=VMEM,
+        send_first_kernel if first else functools.partial(apply_kernel, sending),
+        out_shape=out,
+        in_specs=[SMEM, SMEM] + [HBM if first else VMEM] * 3,
+        out_specs=(VMEM, VMEM, VMEM) if first else VMEM,
         scratch_shapes=scratch,
-        compiler_params=room((50 if sending else 46) if loading else 8),
+        compiler_params=room(8 if first else 8),
         cost_estimate=pl.CostEstimate(
             flops=2 * tasks * width**3, bytes_accessed=2 * tasks * width**2, transcendentals=0
         ),
-        name=("load_" if loading else "") + ("send" if sending else "keep"),
+        name="send_first" if first else ("send" if sending else "keep"),
     )(targets, core, vector, left, right)
 
 
@@ -304,16 +323,18 @@
     row_shape = jax.ShapeDtypeStruct((local_sectors, rows, width), F32)
     offset, mine, theirs, ring = lax.optimization_barrier((offset, mine, theirs, ring))
 
-    def partial_pieces(vector, loading):
-        sent = apply_terms(targets, theirs, vector, left, right, loading, True)
+    def partial_pieces(vector, left, right, first):
+        sent = apply_terms(targets, theirs, vector, left, right, first, True)
+        if first:
+            sent, left, right = sent
         arrived = lax.ppermute(sent, CORE, [(0, 1), (1, 0)])
-        kept = apply_terms(targets, mine, vector, left, right, loading, False)
+        kept = apply_terms(targets, mine, vector, left, right, False, False)
         shape = (owners // 2, local_sectors, rows, width)
         own, *sent = pack(ring, mine, kept, arrived, shape)
         arrived = [along_ring(sent[step - 1], step) for step in (2, 1, 3)]
-        return across_rings(meet(own, arrived))
-
-    pieces = partial_pieces(wavefunction, True)
+        return across_rings(meet(own, arrived)), left, right
+
+    pieces, left, right = partial_pieces(wavefunction, left, right, True)
     devices = lax.axis_size(EVERY)
     sigma_first, again, sums = pl.pallas_call(
         first_kernel,
@@ -332,7 +353,7 @@
         compiler_params=room(4),
         name="second",
     )(offset, sums, again, wavefunction, preconditioner)
-    pieces = partial_pieces(exchange(copies, OP), False)
+    pieces, _, _ = partial_pieces(exchange(copies, OP), left, right, False)
     sigma_second = pl.pallas_call(
         sum_kernel,
         out_shape=row_shape,

time: 129 us -> 127 us (0.984)
  waiting for transfers between devices: 21.9 us -> 26.5 us
  blocking collectives: 69.1 us -> 66.7 us
  starting transfers between devices: 12.1 us -> 10.2 us
  Pallas kernels: 22.6 us -> 21.2 us
    all_to_all x2, blocking collectives: 34.5 us -> 31.1 us  [across_rings(): lax.all_to_all(pieces, EVERY, split_axis=0, concat_axis=0, axis_index_gro...]
    ppermute x2, waiting for transfers between devices: 0.77 us -> 3.79 us  [partial_pieces(): arrived = lax.ppermute(sent, CORE, [(0, 1), (1, 0)])]
    ppermute x6, starting transfers between devices: 11.9 us -> 10.1 us  [along_ring(): return lax.ppermute(value, EVERY, pairs)]
    ppermute x6, waiting for transfers between devices: 21.1 us -> 22.7 us  [along_ring(): return lax.ppermute(value, EVERY, pairs)]
  transfers between devices with their start and end apart: 8 -> 8, of which waited for: 6 -> 6; matrix products, arithmetic and copies ran while one was open for 0% -> 0% of each run, Pallas kernels for 7% -> 4%
where the time goes in v6:
time: 127 us; the launch traced here: 126 us
  blocking collectives  66.7 us (53%)
  waiting for transfers between devices  26.5 us (21%)
  Pallas kernels  21.2 us (17%)
  starting transfers between devices  10.2 us (8%)
    all_to_all x2, blocking collectives, exchange(): return lax.all_to_all(pieces, axis, split_axis=0, concat_axis=0, tiled=True)  35.6 us
    all_to_all x2, blocking collectives, across_rings(): lax.all_to_all(pieces, EVERY, split_axis=0, concat_axis=0, axis_index_gro...  31.1 us
    ppermute x6, waiting for transfers between devices, along_ring(): return lax.ppermute(value, EVERY, pairs)  22.7 us
    pallas_call x4, Pallas kernels, apply_terms(): pl.pallas_call(send_first_kernel if first else functools.partial(apply_ke...  16.2 us
    ppermute x6, starting transfers between devices, along_ring(): return lax.ppermute(value, EVERY, pairs)  10.1 us
    ppermute x2, waiting for transfers between devices, partial_pieces(): arrived = lax.ppermute(sent, CORE, [(0, 1), (1, 0)])  3.79 us
  transfers between devices with their start and end apart: 8, of which 6 were waited for; matrix products, arithmetic and copies ran while one was open for 0% of the time, Pallas kernels for 4%

profile of v6, /device:TPU:0, one launch (start us, length us, event | category | flops | bytes accessed | tf_op | source)
XLA Modules:
  0.0 126.1 jit_solution(17864408221260746949)
XLA Ops:
  0.6 0.0 copy-start.2
  0.7 0.7 copy-done.2
  1.3 0.0 copy-start
  1.3 7.0 %send_first.1 = (bf16[4,512,512]{2,1,0:T(8,128)(2,1)S(1)}, bf16[8,512,512]{2,1,0:T(8,128)(2,1)S(1)}, bf16[8,512,512]{2,1,0:T(8,128)(2,1)S(1)}) custom-call(s32[2,4]{1,0:T(2,128)S(1)} %bitcast.7, s32[1]{0:T(128)S(6)} %sub.3.core, bf16[2,512,512]{2,1,0:T(8,128)(2,1)} %wave.3, bf16[8,512,512]{2,1,0:T(8,128)(2,1)} %bitcast.11, bf16[8,512,512]{2,1,0:T(8,128)(2,1)} %bitcast.12), custom_call_target="tpu_custom_call" | custom-call | flops 2147483648 | bytes 4194304 | tf_op jit(solution)/shard_map/send_first/pallas_call | solution.py:162
  8.3 0.1 collective-permute-start
  8.4 0.0 copy-done
  8.4 2.2 %keep.2.kept = f32[4,512,512]{2,1,0:T(8,128)S(1)} custom-call(s32[2,4]{1,0:T(2,128)S(1)} %bitcast.8, s32[1]{0:T(128)} %bitcast.1.core, bf16[2,512,512]{2,1,0:T(8,128)(2,1)S(1)} %copy-done, bf16[8,512,512]{2,1,0:T(8,128)(2,1)S(1)} %get-tuple-element.24.lefts, bf16[8,512,512]{2,1,0:T(8,128)(2,1)S(1)} %get-tuple-element.25.rights), custom_call_target="tpu_custom_call" | custom-call | flops 2147483648 | bytes 4194304 | tf_op jit(solution)/shard_map/keep/pallas_call | solution.py:162
  10.7 0.0 copy-start.1
  10.7 1.9 %collective-permute-done.arrived = bf16[4,512,512]{2,1,0:T(8,128)(2,1)S(1)} collective-permute-done((bf16[4,512,512]{2,1,0:T(8,128)(2,1)S(1)}, bf16[4,512,512]{2,1,0:T(8,128)(2,1)S(1)}, u32[]{:S(2)}, u32[]{:S(2)}) %collective-permute-start) | collective-permute-done | bytes 2097184 | tf_op jit(solution)/shard_map/ppermute | solution.py:330
  12.6 1.2 pack.2
  13.8 2.5 %collective-permute-start.1 = (bf16[16,2,16,512]{3,2,1,0:T(8,128)(2,1)S(1)}, bf16[16,2,16,512]{3,2,1,0:T(8,128)(2,1)S(1)}, u32[]{:S(2)}, u32[]{:S(2)}) collective-permute-start(bf16[16,2,16,512]{3,2,1,0:T(8,128)(2,1)S(1)} %get-tuple-element.28), channel_id=1, source_target_pairs={{0,32},{1,9},{2,34},{3,11},{4,36},{5,13},{6,38},{7,15},{8,40},{9,1... | collective-permute-start | bytes 1572872 | tf_op jit(solution)/shard_map/ppermute | solution.py:186
  16.3 0.5 collective-permute-start.2
  16.7 2.8 %collective-permute-start.3 = (bf16[16,2,16,512]{3,2,1,0:T(8,128)(2,1)S(1)}, bf16[16,2,16,512]{3,2,1,0:T(8,128)(2,1)S(1)}, u32[]{:S(2)}, u32[]{:S(2)}) collective-permute-start(bf16[16,2,16,512]{3,2,1,0:T(8,128)(2,1)S(1)} %get-tuple-element.30), channel_id=1, source_target_pairs={{0,48},{1,13},{2,50},{3,15},{4,52},{5,1},{6,54},{7,3},{8,56},{9,5}... | collective-permute-start | bytes 1572872 | tf_op jit(solution)/shard_map/ppermute | solution.py:186
  19.5 5.2 %collective-permute-done.1.first = bf16[16,2,16,512]{3,2,1,0:T(8,128)(2,1)S(1)} collective-permute-done((bf16[16,2,16,512]{3,2,1,0:T(8,128)(2,1)S(1)}, bf16[16,2,16,512]{3,2,1,0:T(8,128)(2,1)S(1)}, u32[]{:S(2)}, u32[]{:S(2)}) %collective-permute-start.1) | collective-permute-done | bytes 524320 | tf_op jit(solution)/shard_map/ppermute | solution.py:186
  24.7 5.5 %collective-permute-done.2.second = bf16[16,2,16,512]{3,2,1,0:T(8,128)(2,1)S(1)} collective-permute-done((bf16[16,2,16,512]{3,2,1,0:T(8,128)(2,1)S(1)}, bf16[16,2,16,512]{3,2,1,0:T(8,128)(2,1)S(1)}, u32[]{:S(2)}, u32[]{:S(2)}) %collective-permute-start.2) | collective-permute-done | bytes 524320 | tf_op jit(solution)/shard_map/ppermute | solution.py:186
  30.2 0.0 collective-permute-done.3.third
  30.2 0.2 meet.2
  30.4 17.8 %all_to_all.20.pieces = bf16[16,2,16,512]{3,2,1,0:T(8,128)(2,1)S(1)} all-to-all(bf16[16,2,16,512]{3,2,1,0:T(8,128)(2,1)S(1)} %meet.2), channel_id=1, replica_groups={{0,2,4,6,8,10,12,14,64,66,68,70,72,74,76,78},{16,18,20,22,24,26,28,30,8..., dimensions={0} | all-to-all | bytes 1048576 | tf_op jit(solution)/shard_map/all_to_all | solution.py:193
  48.2 0.0 copy-done.1
  48.2 0.7 first.1
  48.9 15.0 %all_to_all.21.sums = f32[128,1,128]{2,1,0:T(1,128)S(1)} all-to-all(f32[128,1,128]{2,1,0:T(1,128)S(1)} %get-tuple-element.32), channel_id=1, replica_groups=mesh['op_0'=2,'op_1'=4,'op_2'=4,'sector_0'=2,'sector_1'=2] {'op_0','op_1..., dimensions={0} | all-to-all | bytes 131072 | tf_op jit(solution)/shard_map/all_to_all | solution.py:28
  63.9 0.6 second.1
  64.5 20.6 %all_to_all.22.vector = bf16[32,2,16,512]{3,2,1,0:T(8,128)(2,1)S(1)} all-to-all(bf16[32,2,16,512]{3,2,1,0:T(8,128)(2,1)S(1)} %second.1), channel_id=1, replica_groups=mesh['op_0'=2,'op_1'=4,'op_2'=4,'sector_0'=2,'sector_1'=2] {'op_0','op_1..., dimensions={0} | all-to-all | bytes 2097152 | tf_op jit(solution)/shard_map/all_to_all | solution.py:28
  85.2 4.8 %send.1 = bf16[4,512,512]{2,1,0:T(8,128)(2,1)S(1)} custom-call(s32[2,4]{1,0:T(2,128)S(1)} %bitcast.9, s32[1]{0:T(128)S(6)} %sub.3.core, bf16[32,2,16,512]{3,2,1,0:T(8,128)(2,1)S(1)} %all_to_all.22.vector, bf16[8,512,512]{2,1,0:T(8,128)(2,1)S(1)} %get-tuple-element.24.lefts, bf16[8,512,512]{2,1,0:T(8,128)(2,1)S(1)} %get-tuple-element.25.rights), custom_call_target="tpu_custom_call" | custom-call | flops 2147483648 | bytes 4194304 | tf_op jit(solution)/shard_map/send/pallas_call | solution.py:162
  89.9 0.1 collective-permute-start.4
  90.0 2.2 %keep.3.kept = f32[4,512,512]{2,1,0:T(8,128)S(1)} custom-call(s32[2,4]{1,0:T(2,128)S(1)} %bitcast.10, s32[1]{0:T(128)} %bitcast.1.core, bf16[32,2,16,512]{3,2,1,0:T(8,128)(2,1)S(1)} %all_to_all.22.vector, bf16[8,512,512]{2,1,0:T(8,128)(2,1)S(1)} %get-tuple-element.24.lefts, bf16[8,512,512]{2,1,0:T(8,128)(2,1)S(1)} %get-tuple-element.25.rights), custom_call_target="tpu_custom_call" | custom-call | flops 2147483648 | bytes 4194304 | tf_op jit(solution)/shard_map/keep/pallas_call | solution.py:162
  92.3 1.9 %collective-permute-done.4.arrived = bf16[4,512,512]{2,1,0:T(8,128)(2,1)S(1)} collective-permute-done((bf16[4,512,512]{2,1,0:T(8,128)(2,1)S(1)}, bf16[4,512,512]{2,1,0:T(8,128)(2,1)S(1)}, u32[]{:S(2)}, u32[]{:S(2)}) %collective-permute-start.4) | collective-permute-done | bytes 2097184 | tf_op jit(solution)/shard_map/ppermute | solution.py:330
  94.2 1.2 pack.3
  95.4 1.1 collective-permute-start.5
  96.5 0.4 collective-permute-start.6
  96.9 2.8 %collective-permute-start.7 = (bf16[16,2,16,512]{3,2,1,0:T(8,128)(2,1)S(1)}, bf16[16,2,16,512]{3,2,1,0:T(8,128)(2,1)S(1)}, u32[]{:S(2)}, u32[]{:S(2)}) collective-permute-start(bf16[16,2,16,512]{3,2,1,0:T(8,128)(2,1)S(1)} %get-tuple-element.37), channel_id=1, source_target_pairs={{0,48},{1,13},{2,50},{3,15},{4,52},{5,1},{6,54},{7,3},{8,56},{9,5}... | collective-permute-start | bytes 1572872 | tf_op jit(solution)/shard_map/ppermute | solution.py:186
  99.8 6.5 %collective-permute-done.5.first = bf16[16,2,16,512]{3,2,1,0:T(8,128)(2,1)S(1)} collective-permute-done((bf16[16,2,16,512]{3,2,1,0:T(8,128)(2,1)S(1)}, bf16[16,2,16,512]{3,2,1,0:T(8,128)(2,1)S(1)}, u32[]{:S(2)}, u32[]{:S(2)}) %collective-permute-start.5) | collective-permute-done | bytes 524320 | tf_op jit(solution)/shard_map/ppermute | solution.py:186
  106.3 5.5 %collective-permute-done.6.second = bf16[16,2,16,512]{3,2,1,0:T(8,128)(2,1)S(1)} collective-permute-done((bf16[16,2,16,512]{3,2,1,0:T(8,128)(2,1)S(1)}, bf16[16,2,16,512]{3,2,1,0:T(8,128)(2,1)S(1)}, u32[]{:S(2)}, u32[]{:S(2)}) %collective-permute-start.6) | collective-permute-done | bytes 524320 | tf_op jit(solution)/shard_map/ppermute | solution.py:186
  111.8 0.0 collective-permute-done.7.third
  111.8 0.3 meet.3
  112.1 13.3 %all_to_all.23.pieces = bf16[16,2,16,512]{3,2,1,0:T(8,128)(2,1)S(1)} all-to-all(bf16[16,2,16,512]{3,2,1,0:T(8,128)(2,1)S(1)} %meet.3), channel_id=1, replica_groups={{0,2,4,6,8,10,12,14,64,66,68,70,72,74,76,78},{16,18,20,22,24,26,28,30,8..., dimensions={0} | all-to-all | bytes 1048576 | tf_op jit(solution)/shard_map/all_to_all | solution.py:193
  125.4 0.7 last.1
Async XLA Ops:
  0.6 0.7 copy-start.2
  1.3 7.1 %copy-start = (bf16[2,512,512]{2,1,0:T(8,128)(2,1)S(1)}, bf16[2,512,512]{2,1,0:T(8,128)(2,1)}, u32[]{:S(2)}) copy-start(bf16[2,512,512]{2,1,0:T(8,128)(2,1)} %wave.3) | copy-start | bytes 3145732
  8.3 4.2 %collective-permute-start = (bf16[4,512,512]{2,1,0:T(8,128)(2,1)S(1)}, bf16[4,512,512]{2,1,0:T(8,128)(2,1)S(1)}, u32[]{:S(2)}, u32[]{:S(2)}) collective-permute-start(bf16[4,512,512]{2,1,0:T(8,128)(2,1)S(1)} %get-tuple-element.26), channel_id=1, source_target_pairs={{0,1},{1,0},{2,3},{3,2},{4,5},{5,4},{6,7},{7,6},{8,9},{9,8},{10,11... | collective-permute-start | bytes 6291464 | tf_op jit(solution)/shard_map/ppermute | solution.py:330
  10.7 37.5 %copy-start.1 = (f32[2,16,512]{2,1,0:T(8,128)S(1)}, f32[2,16,512]{2,1,0:T(8,128)}, u32[]{:S(2)}) copy-start(f32[2,16,512]{2,1,0:T(8,128)} %precond.3) | copy-start | bytes 196612
  13.8 10.9 %collective-permute-start.1 = (bf16[16,2,16,512]{3,2,1,0:T(8,128)(2,1)S(1)}, bf16[16,2,16,512]{3,2,1,0:T(8,128)(2,1)S(1)}, u32[]{:S(2)}, u32[]{:S(2)}) collective-permute-start(bf16[16,2,16,512]{3,2,1,0:T(8,128)(2,1)S(1)} %get-tuple-element.28), channel_id=1, source_target_pairs={{0,32},{1,9},{2,34},{3,11},{4,36},{5,13},{6,38},{7,15},{8,40},{9,1... | collective-permute-start | bytes 1572872 | tf_op jit(solution)/shard_map/ppermute | solution.py:186
  16.3 13.9 %collective-permute-start.2 = (bf16[16,2,16,512]{3,2,1,0:T(8,128)(2,1)S(1)}, bf16[16,2,16,512]{3,2,1,0:T(8,128)(2,1)S(1)}, u32[]{:S(2)}, u32[]{:S(2)}) collective-permute-start(bf16[16,2,16,512]{3,2,1,0:T(8,128)(2,1)S(1)} %get-tuple-element.29), channel_id=1, source_target_pairs={{0,16},{1,5},{2,18},{3,7},{4,20},{5,9},{6,22},{7,11},{8,24},{9,13}... | collective-permute-start | bytes 1572872 | tf_op jit(solution)/shard_map/ppermute | solution.py:186
  16.7 13.5 %collective-permute-start.3 = (bf16[16,2,16,512]{3,2,1,0:T(8,128)(2,1)S(1)}, bf16[16,2,16,512]{3,2,1,0:T(8,128)(2,1)S(1)}, u32[]{:S(2)}, u32[]{:S(2)}) collective-permute-start(bf16[16,2,16,512]{3,2,1,0:T(8,128)(2,1)S(1)} %get-tuple-element.30), channel_id=1, source_target_pairs={{0,48},{1,13},{2,50},{3,15},{4,52},{5,1},{6,54},{7,3},{8,56},{9,5}... | collective-permute-start | bytes 1572872 | tf_op jit(solution)/shard_map/ppermute | solution.py:186
  89.9 4.2 %collective-permute-start.4 = (bf16[4,512,512]{2,1,0:T(8,128)(2,1)S(1)}, bf16[4,512,512]{2,1,0:T(8,128)(2,1)S(1)}, u32[]{:S(2)}, u32[]{:S(2)}) collective-permute-start(bf16[4,512,512]{2,1,0:T(8,128)(2,1)S(1)} %send.1), channel_id=1, source_target_pairs={{0,1},{1,0},{2,3},{3,2},{4,5},{5,4},{6,7},{7,6},{8,9},{9,8},{10,11... | collective-permute-start | bytes 6291464 | tf_op jit(solution)/shard_map/ppermute | solution.py:330
  95.4 10.9 %collective-permute-start.5 = (bf16[16,2,16,512]{3,2,1,0:T(8,128)(2,1)S(1)}, bf16[16,2,16,512]{3,2,1,0:T(8,128)(2,1)S(1)}, u32[]{:S(2)}, u32[]{:S(2)}) collective-permute-start(bf16[16,2,16,512]{3,2,1,0:T(8,128)(2,1)S(1)} %get-tuple-element.35), channel_id=1, source_target_pairs={{0,32},{1,9},{2,34},{3,11},{4,36},{5,13},{6,38},{7,15},{8,40},{9,1... | collective-permute-start | bytes 1572872 | tf_op jit(solution)/shard_map/ppermute | solution.py:186
  96.5 15.3 %collective-permute-start.6 = (bf16[16,2,16,512]{3,2,1,0:T(8,128)(2,1)S(1)}, bf16[16,2,16,512]{3,2,1,0:T(8,128)(2,1)S(1)}, u32[]{:S(2)}, u32[]{:S(2)}) collective-permute-start(bf16[16,2,16,512]{3,2,1,0:T(8,128)(2,1)S(1)} %get-tuple-element.36), channel_id=1, source_target_pairs={{0,16},{1,5},{2,18},{3,7},{4,20},{5,9},{6,22},{7,11},{8,24},{9,13}... | collective-permute-start | bytes 1572872 | tf_op jit(solution)/shard_map/ppermute | solution.py:186
  96.9 14.9 %collective-permute-start.7 = (bf16[16,2,16,512]{3,2,1,0:T(8,128)(2,1)S(1)}, bf16[16,2,16,512]{3,2,1,0:T(8,128)(2,1)S(1)}, u32[]{:S(2)}, u32[]{:S(2)}) collective-permute-start(bf16[16,2,16,512]{3,2,1,0:T(8,128)(2,1)S(1)} %get-tuple-element.37), channel_id=1, source_target_pairs={{0,48},{1,13},{2,50},{3,15},{4,52},{5,1},{6,54},{7,3},{8,56},{9,5}... | collective-permute-start | bytes 1572872 | tf_op jit(solution)/shard_map/ppermute | solution.py:186

commit v7 on v6

--- a/solution.py
+++ b/solution.py
@@ -28,7 +28,7 @@
     return lax.all_to_all(pieces, axis, split_axis=0, concat_axis=0, tiled=True)
 
 
-def chosen_tasks(targets, core, order, at):
+def listed(targets, core, order, at):
     local_sectors, terms = targets.shape
 
     def scan(task, count):
@@ -36,22 +36,24 @@
         order[count] = task
         return count + (lax.rem(target // local_sectors, 2) == core).astype(jnp.int32)
 
-    return lax.fori_loop(0, local_sectors * terms, scan, jnp.int32(at))
-
-
-def run_tasks(targets, order, count, source, lefts, rights, totals, touched, arrive):
+    return lax.fori_loop(0, local_sectors * terms, scan, at)
+
+
+def slot_of(targets, task):
     local_sectors = targets.shape[0]
-    slots, width, _ = totals.shape
-    for slot in range(slots):
-        touched[slot] = 0
+    target = targets[lax.rem(task, local_sectors), task // local_sectors]
+    return target // (2 * local_sectors) * local_sectors + lax.rem(target, local_sectors)
+
+
+def run_tasks(targets, order, begin, end, source, lefts, rights, totals, touched, arrive):
+    local_sectors = targets.shape[0]
 
     def middle_of(task):
         vector = source(lax.rem(task, local_sectors))
         return jnp.dot(lefts[task], vector, preferred_element_type=F32).astype(BF16)
 
     def add(task, middle):
-        target = targets[lax.rem(task, local_sectors), task // local_sectors]
-        slot = target // (2 * local_sectors) * local_sectors + lax.rem(target, local_sectors)
+        slot = slot_of(targets, task)
         fresh = touched[slot] == 0
         touched[slot] = 1
         share = lax.dot_general(
@@ -60,7 +62,7 @@
         totals[slot] = share + jnp.where(fresh, 0.0, totals[slot])
 
     def pair(index, carry):
-        tasks = order[2 * index], order[2 * index + 1]
+        tasks = order[begin + 2 * index], order[begin + 2 * index + 1]
         for task in tasks:
             arrive(0, task)
         middles = [middle_of(task) for task in tasks]
@@ -70,30 +72,40 @@
             add(task, middle)
         return carry
 
-    lax.fori_loop(0, count // 2, pair, 0)
-
-    @pl.when(lax.rem(count, 2) == 1)
+    lax.fori_loop(0, (end - begin) // 2, pair, 0)
+
+    @pl.when(lax.rem(end - begin, 2) == 1)
     def _():
-        task = order[count - 1]
+        task = order[end - 1]
         arrive(0, task)
         arrive(1, task)
         add(task, middle_of(task))
 
-    for slot in range(slots):
+
+def clear(touched):
+    for slot in range(touched.shape[0]):
+        touched[slot] = 0
+
+
+def fill(totals, touched):
+    for slot in range(totals.shape[0]):
 
         @pl.when(touched[slot] == 0)
         def _(slot=slot):
-            totals[slot] = jnp.zeros((width, width), F32)
-
-
-def send_first_kernel(
-    targets, core, vector, left, right, out, lefts, rights, touched, order, totals, wave, sems, wave_sem
-):
-    tasks = left.shape[0]
+            totals[slot] = jnp.zeros(totals.shape[1:], F32)
+
+
+def early_kernel(first, targets, core, vector, left, right, out, kept, *refs):
+    if first:
+        lefts, rights, touched, order, totals, wave, sems, wave_sem = refs
+    else:
+        lefts, rights = left, right
+        touched, order, totals = refs
+    tasks, width, _ = lefts.shape
 
     def copy(side, task):
-        source, buffer = ((left, lefts), (right, rights))[side]
-        return pltpu.make_async_copy(source.at[task], buffer.at[task], sems.at[side, task])
+        origin, buffer = ((left, lefts), (right, rights))[side]
+        return pltpu.make_async_copy(origin.at[task], buffer.at[task], sems.at[side, task])
 
     def start(sides, index, carry):
         for side in sides:
@@ -101,32 +113,50 @@
         return carry
 
     def arrive(side, task):
-        copy(side, task).wait()
+        if first:
+            copy(side, task).wait()
 
     def rest(index, carry):
         for side in (0, 1):
             arrive(side, order[index])
         return carry
 
-    whole = pltpu.make_async_copy(vector, wave, wave_sem)
-    whole.start()
-    count = chosen_tasks(targets, core[0], order, 0)
-    chosen_tasks(targets, 1 - core[0], order, count)
-    early = jnp.minimum(count, 2)
-    lax.fori_loop(0, early, functools.partial(start, (0,)), 0)
-    lax.fori_loop(0, early, functools.partial(start, (1,)), 0)
-    lax.fori_loop(early, tasks, functools.partial(start, (0, 1)), 0)
-    whole.wait()
-    run_tasks(
-        targets, order, count, lambda sector: wave[sector], lefts, rights, totals, touched, arrive
-    )
-    lax.fori_loop(count, tasks, rest, 0)
+    def source(sector):
+        return wave[sector] if first else vector[:, sector].reshape(width, width)
+
+    if first:
+        whole = pltpu.make_async_copy(vector, wave, wave_sem)
+        whole.start()
+    count = listed(targets, 1 - core[0], order, jnp.int32(0))
+    listed(targets, core[0], order, count)
+    if first:
+        early = jnp.minimum(count, 2)
+        lax.fori_loop(0, early, functools.partial(start, (0,)), 0)
+        lax.fori_loop(0, early, functools.partial(start, (1,)), 0)
+        lax.fori_loop(early, tasks, functools.partial(start, (0, 1)), 0)
+        whole.wait()
+    end = jnp.maximum(count, tasks // 2)
+    clear(touched)
+    run_tasks(targets, order, 0, count, source, lefts, rights, totals, touched, arrive)
+    fill(totals, touched)
     out[...] = totals[...].astype(BF16)
-
-
-def apply_kernel(sending, targets, core, vector, lefts, rights, out, touched, order, *totals):
-    width = lefts.shape[1]
-    count = chosen_tasks(targets, core[0], order, 0)
+    clear(touched)
+    run_tasks(targets, order, count, end, source, lefts, rights, kept, touched, arrive)
+    if first:
+        lax.fori_loop(end, tasks, rest, 0)
+
+
+def late_kernel(targets, core, vector, lefts, rights, begun, kept, touched, order):
+    del begun
+    tasks, width, _ = lefts.shape
+    count = listed(targets, 1 - core[0], order, jnp.int32(0))
+    listed(targets, core[0], order, count)
+    end = jnp.maximum(count, tasks // 2)
+    clear(touched)
+
+    def mark(index, carry):
+        touched[slot_of(targets, order[index])] = 1
+        return carry
 
     def source(sector):
         return (vector[sector] if vector.shape[1] == width else vector[:, sector]).reshape(
@@ -136,19 +166,21 @@
     def arrive(side, task):
         del side, task
 
-    total = totals[0] if sending else out
-    run_tasks(targets, order, count, source, lefts, rights, total, touched, arrive)
-    if sending:
-        out[...] = total[...].astype(BF16)
-
-
-def apply_terms(targets, core, vector, left, right, first, sending):
+    lax.fori_loop(count, end, mark, 0)
+    run_tasks(targets, order, end, tasks, source, lefts, rights, kept, touched, arrive)
+    fill(kept, touched)
+
+
+def apply_early(targets, core, vector, left, right, first):
     tasks, width, _ = left.shape
     slots = tasks // 2
-    scratch = [pltpu.SMEM((slots,), jnp.int32), pltpu.SMEM((tasks + 1,), jnp.int32)]
-    if sending:
-        scratch += [pltpu.VMEM((slots, width, width), F32)]
-    out = jax.ShapeDtypeStruct((slots, width, width), BF16 if sending else F32)
+    block = (slots, width, width)
+    out = [jax.ShapeDtypeStruct(block, BF16), jax.ShapeDtypeStruct(block, F32)]
+    scratch = [
+        pltpu.SMEM((slots,), jnp.int32),
+        pltpu.SMEM((tasks + 1,), jnp.int32),
+        pltpu.VMEM(block, F32),
+    ]
     if first:
         scratch += [
             pltpu.VMEM(vector.shape, BF16),
@@ -158,19 +190,41 @@
         vector, left, right = (
             pltpu.with_memory_space_constraint(value, pltpu.HBM) for value in (vector, left, right)
         )
-        out = (out, jax.ShapeDtypeStruct(left.shape, BF16), jax.ShapeDtypeStruct(left.shape, BF16))
+        out += [jax.ShapeDtypeStruct(left.shape, BF16)] * 2
     return pl.pallas_call(
-        send_first_kernel if first else functools.partial(apply_kernel, sending),
+        functools.partial(early_kernel, first),
         out_shape=out,
         in_specs=[SMEM, SMEM] + [HBM if first else VMEM] * 3,
-        out_specs=(VMEM, VMEM, VMEM) if first else VMEM,
+        out_specs=[VMEM] * len(out),
         scratch_shapes=scratch,
-        compiler_params=room(8 if first else 8),
-        cost_estimate=pl.CostEstimate(
-            flops=2 * tasks * width**3, bytes_accessed=2 * tasks * width**2, transcendentals=0
-        ),
-        name="send_first" if first else ("send" if sending else "keep"),
+        compiler_params=room(8),
+        cost_estimate=work(tasks, width),
+        name="early_first" if first else "early",
     )(targets, core, vector, left, right)
+
+
+def apply_late(targets, core, vector, left, right, begun):
+    tasks, width, _ = left.shape
+    return pl.pallas_call(
+        late_kernel,
+        out_shape=jax.ShapeDtypeStruct(begun.shape, F32),
+        in_specs=[SMEM, SMEM] + [VMEM] * 4,
+        out_specs=VMEM,
+        scratch_shapes=[
+            pltpu.SMEM((tasks // 2,), jnp.int32),
+            pltpu.SMEM((tasks + 1,), jnp.int32),
+        ],
+        input_output_aliases={5: 0},
+        compiler_params=room(8),
+        cost_estimate=work(tasks, width),
+        name="late",
+    )(targets, core, vector, left, right, begun)
+
+
+def work(tasks, width):
+    return pl.CostEstimate(
+        flops=2 * tasks * width**3, bytes_accessed=2 * tasks * width**2, transcendentals=0
+    )
 
 
 def place(op_0, op_1, op_2, half, core):
@@ -197,23 +251,24 @@
 
 def pack_kernel(ring, core, kept, arrived, own, *sent):
     others, local_sectors, rows, _ = own.shape
-
-    def one_block(index, carry):
-        other, sector = index // local_sectors, lax.rem(index, local_sectors)
-        low, at, half = other // 8, lax.rem(other // 2, 4), lax.rem(other, 2)
-        slot = half * local_sectors + sector
-        for step in range(4):
-            to = lax.rem(ring[0] + step, 4)
-            block = low * 16 + jnp.where(core[0] == 0, to * 4 + at, at * 4 + to)
-            here = pl.ds(pl.multiple_of(block * rows, rows), rows)
+    near, far = rows, 4 * rows
+    ring_stride = jnp.where(core[0] == 0, far, near)
+    at_stride = jnp.where(core[0] == 0, near, far)
+    to = [lax.rem(ring[0] + step, 4) * ring_stride for step in range(4)]
+
+    def one_place(place, carry):
+        base = place // 4 * (16 * rows) + lax.rem(place, 4) * at_stride
+        for step, half, sector in itertools.product(range(4), range(2), range(local_sectors)):
+            here = pl.ds(pl.multiple_of(base + to[step], rows), rows)
+            slot = half * local_sectors + sector
             total = kept[slot, here, :] + arrived[slot, here, :].astype(F32)
             if step == 0:
-                own[other, sector] = total
+                own[2 * place + half, sector] = total
             else:
-                sent[step - 1][other, sector] = total.astype(BF16)
-        return carry
-
-    lax.fori_loop(0, others * local_sectors, one_block, 0, unroll=8)
+                sent[step - 1][2 * place + half, sector] = total.astype(BF16)
+        return carry
+
+    lax.fori_loop(0, others // 2, one_place, 0)
 
 
 def pack(ring, core, kept, arrived, shape):
@@ -314,21 +369,19 @@
     owners = lax.axis_size(OP)
     offset = (lax.axis_index(OP) * rows).reshape(1)
     mine = lax.axis_index(CORE).reshape(1)
-    theirs = 1 - mine
     ring = jnp.where(mine == 0, lax.axis_index("op_1"), lax.axis_index("op_2"))
     targets = target_sector.T
     left, right = (
         blocks.reshape(-1, width, width) for blocks in (left_blocks, right_blocks)
     )
     row_shape = jax.ShapeDtypeStruct((local_sectors, rows, width), F32)
-    offset, mine, theirs, ring = lax.optimization_barrier((offset, mine, theirs, ring))
+    offset, mine, ring = lax.optimization_barrier((offset, mine, ring))
 
     def partial_pieces(vector, left, right, first):
-        sent = apply_terms(targets, theirs, vector, left, right, first, True)
-        if first:
-            sent, left, right = sent
+        sent, begun, *blocks = apply_early(targets, mine, vector, left, right, first)
+        left, right = blocks if first else (left, right)
         arrived = lax.ppermute(sent, CORE, [(0, 1), (1, 0)])
-        kept = apply_terms(targets, mine, vector, left, right, False, False)
+        kept = apply_late(targets, mine, vector, left, right, begun)
         shape = (owners // 2, local_sectors, rows, width)
         own, *sent = pack(ring, mine, kept, arrived, shape)
         arrived = [along_ring(sent[step - 1], step) for step in (2, 1, 3)]

time: 127 us -> 125 us (0.984)
  waiting for transfers between devices: 26.5 us -> 23.4 us
  blocking collectives: 66.7 us -> 68.1 us
    ppermute x2, waiting for transfers between devices: 3.79 us -> 0.9 us  [partial_pieces(): arrived = lax.ppermute(sent, CORE, [(0, 1), (1, 0)])]
    pallas_call x2, Pallas kernels: 2.45 us -> 0.85 us  [pack(): pl.pallas_call(pack_kernel, out_shape=[jax.ShapeDtypeStruct(shape, F32)]...]
    all_to_all x2, blocking collectives: 31.1 us -> 32.5 us  [across_rings(): lax.all_to_all(pieces, EVERY, split_axis=0, concat_axis=0, axis_index_gro...]
  transfers between devices with their start and end apart: 8 -> 8, of which waited for: 6 -> 8; matrix products, arithmetic and copies ran while one was open for 0% -> 0% of each run, Pallas kernels for 4% -> 6%
where the time goes in v7:
time: 125 us
  blocking collectives  68.1 us (54%)
  waiting for transfers between devices  23.4 us (19%)
  Pallas kernels  20.4 us (16%)
  starting transfers between devices  11.4 us (9%)
    all_to_all x2, blocking collectives, exchange(): return lax.all_to_all(pieces, axis, split_axis=0, concat_axis=0, tiled=True)  35.6 us
    all_to_all x2, blocking collectives, across_rings(): lax.all_to_all(pieces, EVERY, split_axis=0, concat_axis=0, axis_index_gro...  32.5 us
    ppermute x6, waiting for transfers between devices, along_ring(): return lax.ppermute(value, EVERY, pairs)  22.5 us
    ppermute x6, starting transfers between devices, along_ring(): return lax.ppermute(value, EVERY, pairs)  11.3 us
    pallas_call x2, Pallas kernels, apply_early(): pl.pallas_call(functools.partial(early_kernel, first), out_shape=out, in_...  9.67 us
    pallas_call x2, Pallas kernels, apply_late(): pl.pallas_call(late_kernel, out_shape=jax.ShapeDtypeStruct(begun.shape, F...  7.36 us
  transfers between devices with their start and end apart: 8, of which 8 were waited for; matrix products, arithmetic and copies ran while one was open for 0% of the time, Pallas kernels for 6%

profile of v7, /device:TPU:0, one launch (start us, length us, event | category | flops | bytes accessed | tf_op | source)
XLA Modules:
  0.0 124.7 jit_solution(12571052089157394203)
XLA Ops:
  0.6 0.0 copy-start.2
  0.7 0.7 copy-done.2
  1.3 0.0 copy-start
  1.3 5.7 %early_first.1 = (bf16[4,512,512]{2,1,0:T(8,128)(2,1)S(1)}, f32[4,512,512]{2,1,0:T(8,128)S(1)}, bf16[8,512,512]{2,1,0:T(8,128)(2,1)S(1)}, bf16[8,512,512]{2,1,0:T(8,128)(2,1)S(1)}) custom-call(s32[2,4]{1,0:T(2,128)S(1)} %bitcast.7, s32[1]{0:T(128)} %bitcast.1.core, bf16[2,512,512]{2,1,0:T(8,128)(2,1)} %wave.3, bf16[8,512,512]{2,1,0:T(8,128)(2,1)} %bitcast.11, ...), custom_call_target="tpu_custom_call" | custom-call | flops 2147483648 | bytes 4194304 | tf_op jit(solution)/shard_map/early_first/pallas_call | solution.py:194
  7.0 0.1 collective-permute-start
  7.1 0.0 copy-done
  7.1 3.6 %late.2.kept = f32[4,512,512]{2,1,0:T(8,128)S(1)} custom-call(s32[2,4]{1,0:T(2,128)S(1)} %bitcast.8, s32[1]{0:T(128)} %bitcast.1.core, bf16[2,512,512]{2,1,0:T(8,128)(2,1)S(1)} %copy-done, bf16[8,512,512]{2,1,0:T(8,128)(2,1)S(1)} %get-tuple-element.25.lefts.left, ...), custom_call_target="tpu_custom_call", output_to_operand_aliasing={{}: (5, {})} | custom-call | flops 2147483648 | bytes 4194304 | tf_op jit(solution)/shard_map/late/pallas_call | solution.py:208
  10.7 0.0 copy-start.1
  10.7 0.5 collective-permute-done.arrived
  11.3 0.4 pack.2
  11.7 3.3 %collective-permute-start.1 = (bf16[16,2,16,512]{3,2,1,0:T(8,128)(2,1)S(1)}, bf16[16,2,16,512]{3,2,1,0:T(8,128)(2,1)S(1)}, u32[]{:S(2)}, u32[]{:S(2)}) collective-permute-start(bf16[16,2,16,512]{3,2,1,0:T(8,128)(2,1)S(1)} %get-tuple-element.30), channel_id=1, source_target_pairs={{0,32},{1,9},{2,34},{3,11},{4,36},{5,13},{6,38},{7,15},{8,40},{9,1... | collective-permute-start | bytes 1572872 | tf_op jit(solution)/shard_map/ppermute | solution.py:240
  15.0 1.1 collective-permute-start.2
  16.2 2.1 %collective-permute-start.3 = (bf16[16,2,16,512]{3,2,1,0:T(8,128)(2,1)S(1)}, bf16[16,2,16,512]{3,2,1,0:T(8,128)(2,1)S(1)}, u32[]{:S(2)}, u32[]{:S(2)}) collective-permute-start(bf16[16,2,16,512]{3,2,1,0:T(8,128)(2,1)S(1)} %get-tuple-element.32), channel_id=1, source_target_pairs={{0,48},{1,13},{2,50},{3,15},{4,52},{5,1},{6,54},{7,3},{8,56},{9,5}... | collective-permute-start | bytes 1572872 | tf_op jit(solution)/shard_map/ppermute | solution.py:240
  18.3 4.3 %collective-permute-done.1.first = bf16[16,2,16,512]{3,2,1,0:T(8,128)(2,1)S(1)} collective-permute-done((bf16[16,2,16,512]{3,2,1,0:T(8,128)(2,1)S(1)}, bf16[16,2,16,512]{3,2,1,0:T(8,128)(2,1)S(1)}, u32[]{:S(2)}, u32[]{:S(2)}) %collective-permute-start.1) | collective-permute-done | bytes 524320 | tf_op jit(solution)/shard_map/ppermute | solution.py:240
  22.6 5.5 %collective-permute-done.2.second = bf16[16,2,16,512]{3,2,1,0:T(8,128)(2,1)S(1)} collective-permute-done((bf16[16,2,16,512]{3,2,1,0:T(8,128)(2,1)S(1)}, bf16[16,2,16,512]{3,2,1,0:T(8,128)(2,1)S(1)}, u32[]{:S(2)}, u32[]{:S(2)}) %collective-permute-start.2) | collective-permute-done | bytes 524320 | tf_op jit(solution)/shard_map/ppermute | solution.py:240
  28.1 0.9 collective-permute-done.3.third
  29.0 0.2 meet.2
  29.2 18.0 %all_to_all.20.pieces = bf16[16,2,16,512]{3,2,1,0:T(8,128)(2,1)S(1)} all-to-all(bf16[16,2,16,512]{3,2,1,0:T(8,128)(2,1)S(1)} %meet.2), channel_id=1, replica_groups={{0,2,4,6,8,10,12,14,64,66,68,70,72,74,76,78},{16,18,20,22,24,26,28,30,8..., dimensions={0} | all-to-all | bytes 1048576 | tf_op jit(solution)/shard_map/all_to_all | solution.py:247
  47.3 0.0 copy-done.1
  47.3 0.7 first.1
  48.0 14.9 %all_to_all.21.sums = f32[128,1,128]{2,1,0:T(1,128)S(1)} all-to-all(f32[128,1,128]{2,1,0:T(1,128)S(1)} %get-tuple-element.34), channel_id=1, replica_groups=mesh['op_0'=2,'op_1'=4,'op_2'=4,'sector_0'=2,'sector_1'=2] {'op_0','op_1..., dimensions={0} | all-to-all | bytes 131072 | tf_op jit(solution)/shard_map/all_to_all | solution.py:28
  62.9 0.6 second.1
  63.5 20.6 %all_to_all.22.vector = bf16[32,2,16,512]{3,2,1,0:T(8,128)(2,1)S(1)} all-to-all(bf16[32,2,16,512]{3,2,1,0:T(8,128)(2,1)S(1)} %second.1), channel_id=1, replica_groups=mesh['op_0'=2,'op_1'=4,'op_2'=4,'sector_0'=2,'sector_1'=2] {'op_0','op_1..., dimensions={0} | all-to-all | bytes 2097152 | tf_op jit(solution)/shard_map/all_to_all | solution.py:28
  84.2 4.0 %early.1 = (bf16[4,512,512]{2,1,0:T(8,128)(2,1)S(1)}, f32[4,512,512]{2,1,0:T(8,128)S(1)}) custom-call(s32[2,4]{1,0:T(2,128)S(1)} %bitcast.9, s32[1]{0:T(128)} %bitcast.1.core, bf16[32,2,16,512]{3,2,1,0:T(8,128)(2,1)S(1)} %all_to_all.22.vector, bf16[8,512,512]{2,1,0:T(8,128)(2,1)S(1)} %get-tuple-element.25.lefts.left, ...), custom_call_target="tpu_custom_call" | custom-call | flops 2147483648 | bytes 4194304 | tf_op jit(solution)/shard_map/early/pallas_call | solution.py:194
  88.1 0.1 collective-permute-start.4
  88.2 3.8 %late.3.kept = f32[4,512,512]{2,1,0:T(8,128)S(1)} custom-call(s32[2,4]{1,0:T(2,128)S(1)} %bitcast.10, s32[1]{0:T(128)} %bitcast.1.core, bf16[32,2,16,512]{3,2,1,0:T(8,128)(2,1)S(1)} %all_to_all.22.vector, bf16[8,512,512]{2,1,0:T(8,128)(2,1)S(1)} %get-tuple-element.25.lefts.left, ...), custom_call_target="tpu_custom_call", output_to_operand_aliasing={{}: (5, {})} | custom-call | flops 2147483648 | bytes 4194304 | tf_op jit(solution)/shard_map/late/pallas_call | solution.py:208
  92.0 0.4 collective-permute-done.4.arrived
  92.4 0.4 pack.3
  92.8 1.4 %collective-permute-start.5 = (bf16[16,2,16,512]{3,2,1,0:T(8,128)(2,1)S(1)}, bf16[16,2,16,512]{3,2,1,0:T(8,128)(2,1)S(1)}, u32[]{:S(2)}, u32[]{:S(2)}) collective-permute-start(bf16[16,2,16,512]{3,2,1,0:T(8,128)(2,1)S(1)} %get-tuple-element.39), channel_id=1, source_target_pairs={{0,32},{1,9},{2,34},{3,11},{4,36},{5,13},{6,38},{7,15},{8,40},{9,1... | collective-permute-start | bytes 1572872 | tf_op jit(solution)/shard_map/ppermute | solution.py:240
  94.3 2.2 %collective-permute-start.6 = (bf16[16,2,16,512]{3,2,1,0:T(8,128)(2,1)S(1)}, bf16[16,2,16,512]{3,2,1,0:T(8,128)(2,1)S(1)}, u32[]{:S(2)}, u32[]{:S(2)}) collective-permute-start(bf16[16,2,16,512]{3,2,1,0:T(8,128)(2,1)S(1)} %get-tuple-element.40), channel_id=1, source_target_pairs={{0,16},{1,5},{2,18},{3,7},{4,20},{5,9},{6,22},{7,11},{8,24},{9,13}... | collective-permute-start | bytes 1572872 | tf_op jit(solution)/shard_map/ppermute | solution.py:240
  96.5 1.0 collective-permute-start.7
  97.5 6.2 %collective-permute-done.5.first = bf16[16,2,16,512]{3,2,1,0:T(8,128)(2,1)S(1)} collective-permute-done((bf16[16,2,16,512]{3,2,1,0:T(8,128)(2,1)S(1)}, bf16[16,2,16,512]{3,2,1,0:T(8,128)(2,1)S(1)}, u32[]{:S(2)}, u32[]{:S(2)}) %collective-permute-start.5) | collective-permute-done | bytes 524320 | tf_op jit(solution)/shard_map/ppermute | solution.py:240
  103.7 5.5 %collective-permute-done.6.second = bf16[16,2,16,512]{3,2,1,0:T(8,128)(2,1)S(1)} collective-permute-done((bf16[16,2,16,512]{3,2,1,0:T(8,128)(2,1)S(1)}, bf16[16,2,16,512]{3,2,1,0:T(8,128)(2,1)S(1)}, u32[]{:S(2)}, u32[]{:S(2)}) %collective-permute-start.6) | collective-permute-done | bytes 524320 | tf_op jit(solution)/shard_map/ppermute | solution.py:240
  109.2 0.1 collective-permute-done.7.third
  109.3 0.2 meet.3
  109.5 14.5 %all_to_all.23.pieces = bf16[16,2,16,512]{3,2,1,0:T(8,128)(2,1)S(1)} all-to-all(bf16[16,2,16,512]{3,2,1,0:T(8,128)(2,1)S(1)} %meet.3), channel_id=1, replica_groups={{0,2,4,6,8,10,12,14,64,66,68,70,72,74,76,78},{16,18,20,22,24,26,28,30,8..., dimensions={0} | all-to-all | bytes 1048576 | tf_op jit(solution)/shard_map/all_to_all | solution.py:247
  124.0 0.7 last.1
Async XLA Ops:
  0.6 0.7 copy-start.2
  1.3 5.8 %copy-start = (bf16[2,512,512]{2,1,0:T(8,128)(2,1)S(1)}, bf16[2,512,512]{2,1,0:T(8,128)(2,1)}, u32[]{:S(2)}) copy-start(bf16[2,512,512]{2,1,0:T(8,128)(2,1)} %wave.3) | copy-start | bytes 3145732
  7.0 4.2 %collective-permute-start = (bf16[4,512,512]{2,1,0:T(8,128)(2,1)S(1)}, bf16[4,512,512]{2,1,0:T(8,128)(2,1)S(1)}, u32[]{:S(2)}, u32[]{:S(2)}) collective-permute-start(bf16[4,512,512]{2,1,0:T(8,128)(2,1)S(1)} %get-tuple-element.28), channel_id=1, source_target_pairs={{0,1},{1,0},{2,3},{3,2},{4,5},{5,4},{6,7},{7,6},{8,9},{9,8},{10,11... | collective-permute-start | bytes 6291464 | tf_op jit(solution)/shard_map/ppermute | solution.py:383
  10.7 36.5 %copy-start.1 = (f32[2,16,512]{2,1,0:T(8,128)S(1)}, f32[2,16,512]{2,1,0:T(8,128)}, u32[]{:S(2)}) copy-start(f32[2,16,512]{2,1,0:T(8,128)} %precond.3) | copy-start | bytes 196612
  11.7 10.9 %collective-permute-start.1 = (bf16[16,2,16,512]{3,2,1,0:T(8,128)(2,1)S(1)}, bf16[16,2,16,512]{3,2,1,0:T(8,128)(2,1)S(1)}, u32[]{:S(2)}, u32[]{:S(2)}) collective-permute-start(bf16[16,2,16,512]{3,2,1,0:T(8,128)(2,1)S(1)} %get-tuple-element.30), channel_id=1, source_target_pairs={{0,32},{1,9},{2,34},{3,11},{4,36},{5,13},{6,38},{7,15},{8,40},{9,1... | collective-permute-start | bytes 1572872 | tf_op jit(solution)/shard_map/ppermute | solution.py:240
  15.0 13.0 %collective-permute-start.2 = (bf16[16,2,16,512]{3,2,1,0:T(8,128)(2,1)S(1)}, bf16[16,2,16,512]{3,2,1,0:T(8,128)(2,1)S(1)}, u32[]{:S(2)}, u32[]{:S(2)}) collective-permute-start(bf16[16,2,16,512]{3,2,1,0:T(8,128)(2,1)S(1)} %get-tuple-element.31), channel_id=1, source_target_pairs={{0,16},{1,5},{2,18},{3,7},{4,20},{5,9},{6,22},{7,11},{8,24},{9,13}... | collective-permute-start | bytes 1572872 | tf_op jit(solution)/shard_map/ppermute | solution.py:240
  16.2 12.8 %collective-permute-start.3 = (bf16[16,2,16,512]{3,2,1,0:T(8,128)(2,1)S(1)}, bf16[16,2,16,512]{3,2,1,0:T(8,128)(2,1)S(1)}, u32[]{:S(2)}, u32[]{:S(2)}) collective-permute-start(bf16[16,2,16,512]{3,2,1,0:T(8,128)(2,1)S(1)} %get-tuple-element.32), channel_id=1, source_target_pairs={{0,48},{1,13},{2,50},{3,15},{4,52},{5,1},{6,54},{7,3},{8,56},{9,5}... | collective-permute-start | bytes 1572872 | tf_op jit(solution)/shard_map/ppermute | solution.py:240
  88.1 4.2 %collective-permute-start.4 = (bf16[4,512,512]{2,1,0:T(8,128)(2,1)S(1)}, bf16[4,512,512]{2,1,0:T(8,128)(2,1)S(1)}, u32[]{:S(2)}, u32[]{:S(2)}) collective-permute-start(bf16[4,512,512]{2,1,0:T(8,128)(2,1)S(1)} %get-tuple-element.37), channel_id=1, source_target_pairs={{0,1},{1,0},{2,3},{3,2},{4,5},{5,4},{6,7},{7,6},{8,9},{9,8},{10,11... | collective-permute-start | bytes 6291464 | tf_op jit(solution)/shard_map/ppermute | solution.py:383
  92.8 10.9 %collective-permute-start.5 = (bf16[16,2,16,512]{3,2,1,0:T(8,128)(2,1)S(1)}, bf16[16,2,16,512]{3,2,1,0:T(8,128)(2,1)S(1)}, u32[]{:S(2)}, u32[]{:S(2)}) collective-permute-start(bf16[16,2,16,512]{3,2,1,0:T(8,128)(2,1)S(1)} %get-tuple-element.39), channel_id=1, source_target_pairs={{0,32},{1,9},{2,34},{3,11},{4,36},{5,13},{6,38},{7,15},{8,40},{9,1... | collective-permute-start | bytes 1572872 | tf_op jit(solution)/shard_map/ppermute | solution.py:240
  94.3 14.9 %collective-permute-start.6 = (bf16[16,2,16,512]{3,2,1,0:T(8,128)(2,1)S(1)}, bf16[16,2,16,512]{3,2,1,0:T(8,128)(2,1)S(1)}, u32[]{:S(2)}, u32[]{:S(2)}) collective-permute-start(bf16[16,2,16,512]{3,2,1,0:T(8,128)(2,1)S(1)} %get-tuple-element.40), channel_id=1, source_target_pairs={{0,16},{1,5},{2,18},{3,7},{4,20},{5,9},{6,22},{7,11},{8,24},{9,13}... | collective-permute-start | bytes 1572872 | tf_op jit(solution)/shard_map/ppermute | solution.py:240
  96.5 12.8 %collective-permute-start.7 = (bf16[16,2,16,512]{3,2,1,0:T(8,128)(2,1)S(1)}, bf16[16,2,16,512]{3,2,1,0:T(8,128)(2,1)S(1)}, u32[]{:S(2)}, u32[]{:S(2)}) collective-permute-start(bf16[16,2,16,512]{3,2,1,0:T(8,128)(2,1)S(1)} %get-tuple-element.41), channel_id=1, source_target_pairs={{0,48},{1,13},{2,50},{3,15},{4,52},{5,1},{6,54},{7,3},{8,56},{9,5}... | collective-permute-start | bytes 1572872 | tf_op jit(solution)/shard_map/ppermute | solution.py:240

commit v8 on v7

--- a/solution.py
+++ b/solution.py
@@ -1,5 +1,6 @@
 import functools
 import itertools
+import random
 
 import jax
 import jax.numpy as jnp
@@ -24,8 +25,37 @@
     return pltpu.CompilerParams(vmem_limit_bytes=mebibytes * 2**20)
 
 
-def exchange(pieces, axis):
-    return lax.all_to_all(pieces, axis, split_axis=0, concat_axis=0, tiled=True)
+def place(op_0, op_1, op_2, half, core):
+    return (((op_0 * 4 + op_1) * 4 + op_2) * 2 + half) * 2 + core
+
+
+def mixed(members, seed):
+    members = list(members)
+    random.Random(seed).shuffle(members)
+    return members
+
+
+OP_ORDER = mixed(itertools.product(range(2), range(4), range(4)), 8)
+REST_ORDER = mixed(itertools.product(range(2), range(4), range(2)), 3)
+OP_AT = [(low * 4 + first) * 4 + second for low, first, second in OP_ORDER]
+REST_AT = [(low * 4 + at) * 2 + half for low, at, half in REST_ORDER]
+
+
+def exchange(pieces, groups):
+    return lax.all_to_all(
+        pieces, EVERY, split_axis=0, concat_axis=0, axis_index_groups=groups, tiled=True
+    )
+
+
+def with_everyone(pieces):
+    return exchange(pieces, [mixed(range(lax.axis_size(EVERY)), 0)])
+
+
+def over_terms(pieces):
+    sectors = itertools.product(range(2), range(2))
+    return exchange(
+        pieces, [[place(*op, half, core) for op in OP_ORDER] for half, core in sectors]
+    )
 
 
 def listed(targets, core, order, at):
@@ -100,8 +130,11 @@
         lefts, rights, touched, order, totals, wave, sems, wave_sem = refs
     else:
         lefts, rights = left, right
-        touched, order, totals = refs
-    tasks, width, _ = lefts.shape
+        wave, touched, order, totals = refs
+        rows = vector.shape[2]
+        for index, owner in enumerate(OP_AT):
+            wave[:, owner * rows : (owner + 1) * rows, :] = vector[index]
+    tasks = lefts.shape[0]
 
     def copy(side, task):
         origin, buffer = ((left, lefts), (right, rights))[side]
@@ -122,7 +155,7 @@
         return carry
 
     def source(sector):
-        return wave[sector] if first else vector[:, sector].reshape(width, width)
+        return wave[sector]
 
     if first:
         whole = pltpu.make_async_copy(vector, wave, wave_sem)
@@ -148,7 +181,7 @@
 
 def late_kernel(targets, core, vector, lefts, rights, begun, kept, touched, order):
     del begun
-    tasks, width, _ = lefts.shape
+    tasks = lefts.shape[0]
     count = listed(targets, 1 - core[0], order, jnp.int32(0))
     listed(targets, core[0], order, count)
     end = jnp.maximum(count, tasks // 2)
@@ -159,9 +192,7 @@
         return carry
 
     def source(sector):
-        return (vector[sector] if vector.shape[1] == width else vector[:, sector]).reshape(
-            width, width
-        )
+        return vector[sector]
 
     def arrive(side, task):
         del side, task
@@ -191,6 +222,8 @@
             pltpu.with_memory_space_constraint(value, pltpu.HBM) for value in (vector, left, right)
         )
         out += [jax.ShapeDtypeStruct(left.shape, BF16)] * 2
+    else:
+        out += [jax.ShapeDtypeStruct((vector.shape[1], width, width), BF16)]
     return pl.pallas_call(
         functools.partial(early_kernel, first),
         out_shape=out,
@@ -227,10 +260,6 @@
     )
 
 
-def place(op_0, op_1, op_2, half, core):
-    return (((op_0 * 4 + op_1) * 4 + op_2) * 2 + half) * 2 + core
-
-
 def along_ring(value, step):
     pairs = []
     for op_0, op_1, op_2, half in itertools.product(range(2), range(4), range(4), range(2)):
@@ -241,12 +270,10 @@
 
 
 def across_rings(pieces):
-    rest = list(itertools.product(range(2), range(4), range(2)))
+    rest = REST_ORDER
     groups = [[place(low, ring, at, half, 0) for low, at, half in rest] for ring in range(4)]
     groups += [[place(low, at, ring, half, 1) for low, at, half in rest] for ring in range(4)]
-    return lax.all_to_all(
-        pieces, EVERY, split_axis=0, concat_axis=0, axis_index_groups=groups, tiled=True
-    )
+    return exchange(pieces, groups)
 
 
 def pack_kernel(ring, core, kept, arrived, own, *sent):
@@ -283,13 +310,10 @@
 
 
 def meet_kernel(own, first, second, third, out):
-    def one(index, carry):
+    for to, index in enumerate(REST_AT):
         total = own[index] + first[index].astype(F32)
         total += second[index].astype(F32) + third[index].astype(F32)
-        out[index] = total.astype(BF16)
-        return carry
-
-    lax.fori_loop(0, own.shape[0], one, 0, unroll=4)
+        out[to] = total.astype(BF16)
 
 
 def meet(own, arrived):
@@ -378,8 +402,11 @@
     offset, mine, ring = lax.optimization_barrier((offset, mine, ring))
 
     def partial_pieces(vector, left, right, first):
-        sent, begun, *blocks = apply_early(targets, mine, vector, left, right, first)
-        left, right = blocks if first else (left, right)
+        sent, begun, *rest = apply_early(targets, mine, vector, left, right, first)
+        if first:
+            left, right = rest
+        else:
+            (vector,) = rest
         arrived = lax.ppermute(sent, CORE, [(0, 1), (1, 0)])
         kept = apply_late(targets, mine, vector, left, right, begun)
         shape = (owners // 2, local_sectors, rows, width)
@@ -397,7 +424,7 @@
         compiler_params=room(4),
         name="first",
     )(offset, pieces, wavefunction, preconditioner)
-    sums = exchange(sums, EVERY)
+    sums = with_everyone(sums)
     copies = pl.pallas_call(
         second_kernel,
         out_shape=jax.ShapeDtypeStruct((owners, local_sectors, rows, width), BF16),
@@ -406,7 +433,7 @@
         compiler_params=room(4),
         name="second",
     )(offset, sums, again, wavefunction, preconditioner)
-    pieces, _, _ = partial_pieces(exchange(copies, OP), left, right, False)
+    pieces, _, _ = partial_pieces(over_terms(copies), left, right, False)
     sigma_second = pl.pallas_call(
         sum_kernel,
         out_shape=row_shape,

time: 125 us -> 125 us (level)
  blocking collectives: 68.1 us -> 65.9 us
  starting transfers between devices: 11.4 us -> 13.1 us
    all_to_all x4, blocking collectives: 68.1 us -> 65.9 us  [exchange(): lax.all_to_all(pieces, EVERY, split_axis=0, concat_axis=0, axis_index_gro...]
    ppermute x6, starting transfers between devices: 11.3 us -> 12.7 us  [along_ring(): return lax.ppermute(value, EVERY, pairs)]
where the time goes in v8:
time: 125 us; the launch traced here: 124 us
  blocking collectives  65.9 us (53%)
  waiting for transfers between devices  23.9 us (19%)
  Pallas kernels  20.1 us (16%)
  starting transfers between devices  13.1 us (10%)
    all_to_all x4, blocking collectives, exchange(): lax.all_to_all(pieces, EVERY, split_axis=0, concat_axis=0, axis_index_gro...  65.9 us
    ppermute x6, waiting for transfers between devices, along_ring(): return lax.ppermute(value, EVERY, pairs)  22.8 us
    ppermute x6, starting transfers between devices, along_ring(): return lax.ppermute(value, EVERY, pairs)  12.7 us
    pallas_call x2, Pallas kernels, apply_early(): pl.pallas_call(functools.partial(early_kernel, first), out_shape=out, in_...  9.6 us
    pallas_call x2, Pallas kernels, apply_late(): pl.pallas_call(late_kernel, out_shape=jax.ShapeDtypeStruct(begun.shape, F...  7.18 us
  transfers between devices with their start and end apart: 8, of which 8 were waited for; matrix products, arithmetic and copies ran while one was open for 0% of the time, Pallas kernels for 6%

profile of v8, /device:TPU:0, one launch (start us, length us, event | category | flops | bytes accessed | tf_op | source)
XLA Modules:
  0.0 124.5 jit_solution(16664206128605622387)
XLA Ops:
  0.6 0.0 copy-start.2
  0.7 0.7 copy-done.2
  1.3 0.0 copy-start
  1.3 5.6 %early_first.1 = (bf16[4,512,512]{2,1,0:T(8,128)(2,1)S(1)}, f32[4,512,512]{2,1,0:T(8,128)S(1)}, bf16[8,512,512]{2,1,0:T(8,128)(2,1)S(1)}, bf16[8,512,512]{2,1,0:T(8,128)(2,1)S(1)}) custom-call(s32[2,4]{1,0:T(2,128)S(1)} %bitcast.7, s32[1]{0:T(128)} %bitcast.1.core, bf16[2,512,512]{2,1,0:T(8,128)(2,1)} %wave.3, bf16[8,512,512]{2,1,0:T(8,128)(2,1)} %bitcast.11, ...), custom_call_target="tpu_custom_call" | custom-call | flops 2147483648 | bytes 4194304 | tf_op jit(solution)/shard_map/early_first/pallas_call | solution.py:227
  6.9 0.1 collective-permute-start
  7.0 0.0 copy-done
  7.1 3.6 %late.2.kept = f32[4,512,512]{2,1,0:T(8,128)S(1)} custom-call(s32[2,4]{1,0:T(2,128)S(1)} %bitcast.8, s32[1]{0:T(128)} %bitcast.1.core, bf16[2,512,512]{2,1,0:T(8,128)(2,1)S(1)} %copy-done, bf16[8,512,512]{2,1,0:T(8,128)(2,1)S(1)} %get-tuple-element.26.lefts.left, ...), custom_call_target="tpu_custom_call", output_to_operand_aliasing={{}: (5, {})} | custom-call | flops 2147483648 | bytes 4194304 | tf_op jit(solution)/shard_map/late/pallas_call | solution.py:241
  10.7 0.0 copy-start.1
  10.7 0.5 collective-permute-done.arrived
  11.2 0.4 pack.2
  11.6 3.9 %collective-permute-start.1 = (bf16[16,2,16,512]{3,2,1,0:T(8,128)(2,1)S(1)}, bf16[16,2,16,512]{3,2,1,0:T(8,128)(2,1)S(1)}, u32[]{:S(2)}, u32[]{:S(2)}) collective-permute-start(bf16[16,2,16,512]{3,2,1,0:T(8,128)(2,1)S(1)} %get-tuple-element.31), channel_id=1, source_target_pairs={{0,32},{1,9},{2,34},{3,11},{4,36},{5,13},{6,38},{7,15},{8,40},{9,1... | collective-permute-start | bytes 1572872 | tf_op jit(solution)/shard_map/ppermute | solution.py:269
  15.5 1.3 %collective-permute-start.2 = (bf16[16,2,16,512]{3,2,1,0:T(8,128)(2,1)S(1)}, bf16[16,2,16,512]{3,2,1,0:T(8,128)(2,1)S(1)}, u32[]{:S(2)}, u32[]{:S(2)}) collective-permute-start(bf16[16,2,16,512]{3,2,1,0:T(8,128)(2,1)S(1)} %get-tuple-element.32), channel_id=1, source_target_pairs={{0,16},{1,5},{2,18},{3,7},{4,20},{5,9},{6,22},{7,11},{8,24},{9,13}... | collective-permute-start | bytes 1572872 | tf_op jit(solution)/shard_map/ppermute | solution.py:269
  16.8 1.9 %collective-permute-start.3 = (bf16[16,2,16,512]{3,2,1,0:T(8,128)(2,1)S(1)}, bf16[16,2,16,512]{3,2,1,0:T(8,128)(2,1)S(1)}, u32[]{:S(2)}, u32[]{:S(2)}) collective-permute-start(bf16[16,2,16,512]{3,2,1,0:T(8,128)(2,1)S(1)} %get-tuple-element.33), channel_id=1, source_target_pairs={{0,48},{1,13},{2,50},{3,15},{4,52},{5,1},{6,54},{7,3},{8,56},{9,5}... | collective-permute-start | bytes 1572872 | tf_op jit(solution)/shard_map/ppermute | solution.py:269
  18.7 4.0 %collective-permute-done.1.first = bf16[16,2,16,512]{3,2,1,0:T(8,128)(2,1)S(1)} collective-permute-done((bf16[16,2,16,512]{3,2,1,0:T(8,128)(2,1)S(1)}, bf16[16,2,16,512]{3,2,1,0:T(8,128)(2,1)S(1)}, u32[]{:S(2)}, u32[]{:S(2)}) %collective-permute-start.1) | collective-permute-done | bytes 524320 | tf_op jit(solution)/shard_map/ppermute | solution.py:269
  22.8 5.5 %collective-permute-done.2.second = bf16[16,2,16,512]{3,2,1,0:T(8,128)(2,1)S(1)} collective-permute-done((bf16[16,2,16,512]{3,2,1,0:T(8,128)(2,1)S(1)}, bf16[16,2,16,512]{3,2,1,0:T(8,128)(2,1)S(1)}, u32[]{:S(2)}, u32[]{:S(2)}) %collective-permute-start.2) | collective-permute-done | bytes 524320 | tf_op jit(solution)/shard_map/ppermute | solution.py:269
  28.3 1.4 %collective-permute-done.3.third = bf16[16,2,16,512]{3,2,1,0:T(8,128)(2,1)S(1)} collective-permute-done((bf16[16,2,16,512]{3,2,1,0:T(8,128)(2,1)S(1)}, bf16[16,2,16,512]{3,2,1,0:T(8,128)(2,1)S(1)}, u32[]{:S(2)}, u32[]{:S(2)}) %collective-permute-start.3) | collective-permute-done | bytes 524320 | tf_op jit(solution)/shard_map/ppermute | solution.py:269
  29.7 0.2 meet.2
  29.9 17.1 %all_to_all.20.pieces = bf16[16,2,16,512]{3,2,1,0:T(8,128)(2,1)S(1)} all-to-all(bf16[16,2,16,512]{3,2,1,0:T(8,128)(2,1)S(1)} %meet.2), channel_id=1, replica_groups={{8,70,68,74,72,6,12,0,2,78,76,10,4,64,66,14},{24,86,84,90,88,22,28,16,1..., dimensions={0} | all-to-all | bytes 1048576 | tf_op jit(solution)/shard_map/all_to_all | solution.py:45
  46.9 0.0 copy-done.1
  47.0 0.7 first.1
  47.7 15.0 %all_to_all.21.sums = f32[128,1,128]{2,1,0:T(1,128)S(1)} all-to-all(f32[128,1,128]{2,1,0:T(1,128)S(1)} %get-tuple-element.35), channel_id=1, replica_groups={{48,43,108,72,29,14,54,23,124,94,10,44,3,49,83,111,16,95,107,101,110,22..., dimensions={0} | all-to-all | bytes 131072 | tf_op jit(solution)/shard_map/all_to_all | solution.py:45
  62.7 0.6 second.1
  63.3 20.2 %all_to_all.22.vector = bf16[32,2,16,512]{3,2,1,0:T(8,128)(2,1)S(1)} all-to-all(bf16[32,2,16,512]{3,2,1,0:T(8,128)(2,1)S(1)} %second.1), channel_id=1, replica_groups={{20,92,76,32,96,72,40,120,52,100,84,12,36,104,80,68,60,124,0,116,108,64..., dimensions={0} | all-to-all | bytes 2097152 | tf_op jit(solution)/shard_map/all_to_all | solution.py:45
  83.5 4.0 %early.1 = (bf16[4,512,512]{2,1,0:T(8,128)(2,1)S(1)}, f32[4,512,512]{2,1,0:T(8,128)S(1)}, bf16[2,512,512]{2,1,0:T(8,128)(2,1)S(1)}) custom-call(s32[2,4]{1,0:T(2,128)S(1)} %bitcast.9, s32[1]{0:T(128)} %bitcast.1.core, bf16[32,2,16,512]{3,2,1,0:T(8,128)(2,1)S(1)} %all_to_all.22.vector, bf16[8,512,512]{2,1,0:T(8,128)(2,1)S(1)} %get-tuple-element.26.lefts.left, ...), custom_call_target="tpu_custom_call" | custom-call | flops 2147483648 | bytes 4194304 | tf_op jit(solution)/shard_map/early/pallas_call | solution.py:227
  87.5 0.3 collective-permute-start.4
  87.8 3.6 %late.3.kept = f32[4,512,512]{2,1,0:T(8,128)S(1)} custom-call(s32[2,4]{1,0:T(2,128)S(1)} %bitcast.10, s32[1]{0:T(128)} %bitcast.1.core, bf16[2,512,512]{2,1,0:T(8,128)(2,1)S(1)} %get-tuple-element.37.vector, bf16[8,512,512]{2,1,0:T(8,128)(2,1)S(1)} %get-tuple-element.26.lefts.left, ...), custom_call_target="tpu_custom_call", output_to_operand_aliasing={{}: (5, {})} | custom-call | flops 2147483648 | bytes 4194304 | tf_op jit(solution)/shard_map/late/pallas_call | solution.py:241
  91.4 0.5 collective-permute-done.4.arrived
  92.0 0.4 pack.3
  92.4 2.4 %collective-permute-start.5 = (bf16[16,2,16,512]{3,2,1,0:T(8,128)(2,1)S(1)}, bf16[16,2,16,512]{3,2,1,0:T(8,128)(2,1)S(1)}, u32[]{:S(2)}, u32[]{:S(2)}) collective-permute-start(bf16[16,2,16,512]{3,2,1,0:T(8,128)(2,1)S(1)} %get-tuple-element.41), channel_id=1, source_target_pairs={{0,32},{1,9},{2,34},{3,11},{4,36},{5,13},{6,38},{7,15},{8,40},{9,1... | collective-permute-start | bytes 1572872 | tf_op jit(solution)/shard_map/ppermute | solution.py:269
  94.8 2.3 %collective-permute-start.6 = (bf16[16,2,16,512]{3,2,1,0:T(8,128)(2,1)S(1)}, bf16[16,2,16,512]{3,2,1,0:T(8,128)(2,1)S(1)}, u32[]{:S(2)}, u32[]{:S(2)}) collective-permute-start(bf16[16,2,16,512]{3,2,1,0:T(8,128)(2,1)S(1)} %get-tuple-element.42), channel_id=1, source_target_pairs={{0,16},{1,5},{2,18},{3,7},{4,20},{5,9},{6,22},{7,11},{8,24},{9,13}... | collective-permute-start | bytes 1572872 | tf_op jit(solution)/shard_map/ppermute | solution.py:269
  97.1 0.9 collective-permute-start.7
  98.0 5.3 %collective-permute-done.5.first = bf16[16,2,16,512]{3,2,1,0:T(8,128)(2,1)S(1)} collective-permute-done((bf16[16,2,16,512]{3,2,1,0:T(8,128)(2,1)S(1)}, bf16[16,2,16,512]{3,2,1,0:T(8,128)(2,1)S(1)}, u32[]{:S(2)}, u32[]{:S(2)}) %collective-permute-start.5) | collective-permute-done | bytes 524320 | tf_op jit(solution)/shard_map/ppermute | solution.py:269
  103.3 5.5 %collective-permute-done.6.second = bf16[16,2,16,512]{3,2,1,0:T(8,128)(2,1)S(1)} collective-permute-done((bf16[16,2,16,512]{3,2,1,0:T(8,128)(2,1)S(1)}, bf16[16,2,16,512]{3,2,1,0:T(8,128)(2,1)S(1)}, u32[]{:S(2)}, u32[]{:S(2)}) %collective-permute-start.6) | collective-permute-done | bytes 524320 | tf_op jit(solution)/shard_map/ppermute | solution.py:269
  108.8 1.1 collective-permute-done.7.third
  109.9 0.2 meet.3
  110.1 13.6 %all_to_all.23.pieces = bf16[16,2,16,512]{3,2,1,0:T(8,128)(2,1)S(1)} all-to-all(bf16[16,2,16,512]{3,2,1,0:T(8,128)(2,1)S(1)} %meet.3), channel_id=1, replica_groups={{8,70,68,74,72,6,12,0,2,78,76,10,4,64,66,14},{24,86,84,90,88,22,28,16,1..., dimensions={0} | all-to-all | bytes 1048576 | tf_op jit(solution)/shard_map/all_to_all | solution.py:45
  123.7 0.7 last.1
Async XLA Ops:
  0.6 0.7 copy-start.2
  1.3 5.7 %copy-start = (bf16[2,512,512]{2,1,0:T(8,128)(2,1)S(1)}, bf16[2,512,512]{2,1,0:T(8,128)(2,1)}, u32[]{:S(2)}) copy-start(bf16[2,512,512]{2,1,0:T(8,128)(2,1)} %wave.3) | copy-start | bytes 3145732
  6.9 4.2 %collective-permute-start = (bf16[4,512,512]{2,1,0:T(8,128)(2,1)S(1)}, bf16[4,512,512]{2,1,0:T(8,128)(2,1)S(1)}, u32[]{:S(2)}, u32[]{:S(2)}) collective-permute-start(bf16[4,512,512]{2,1,0:T(8,128)(2,1)S(1)} %get-tuple-element.29), channel_id=1, source_target_pairs={{0,1},{1,0},{2,3},{3,2},{4,5},{5,4},{6,7},{7,6},{8,9},{9,8},{10,11... | collective-permute-start | bytes 6291464 | tf_op jit(solution)/shard_map/ppermute | solution.py:410
  10.7 36.3 %copy-start.1 = (f32[2,16,512]{2,1,0:T(8,128)S(1)}, f32[2,16,512]{2,1,0:T(8,128)}, u32[]{:S(2)}) copy-start(f32[2,16,512]{2,1,0:T(8,128)} %precond.3) | copy-start | bytes 196612
  11.6 11.1 %collective-permute-start.1 = (bf16[16,2,16,512]{3,2,1,0:T(8,128)(2,1)S(1)}, bf16[16,2,16,512]{3,2,1,0:T(8,128)(2,1)S(1)}, u32[]{:S(2)}, u32[]{:S(2)}) collective-permute-start(bf16[16,2,16,512]{3,2,1,0:T(8,128)(2,1)S(1)} %get-tuple-element.31), channel_id=1, source_target_pairs={{0,32},{1,9},{2,34},{3,11},{4,36},{5,13},{6,38},{7,15},{8,40},{9,1... | collective-permute-start | bytes 1572872 | tf_op jit(solution)/shard_map/ppermute | solution.py:269
  15.5 12.8 %collective-permute-start.2 = (bf16[16,2,16,512]{3,2,1,0:T(8,128)(2,1)S(1)}, bf16[16,2,16,512]{3,2,1,0:T(8,128)(2,1)S(1)}, u32[]{:S(2)}, u32[]{:S(2)}) collective-permute-start(bf16[16,2,16,512]{3,2,1,0:T(8,128)(2,1)S(1)} %get-tuple-element.32), channel_id=1, source_target_pairs={{0,16},{1,5},{2,18},{3,7},{4,20},{5,9},{6,22},{7,11},{8,24},{9,13}... | collective-permute-start | bytes 1572872 | tf_op jit(solution)/shard_map/ppermute | solution.py:269
  16.8 12.8 %collective-permute-start.3 = (bf16[16,2,16,512]{3,2,1,0:T(8,128)(2,1)S(1)}, bf16[16,2,16,512]{3,2,1,0:T(8,128)(2,1)S(1)}, u32[]{:S(2)}, u32[]{:S(2)}) collective-permute-start(bf16[16,2,16,512]{3,2,1,0:T(8,128)(2,1)S(1)} %get-tuple-element.33), channel_id=1, source_target_pairs={{0,48},{1,13},{2,50},{3,15},{4,52},{5,1},{6,54},{7,3},{8,56},{9,5}... | collective-permute-start | bytes 1572872 | tf_op jit(solution)/shard_map/ppermute | solution.py:269
  87.5 4.4 %collective-permute-start.4 = (bf16[4,512,512]{2,1,0:T(8,128)(2,1)S(1)}, bf16[4,512,512]{2,1,0:T(8,128)(2,1)S(1)}, u32[]{:S(2)}, u32[]{:S(2)}) collective-permute-start(bf16[4,512,512]{2,1,0:T(8,128)(2,1)S(1)} %get-tuple-element.39), channel_id=1, source_target_pairs={{0,1},{1,0},{2,3},{3,2},{4,5},{5,4},{6,7},{7,6},{8,9},{9,8},{10,11... | collective-permute-start | bytes 6291464 | tf_op jit(solution)/shard_map/ppermute | solution.py:410
  92.4 10.9 %collective-permute-start.5 = (bf16[16,2,16,512]{3,2,1,0:T(8,128)(2,1)S(1)}, bf16[16,2,16,512]{3,2,1,0:T(8,128)(2,1)S(1)}, u32[]{:S(2)}, u32[]{:S(2)}) collective-permute-start(bf16[16,2,16,512]{3,2,1,0:T(8,128)(2,1)S(1)} %get-tuple-element.41), channel_id=1, source_target_pairs={{0,32},{1,9},{2,34},{3,11},{4,36},{5,13},{6,38},{7,15},{8,40},{9,1... | collective-permute-start | bytes 1572872 | tf_op jit(solution)/shard_map/ppermute | solution.py:269
  94.8 14.0 %collective-permute-start.6 = (bf16[16,2,16,512]{3,2,1,0:T(8,128)(2,1)S(1)}, bf16[16,2,16,512]{3,2,1,0:T(8,128)(2,1)S(1)}, u32[]{:S(2)}, u32[]{:S(2)}) collective-permute-start(bf16[16,2,16,512]{3,2,1,0:T(8,128)(2,1)S(1)} %get-tuple-element.42), channel_id=1, source_target_pairs={{0,16},{1,5},{2,18},{3,7},{4,20},{5,9},{6,22},{7,11},{8,24},{9,13}... | collective-permute-start | bytes 1572872 | tf_op jit(solution)/shard_map/ppermute | solution.py:269
  97.1 12.8 %collective-permute-start.7 = (bf16[16,2,16,512]{3,2,1,0:T(8,128)(2,1)S(1)}, bf16[16,2,16,512]{3,2,1,0:T(8,128)(2,1)S(1)}, u32[]{:S(2)}, u32[]{:S(2)}) collective-permute-start(bf16[16,2,16,512]{3,2,1,0:T(8,128)(2,1)S(1)} %get-tuple-element.43), channel_id=1, source_target_pairs={{0,48},{1,13},{2,50},{3,15},{4,52},{5,1},{6,54},{7,3},{8,56},{9,5}... | collective-permute-start | bytes 1572872 | tf_op jit(solution)/shard_map/ppermute | solution.py:269

commit v9 on v8

--- a/solution.py
+++ b/solution.py
@@ -127,7 +127,13 @@
 
 def early_kernel(first, targets, core, vector, left, right, out, kept, *refs):
     if first:
-        lefts, rights, touched, order, totals, wave, sems, wave_sem = refs
+        lefts, rights, touched, order, totals, wave, known, sems, wave_sem, known_sem = refs
+        whole = pltpu.make_async_copy(vector, wave, wave_sem)
+        listing = pltpu.make_async_copy(targets, known, known_sem)
+        listing.start()
+        whole.start()
+        listing.wait()
+        targets = known
     else:
         lefts, rights = left, right
         wave, touched, order, totals = refs
@@ -157,9 +163,6 @@
     def source(sector):
         return wave[sector]
 
-    if first:
-        whole = pltpu.make_async_copy(vector, wave, wave_sem)
-        whole.start()
     count = listed(targets, 1 - core[0], order, jnp.int32(0))
     listed(targets, core[0], order, count)
     if first:
@@ -215,11 +218,14 @@
     if first:
         scratch += [
             pltpu.VMEM(vector.shape, BF16),
+            pltpu.SMEM(targets.shape, jnp.int32),
             pltpu.SemaphoreType.DMA((2, tasks)),
             pltpu.SemaphoreType.DMA,
+            pltpu.SemaphoreType.DMA,
         ]
-        vector, left, right = (
-            pltpu.with_memory_space_constraint(value, pltpu.HBM) for value in (vector, left, right)
+        targets, vector, left, right = (
+            pltpu.with_memory_space_constraint(value, pltpu.HBM)
+            for value in (targets, vector, left, right)
         )
         out += [jax.ShapeDtypeStruct(left.shape, BF16)] * 2
     else:
@@ -227,7 +233,7 @@
     return pl.pallas_call(
         functools.partial(early_kernel, first),
         out_shape=out,
-        in_specs=[SMEM, SMEM] + [HBM if first else VMEM] * 3,
+        in_specs=[HBM, SMEM, HBM, HBM, HBM] if first else [SMEM, SMEM, VMEM, VMEM, VMEM],
         out_specs=[VMEM] * len(out),
         scratch_shapes=scratch,
         compiler_params=room(8),
@@ -376,7 +382,7 @@
     projected = w_r - shift * w_b
     correction_sq = r_r - 2.0 * shift * r_b + shift * shift * b_b
     along = projected / norm_sq
-    update_sq = correction_sq - projected * along
+    update_sq = jnp.maximum(correction_sq - projected * along, 0.0)
     scale = jnp.sqrt(norm_sq) * lax.rsqrt(update_sq + 1e-06)
     correction = (sigma[...] - shift[None] * own) / precond[...]
     new = ((correction - along[None] * own) * scale[None]).astype(BF16)

time: 125 us -> 124 us (level)
  blocking collectives: 65.9 us -> 67.4 us
  waiting for transfers between devices: 23.9 us -> 22.5 us
    ppermute x6, waiting for transfers between devices: 22.8 us -> 21.4 us  [along_ring(): return lax.ppermute(value, EVERY, pairs)]
    all_to_all x4, blocking collectives: 65.9 us -> 67.4 us  [exchange(): lax.all_to_all(pieces, EVERY, split_axis=0, concat_axis=0, axis_index_gro...]
where the time goes in v9:
time: 124 us; the launch traced here: 123 us
  blocking collectives  67.4 us (54%)
  waiting for transfers between devices  22.5 us (18%)
  Pallas kernels  20.2 us (16%)
  starting transfers between devices  12.2 us (10%)
    all_to_all x4, blocking collectives, exchange(): lax.all_to_all(pieces, EVERY, split_axis=0, concat_axis=0, axis_index_gro...  67.4 us
    ppermute x6, waiting for transfers between devices, along_ring(): return lax.ppermute(value, EVERY, pairs)  21.4 us
    ppermute x6, starting transfers between devices, along_ring(): return lax.ppermute(value, EVERY, pairs)  11.8 us
    pallas_call x2, Pallas kernels, apply_early(): pl.pallas_call(functools.partial(early_kernel, first), out_shape=out, in_...  9.69 us
    pallas_call x2, Pallas kernels, apply_late(): pl.pallas_call(late_kernel, out_shape=jax.ShapeDtypeStruct(begun.shape, F...  7.14 us
  transfers between devices with their start and end apart: 8, of which 8 were waited for; matrix products, arithmetic and copies ran while one was open for 0% of the time, Pallas kernels for 6%

profile of v9, /device:TPU:0, one launch (start us, length us, event | category | flops | bytes accessed | tf_op | source)
XLA Modules:
  0.0 123.0 jit_solution(15180318739935491160)
XLA Ops:
  0.6 0.0 copy-start
  0.7 0.0 copy-start.2
  0.7 5.9 %early_first.1 = (bf16[4,512,512]{2,1,0:T(8,128)(2,1)S(1)}, f32[4,512,512]{2,1,0:T(8,128)S(1)}, bf16[8,512,512]{2,1,0:T(8,128)(2,1)S(1)}, bf16[8,512,512]{2,1,0:T(8,128)(2,1)S(1)}) custom-call(s32[2,4]{1,0:T(2,128)} %bitcast.7, s32[1]{0:T(128)} %bitcast.1.core, bf16[2,512,512]{2,1,0:T(8,128)(2,1)} %wave.3, bf16[8,512,512]{2,1,0:T(8,128)(2,1)} %bitcast.11, ...), custom_call_target="tpu_custom_call" | custom-call | flops 2147483648 | bytes 4194304 | tf_op jit(solution)/shard_map/early_first/pallas_call | solution.py:233
  6.5 0.1 collective-permute-start
  6.6 0.0 copy-done
  6.6 0.0 copy-done.2
  6.7 3.6 %late.2.kept = f32[4,512,512]{2,1,0:T(8,128)S(1)} custom-call(s32[2,4]{1,0:T(2,128)S(1)} %bitcast.8, s32[1]{0:T(128)} %bitcast.1.core, bf16[2,512,512]{2,1,0:T(8,128)(2,1)S(1)} %copy-done, bf16[8,512,512]{2,1,0:T(8,128)(2,1)S(1)} %get-tuple-element.26.lefts.left, ...), custom_call_target="tpu_custom_call", output_to_operand_aliasing={{}: (5, {})} | custom-call | flops 2147483648 | bytes 4194304 | tf_op jit(solution)/shard_map/late/pallas_call | solution.py:247
  10.2 0.0 copy-start.1
  10.2 0.5 collective-permute-done.arrived
  10.8 0.4 pack.2
  11.2 3.2 %collective-permute-start.1 = (bf16[16,2,16,512]{3,2,1,0:T(8,128)(2,1)S(1)}, bf16[16,2,16,512]{3,2,1,0:T(8,128)(2,1)S(1)}, u32[]{:S(2)}, u32[]{:S(2)}) collective-permute-start(bf16[16,2,16,512]{3,2,1,0:T(8,128)(2,1)S(1)} %get-tuple-element.31), channel_id=1, source_target_pairs={{0,32},{1,9},{2,34},{3,11},{4,36},{5,13},{6,38},{7,15},{8,40},{9,1... | collective-permute-start | bytes 1572872 | tf_op jit(solution)/shard_map/ppermute | solution.py:275
  14.5 0.7 collective-permute-start.2
  15.1 2.6 %collective-permute-start.3 = (bf16[16,2,16,512]{3,2,1,0:T(8,128)(2,1)S(1)}, bf16[16,2,16,512]{3,2,1,0:T(8,128)(2,1)S(1)}, u32[]{:S(2)}, u32[]{:S(2)}) collective-permute-start(bf16[16,2,16,512]{3,2,1,0:T(8,128)(2,1)S(1)} %get-tuple-element.33), channel_id=1, source_target_pairs={{0,48},{1,13},{2,50},{3,15},{4,52},{5,1},{6,54},{7,3},{8,56},{9,5}... | collective-permute-start | bytes 1572872 | tf_op jit(solution)/shard_map/ppermute | solution.py:275
  17.7 4.4 %collective-permute-done.1.first = bf16[16,2,16,512]{3,2,1,0:T(8,128)(2,1)S(1)} collective-permute-done((bf16[16,2,16,512]{3,2,1,0:T(8,128)(2,1)S(1)}, bf16[16,2,16,512]{3,2,1,0:T(8,128)(2,1)S(1)}, u32[]{:S(2)}, u32[]{:S(2)}) %collective-permute-start.1) | collective-permute-done | bytes 524320 | tf_op jit(solution)/shard_map/ppermute | solution.py:275
  22.1 5.5 %collective-permute-done.2.second = bf16[16,2,16,512]{3,2,1,0:T(8,128)(2,1)S(1)} collective-permute-done((bf16[16,2,16,512]{3,2,1,0:T(8,128)(2,1)S(1)}, bf16[16,2,16,512]{3,2,1,0:T(8,128)(2,1)S(1)}, u32[]{:S(2)}, u32[]{:S(2)}) %collective-permute-start.2) | collective-permute-done | bytes 524320 | tf_op jit(solution)/shard_map/ppermute | solution.py:275
  27.6 0.3 collective-permute-done.3.third
  27.9 0.2 meet.2
  28.2 17.4 %all_to_all.20.pieces = bf16[16,2,16,512]{3,2,1,0:T(8,128)(2,1)S(1)} all-to-all(bf16[16,2,16,512]{3,2,1,0:T(8,128)(2,1)S(1)} %meet.2), channel_id=1, replica_groups={{8,70,68,74,72,6,12,0,2,78,76,10,4,64,66,14},{24,86,84,90,88,22,28,16,1..., dimensions={0} | all-to-all | bytes 1048576 | tf_op jit(solution)/shard_map/all_to_all | solution.py:45
  45.6 0.0 copy-done.1
  45.6 0.7 first.1
  46.3 15.3 %all_to_all.21.sums = f32[128,1,128]{2,1,0:T(1,128)S(1)} all-to-all(f32[128,1,128]{2,1,0:T(1,128)S(1)} %get-tuple-element.35), channel_id=1, replica_groups={{48,43,108,72,29,14,54,23,124,94,10,44,3,49,83,111,16,95,107,101,110,22..., dimensions={0} | all-to-all | bytes 131072 | tf_op jit(solution)/shard_map/all_to_all | solution.py:45
  61.6 0.6 second.1
  62.2 20.2 %all_to_all.22.vector = bf16[32,2,16,512]{3,2,1,0:T(8,128)(2,1)S(1)} all-to-all(bf16[32,2,16,512]{3,2,1,0:T(8,128)(2,1)S(1)} %second.1), channel_id=1, replica_groups={{20,92,76,32,96,72,40,120,52,100,84,12,36,104,80,68,60,124,0,116,108,64..., dimensions={0} | all-to-all | bytes 2097152 | tf_op jit(solution)/shard_map/all_to_all | solution.py:45
  82.4 3.8 %early.1 = (bf16[4,512,512]{2,1,0:T(8,128)(2,1)S(1)}, f32[4,512,512]{2,1,0:T(8,128)S(1)}, bf16[2,512,512]{2,1,0:T(8,128)(2,1)S(1)}) custom-call(s32[2,4]{1,0:T(2,128)S(1)} %bitcast.9, s32[1]{0:T(128)} %bitcast.1.core, bf16[32,2,16,512]{3,2,1,0:T(8,128)(2,1)S(1)} %all_to_all.22.vector, bf16[8,512,512]{2,1,0:T(8,128)(2,1)S(1)} %get-tuple-element.26.lefts.left, ...), custom_call_target="tpu_custom_call" | custom-call | flops 2147483648 | bytes 4194304 | tf_op jit(solution)/shard_map/early/pallas_call | solution.py:233
  86.3 0.3 collective-permute-start.4
  86.5 3.6 %late.3.kept = f32[4,512,512]{2,1,0:T(8,128)S(1)} custom-call(s32[2,4]{1,0:T(2,128)S(1)} %bitcast.10, s32[1]{0:T(128)} %bitcast.1.core, bf16[2,512,512]{2,1,0:T(8,128)(2,1)S(1)} %get-tuple-element.37.vector, bf16[8,512,512]{2,1,0:T(8,128)(2,1)S(1)} %get-tuple-element.26.lefts.left, ...), custom_call_target="tpu_custom_call", output_to_operand_aliasing={{}: (5, {})} | custom-call | flops 2147483648 | bytes 4194304 | tf_op jit(solution)/shard_map/late/pallas_call | solution.py:247
  90.1 0.6 collective-permute-done.4.arrived
  90.7 0.4 pack.3
  91.1 2.1 %collective-permute-start.5 = (bf16[16,2,16,512]{3,2,1,0:T(8,128)(2,1)S(1)}, bf16[16,2,16,512]{3,2,1,0:T(8,128)(2,1)S(1)}, u32[]{:S(2)}, u32[]{:S(2)}) collective-permute-start(bf16[16,2,16,512]{3,2,1,0:T(8,128)(2,1)S(1)} %get-tuple-element.41), channel_id=1, source_target_pairs={{0,32},{1,9},{2,34},{3,11},{4,36},{5,13},{6,38},{7,15},{8,40},{9,1... | collective-permute-start | bytes 1572872 | tf_op jit(solution)/shard_map/ppermute | solution.py:275
  93.2 1.6 %collective-permute-start.6 = (bf16[16,2,16,512]{3,2,1,0:T(8,128)(2,1)S(1)}, bf16[16,2,16,512]{3,2,1,0:T(8,128)(2,1)S(1)}, u32[]{:S(2)}, u32[]{:S(2)}) collective-permute-start(bf16[16,2,16,512]{3,2,1,0:T(8,128)(2,1)S(1)} %get-tuple-element.42), channel_id=1, source_target_pairs={{0,16},{1,5},{2,18},{3,7},{4,20},{5,9},{6,22},{7,11},{8,24},{9,13}... | collective-permute-start | bytes 1572872 | tf_op jit(solution)/shard_map/ppermute | solution.py:275
  94.8 1.7 %collective-permute-start.7 = (bf16[16,2,16,512]{3,2,1,0:T(8,128)(2,1)S(1)}, bf16[16,2,16,512]{3,2,1,0:T(8,128)(2,1)S(1)}, u32[]{:S(2)}, u32[]{:S(2)}) collective-permute-start(bf16[16,2,16,512]{3,2,1,0:T(8,128)(2,1)S(1)} %get-tuple-element.43), channel_id=1, source_target_pairs={{0,48},{1,13},{2,50},{3,15},{4,52},{5,1},{6,54},{7,3},{8,56},{9,5}... | collective-permute-start | bytes 1572872 | tf_op jit(solution)/shard_map/ppermute | solution.py:275
  96.5 5.5 %collective-permute-done.5.first = bf16[16,2,16,512]{3,2,1,0:T(8,128)(2,1)S(1)} collective-permute-done((bf16[16,2,16,512]{3,2,1,0:T(8,128)(2,1)S(1)}, bf16[16,2,16,512]{3,2,1,0:T(8,128)(2,1)S(1)}, u32[]{:S(2)}, u32[]{:S(2)}) %collective-permute-start.5) | collective-permute-done | bytes 524320 | tf_op jit(solution)/shard_map/ppermute | solution.py:275
  102.0 5.5 %collective-permute-done.6.second = bf16[16,2,16,512]{3,2,1,0:T(8,128)(2,1)S(1)} collective-permute-done((bf16[16,2,16,512]{3,2,1,0:T(8,128)(2,1)S(1)}, bf16[16,2,16,512]{3,2,1,0:T(8,128)(2,1)S(1)}, u32[]{:S(2)}, u32[]{:S(2)}) %collective-permute-start.6) | collective-permute-done | bytes 524320 | tf_op jit(solution)/shard_map/ppermute | solution.py:275
  107.5 0.1 collective-permute-done.7.third
  107.6 0.2 meet.3
  107.8 14.5 %all_to_all.23.pieces = bf16[16,2,16,512]{3,2,1,0:T(8,128)(2,1)S(1)} all-to-all(bf16[16,2,16,512]{3,2,1,0:T(8,128)(2,1)S(1)} %meet.3), channel_id=1, replica_groups={{8,70,68,74,72,6,12,0,2,78,76,10,4,64,66,14},{24,86,84,90,88,22,28,16,1..., dimensions={0} | all-to-all | bytes 1048576 | tf_op jit(solution)/shard_map/all_to_all | solution.py:45
  122.3 0.7 last.1
Async XLA Ops:
  0.6 6.0 %copy-start = (bf16[2,512,512]{2,1,0:T(8,128)(2,1)S(1)}, bf16[2,512,512]{2,1,0:T(8,128)(2,1)}, u32[]{:S(2)}) copy-start(bf16[2,512,512]{2,1,0:T(8,128)(2,1)} %wave.3) | copy-start | bytes 3145732
  0.7 6.0 %copy-start.2 = (s32[4,2]{0,1:T(2,128)S(1)}, s32[4,2]{0,1:T(2,128)}, u32[]{:S(2)}) copy-start(s32[4,2]{0,1:T(2,128)} %param.8) | copy-start | bytes 100
  6.5 4.2 %collective-permute-start = (bf16[4,512,512]{2,1,0:T(8,128)(2,1)S(1)}, bf16[4,512,512]{2,1,0:T(8,128)(2,1)S(1)}, u32[]{:S(2)}, u32[]{:S(2)}) collective-permute-start(bf16[4,512,512]{2,1,0:T(8,128)(2,1)S(1)} %get-tuple-element.29), channel_id=1, source_target_pairs={{0,1},{1,0},{2,3},{3,2},{4,5},{5,4},{6,7},{7,6},{8,9},{9,8},{10,11... | collective-permute-start | bytes 6291464 | tf_op jit(solution)/shard_map/ppermute | solution.py:416
  10.2 35.4 %copy-start.1 = (f32[2,16,512]{2,1,0:T(8,128)S(1)}, f32[2,16,512]{2,1,0:T(8,128)}, u32[]{:S(2)}) copy-start(f32[2,16,512]{2,1,0:T(8,128)} %precond.3) | copy-start | bytes 196612
  11.2 10.9 %collective-permute-start.1 = (bf16[16,2,16,512]{3,2,1,0:T(8,128)(2,1)S(1)}, bf16[16,2,16,512]{3,2,1,0:T(8,128)(2,1)S(1)}, u32[]{:S(2)}, u32[]{:S(2)}) collective-permute-start(bf16[16,2,16,512]{3,2,1,0:T(8,128)(2,1)S(1)} %get-tuple-element.31), channel_id=1, source_target_pairs={{0,32},{1,9},{2,34},{3,11},{4,36},{5,13},{6,38},{7,15},{8,40},{9,1... | collective-permute-start | bytes 1572872 | tf_op jit(solution)/shard_map/ppermute | solution.py:275
  14.5 13.1 %collective-permute-start.2 = (bf16[16,2,16,512]{3,2,1,0:T(8,128)(2,1)S(1)}, bf16[16,2,16,512]{3,2,1,0:T(8,128)(2,1)S(1)}, u32[]{:S(2)}, u32[]{:S(2)}) collective-permute-start(bf16[16,2,16,512]{3,2,1,0:T(8,128)(2,1)S(1)} %get-tuple-element.32), channel_id=1, source_target_pairs={{0,16},{1,5},{2,18},{3,7},{4,20},{5,9},{6,22},{7,11},{8,24},{9,13}... | collective-permute-start | bytes 1572872 | tf_op jit(solution)/shard_map/ppermute | solution.py:275
  15.1 12.8 %collective-permute-start.3 = (bf16[16,2,16,512]{3,2,1,0:T(8,128)(2,1)S(1)}, bf16[16,2,16,512]{3,2,1,0:T(8,128)(2,1)S(1)}, u32[]{:S(2)}, u32[]{:S(2)}) collective-permute-start(bf16[16,2,16,512]{3,2,1,0:T(8,128)(2,1)S(1)} %get-tuple-element.33), channel_id=1, source_target_pairs={{0,48},{1,13},{2,50},{3,15},{4,52},{5,1},{6,54},{7,3},{8,56},{9,5}... | collective-permute-start | bytes 1572872 | tf_op jit(solution)/shard_map/ppermute | solution.py:275
  86.3 4.4 %collective-permute-start.4 = (bf16[4,512,512]{2,1,0:T(8,128)(2,1)S(1)}, bf16[4,512,512]{2,1,0:T(8,128)(2,1)S(1)}, u32[]{:S(2)}, u32[]{:S(2)}) collective-permute-start(bf16[4,512,512]{2,1,0:T(8,128)(2,1)S(1)} %get-tuple-element.39), channel_id=1, source_target_pairs={{0,1},{1,0},{2,3},{3,2},{4,5},{5,4},{6,7},{7,6},{8,9},{9,8},{10,11... | collective-permute-start | bytes 6291464 | tf_op jit(solution)/shard_map/ppermute | solution.py:416
  91.1 10.9 %collective-permute-start.5 = (bf16[16,2,16,512]{3,2,1,0:T(8,128)(2,1)S(1)}, bf16[16,2,16,512]{3,2,1,0:T(8,128)(2,1)S(1)}, u32[]{:S(2)}, u32[]{:S(2)}) collective-permute-start(bf16[16,2,16,512]{3,2,1,0:T(8,128)(2,1)S(1)} %get-tuple-element.41), channel_id=1, source_target_pairs={{0,32},{1,9},{2,34},{3,11},{4,36},{5,13},{6,38},{7,15},{8,40},{9,1... | collective-permute-start | bytes 1572872 | tf_op jit(solution)/shard_map/ppermute | solution.py:275
  93.2 14.3 %collective-permute-start.6 = (bf16[16,2,16,512]{3,2,1,0:T(8,128)(2,1)S(1)}, bf16[16,2,16,512]{3,2,1,0:T(8,128)(2,1)S(1)}, u32[]{:S(2)}, u32[]{:S(2)}) collective-permute-start(bf16[16,2,16,512]{3,2,1,0:T(8,128)(2,1)S(1)} %get-tuple-element.42), channel_id=1, source_target_pairs={{0,16},{1,5},{2,18},{3,7},{4,20},{5,9},{6,22},{7,11},{8,24},{9,13}... | collective-permute-start | bytes 1572872 | tf_op jit(solution)/shard_map/ppermute | solution.py:275
  94.8 12.8 %collective-permute-start.7 = (bf16[16,2,16,512]{3,2,1,0:T(8,128)(2,1)S(1)}, bf16[16,2,16,512]{3,2,1,0:T(8,128)(2,1)S(1)}, u32[]{:S(2)}, u32[]{:S(2)}) collective-permute-start(bf16[16,2,16,512]{3,2,1,0:T(8,128)(2,1)S(1)} %get-tuple-element.43), channel_id=1, source_target_pairs={{0,48},{1,13},{2,50},{3,15},{4,52},{5,1},{6,54},{7,3},{8,56},{9,5}... | collective-permute-start | bytes 1572872 | tf_op jit(solution)/shard_map/ppermute | solution.py:275

commit v10 on v9

--- a/solution.py
+++ b/solution.py
@@ -35,9 +35,8 @@
     return members
 
 
-OP_ORDER = mixed(itertools.product(range(2), range(4), range(4)), 8)
+OP_ORDER = list(itertools.product(range(2), range(4), range(4)))
 REST_ORDER = mixed(itertools.product(range(2), range(4), range(2)), 3)
-OP_AT = [(low * 4 + first) * 4 + second for low, first, second in OP_ORDER]
 REST_AT = [(low * 4 + at) * 2 + half for low, at, half in REST_ORDER]
 
 
@@ -48,7 +47,7 @@
 
 
 def with_everyone(pieces):
-    return exchange(pieces, [mixed(range(lax.axis_size(EVERY)), 0)])
+    return exchange(pieces, [list(range(lax.axis_size(EVERY)))])
 
 
 def over_terms(pieces):
@@ -136,10 +135,7 @@
         targets = known
     else:
         lefts, rights = left, right
-        wave, touched, order, totals = refs
-        rows = vector.shape[2]
-        for index, owner in enumerate(OP_AT):
-            wave[:, owner * rows : (owner + 1) * rows, :] = vector[index]
+        touched, order, totals = refs
     tasks = lefts.shape[0]
 
     def copy(side, task):
@@ -161,7 +157,7 @@
         return carry
 
     def source(sector):
-        return wave[sector]
+        return wave[sector] if first else vector[:, sector].reshape(lefts.shape[1:])
 
     count = listed(targets, 1 - core[0], order, jnp.int32(0))
     listed(targets, core[0], order, count)
@@ -195,7 +191,8 @@
         return carry
 
     def source(sector):
-        return vector[sector]
+        whole = vector[sector] if vector.shape[1:] == lefts.shape[1:] else vector[:, sector]
+        return whole.reshape(lefts.shape[1:])
 
     def arrive(side, task):
         del side, task
@@ -228,8 +225,6 @@
             for value in (targets, vector, left, right)
         )
         out += [jax.ShapeDtypeStruct(left.shape, BF16)] * 2
-    else:
-        out += [jax.ShapeDtypeStruct((vector.shape[1], width, width), BF16)]
     return pl.pallas_call(
         functools.partial(early_kernel, first),
         out_shape=out,
@@ -408,11 +403,8 @@
     offset, mine, ring = lax.optimization_barrier((offset, mine, ring))
 
     def partial_pieces(vector, left, right, first):
-        sent, begun, *rest = apply_early(targets, mine, vector, left, right, first)
-        if first:
-            left, right = rest
-        else:
-            (vector,) = rest
+        sent, begun, *blocks = apply_early(targets, mine, vector, left, right, first)
+        left, right = blocks if first else (left, right)
         arrived = lax.ppermute(sent, CORE, [(0, 1), (1, 0)])
         kept = apply_late(targets, mine, vector, left, right, begun)
         shape = (owners // 2, local_sectors, rows, width)

time: 124 us -> 124 us (level)
  transfers between devices with their start and end apart: 8 -> 8, of which waited for: 8 -> 7; matrix products, arithmetic and copies ran while one was open for 0% -> 0% of each run, Pallas kernels for 6% -> 6%
where the time goes in v10:
time: 124 us; the launch traced here: 123 us
  blocking collectives  67.3 us (54%)
  waiting for transfers between devices  22.5 us (18%)
  Pallas kernels  20.2 us (16%)
  starting transfers between devices  11.9 us (10%)
    all_to_all x4, blocking collectives, exchange(): lax.all_to_all(pieces, EVERY, split_axis=0, concat_axis=0, axis_index_gro...  67.3 us
    ppermute x6, waiting for transfers between devices, along_ring(): return lax.ppermute(value, EVERY, pairs)  21.4 us
    ppermute x6, starting transfers between devices, along_ring(): return lax.ppermute(value, EVERY, pairs)  11.6 us
    pallas_call x2, Pallas kernels, apply_early(): pl.pallas_call(functools.partial(early_kernel, first), out_shape=out, in_...  9.76 us
    pallas_call x2, Pallas kernels, apply_late(): pl.pallas_call(late_kernel, out_shape=jax.ShapeDtypeStruct(begun.shape, F...  7.1 us
  transfers between devices with their start and end apart: 8, of which 7 were waited for; matrix products, arithmetic and copies ran while one was open for 0% of the time, Pallas kernels for 6%

profile of v10, /device:TPU:0, one launch (start us, length us, event | category | flops | bytes accessed | tf_op | source)
XLA Modules:
  0.0 122.7 jit_solution(3516900967247453750)
XLA Ops:
  0.6 0.0 copy-start
  0.7 0.0 copy-start.2
  0.7 5.9 %early_first.1 = (bf16[4,512,512]{2,1,0:T(8,128)(2,1)S(1)}, f32[4,512,512]{2,1,0:T(8,128)S(1)}, bf16[8,512,512]{2,1,0:T(8,128)(2,1)S(1)}, bf16[8,512,512]{2,1,0:T(8,128)(2,1)S(1)}) custom-call(s32[2,4]{1,0:T(2,128)} %bitcast.7, s32[1]{0:T(128)} %bitcast.1.core, bf16[2,512,512]{2,1,0:T(8,128)(2,1)} %wave.3, bf16[8,512,512]{2,1,0:T(8,128)(2,1)} %bitcast.11, ...), custom_call_target="tpu_custom_call" | custom-call | flops 2147483648 | bytes 4194304 | tf_op jit(solution)/shard_map/early_first/pallas_call | solution.py:228
  6.6 0.1 collective-permute-start
  6.7 0.0 copy-done
  6.7 0.0 copy-done.2
  6.7 3.5 %late.2.kept = f32[4,512,512]{2,1,0:T(8,128)S(1)} custom-call(s32[2,4]{1,0:T(2,128)S(1)} %bitcast.8, s32[1]{0:T(128)} %bitcast.1.core, bf16[2,512,512]{2,1,0:T(8,128)(2,1)S(1)} %copy-done, bf16[8,512,512]{2,1,0:T(8,128)(2,1)S(1)} %get-tuple-element.25.lefts.left, ...), custom_call_target="tpu_custom_call", output_to_operand_aliasing={{}: (5, {})} | custom-call | flops 2147483648 | bytes 4194304 | tf_op jit(solution)/shard_map/late/pallas_call | solution.py:242
  10.3 0.0 copy-start.1
  10.3 0.6 collective-permute-done.arrived
  10.8 0.4 pack.2
  11.3 3.3 %collective-permute-start.1 = (bf16[16,2,16,512]{3,2,1,0:T(8,128)(2,1)S(1)}, bf16[16,2,16,512]{3,2,1,0:T(8,128)(2,1)S(1)}, u32[]{:S(2)}, u32[]{:S(2)}) collective-permute-start(bf16[16,2,16,512]{3,2,1,0:T(8,128)(2,1)S(1)} %get-tuple-element.30), channel_id=1, source_target_pairs={{0,32},{1,9},{2,34},{3,11},{4,36},{5,13},{6,38},{7,15},{8,40},{9,1... | collective-permute-start | bytes 1572872 | tf_op jit(solution)/shard_map/ppermute | solution.py:270
  14.6 0.4 collective-permute-start.2
  15.0 2.8 %collective-permute-start.3 = (bf16[16,2,16,512]{3,2,1,0:T(8,128)(2,1)S(1)}, bf16[16,2,16,512]{3,2,1,0:T(8,128)(2,1)S(1)}, u32[]{:S(2)}, u32[]{:S(2)}) collective-permute-start(bf16[16,2,16,512]{3,2,1,0:T(8,128)(2,1)S(1)} %get-tuple-element.32), channel_id=1, source_target_pairs={{0,48},{1,13},{2,50},{3,15},{4,52},{5,1},{6,54},{7,3},{8,56},{9,5}... | collective-permute-start | bytes 1572872 | tf_op jit(solution)/shard_map/ppermute | solution.py:270
  17.8 4.3 %collective-permute-done.1.first = bf16[16,2,16,512]{3,2,1,0:T(8,128)(2,1)S(1)} collective-permute-done((bf16[16,2,16,512]{3,2,1,0:T(8,128)(2,1)S(1)}, bf16[16,2,16,512]{3,2,1,0:T(8,128)(2,1)S(1)}, u32[]{:S(2)}, u32[]{:S(2)}) %collective-permute-start.1) | collective-permute-done | bytes 524320 | tf_op jit(solution)/shard_map/ppermute | solution.py:270
  22.1 5.5 %collective-permute-done.2.second = bf16[16,2,16,512]{3,2,1,0:T(8,128)(2,1)S(1)} collective-permute-done((bf16[16,2,16,512]{3,2,1,0:T(8,128)(2,1)S(1)}, bf16[16,2,16,512]{3,2,1,0:T(8,128)(2,1)S(1)}, u32[]{:S(2)}, u32[]{:S(2)}) %collective-permute-start.2) | collective-permute-done | bytes 524320 | tf_op jit(solution)/shard_map/ppermute | solution.py:270
  27.7 0.1 collective-permute-done.3.third
  27.8 0.2 meet.2
  28.0 18.0 %all_to_all.20.pieces = bf16[16,2,16,512]{3,2,1,0:T(8,128)(2,1)S(1)} all-to-all(bf16[16,2,16,512]{3,2,1,0:T(8,128)(2,1)S(1)} %meet.2), channel_id=1, replica_groups={{8,70,68,74,72,6,12,0,2,78,76,10,4,64,66,14},{24,86,84,90,88,22,28,16,1..., dimensions={0} | all-to-all | bytes 1048576 | tf_op jit(solution)/shard_map/all_to_all | solution.py:44
  46.0 0.0 copy-done.1
  46.0 0.7 first.1
  46.7 14.8 %all_to_all.21.sums = f32[128,1,128]{2,1,0:T(1,128)S(1)} all-to-all(f32[128,1,128]{2,1,0:T(1,128)S(1)} %get-tuple-element.34), channel_id=1, replica_groups={{0,1,2,3,4,5,6,7,8,9,10,11,12,13,14,15,16,17,18,19,20,21,22,23,24,25,26..., dimensions={0} | all-to-all | bytes 131072 | tf_op jit(solution)/shard_map/all_to_all | solution.py:44
  61.6 0.6 second.1
  62.2 20.6 %all_to_all.22.vector = bf16[32,2,16,512]{3,2,1,0:T(8,128)(2,1)S(1)} all-to-all(bf16[32,2,16,512]{3,2,1,0:T(8,128)(2,1)S(1)} %second.1), channel_id=1, replica_groups={{0,4,8,12,16,20,24,28,32,36,40,44,48,52,56,60,64,68,72,76,80,84,88,92,9..., dimensions={0} | all-to-all | bytes 2097152 | tf_op jit(solution)/shard_map/all_to_all | solution.py:44
  82.8 3.8 %early.1 = (bf16[4,512,512]{2,1,0:T(8,128)(2,1)S(1)}, f32[4,512,512]{2,1,0:T(8,128)S(1)}) custom-call(s32[2,4]{1,0:T(2,128)S(1)} %bitcast.9, s32[1]{0:T(128)} %bitcast.1.core, bf16[32,2,16,512]{3,2,1,0:T(8,128)(2,1)S(1)} %all_to_all.22.vector, bf16[8,512,512]{2,1,0:T(8,128)(2,1)S(1)} %get-tuple-element.25.lefts.left, ...), custom_call_target="tpu_custom_call" | custom-call | flops 2147483648 | bytes 4194304 | tf_op jit(solution)/shard_map/early/pallas_call | solution.py:228
  86.6 0.3 collective-permute-start.4
  86.9 3.5 %late.3.kept = f32[4,512,512]{2,1,0:T(8,128)S(1)} custom-call(s32[2,4]{1,0:T(2,128)S(1)} %bitcast.10, s32[1]{0:T(128)} %bitcast.1.core, bf16[32,2,16,512]{3,2,1,0:T(8,128)(2,1)S(1)} %all_to_all.22.vector, bf16[8,512,512]{2,1,0:T(8,128)(2,1)S(1)} %get-tuple-element.25.lefts.left, ...), custom_call_target="tpu_custom_call", output_to_operand_aliasing={{}: (5, {})} | custom-call | flops 2147483648 | bytes 4194304 | tf_op jit(solution)/shard_map/late/pallas_call | solution.py:242
  90.4 0.6 collective-permute-done.4.arrived
  91.0 0.4 pack.3
  91.5 1.8 %collective-permute-start.5 = (bf16[16,2,16,512]{3,2,1,0:T(8,128)(2,1)S(1)}, bf16[16,2,16,512]{3,2,1,0:T(8,128)(2,1)S(1)}, u32[]{:S(2)}, u32[]{:S(2)}) collective-permute-start(bf16[16,2,16,512]{3,2,1,0:T(8,128)(2,1)S(1)} %get-tuple-element.39), channel_id=1, source_target_pairs={{0,32},{1,9},{2,34},{3,11},{4,36},{5,13},{6,38},{7,15},{8,40},{9,1... | collective-permute-start | bytes 1572872 | tf_op jit(solution)/shard_map/ppermute | solution.py:270
  93.2 1.5 %collective-permute-start.6 = (bf16[16,2,16,512]{3,2,1,0:T(8,128)(2,1)S(1)}, bf16[16,2,16,512]{3,2,1,0:T(8,128)(2,1)S(1)}, u32[]{:S(2)}, u32[]{:S(2)}) collective-permute-start(bf16[16,2,16,512]{3,2,1,0:T(8,128)(2,1)S(1)} %get-tuple-element.40), channel_id=1, source_target_pairs={{0,16},{1,5},{2,18},{3,7},{4,20},{5,9},{6,22},{7,11},{8,24},{9,13}... | collective-permute-start | bytes 1572872 | tf_op jit(solution)/shard_map/ppermute | solution.py:270
  94.7 1.7 %collective-permute-start.7 = (bf16[16,2,16,512]{3,2,1,0:T(8,128)(2,1)S(1)}, bf16[16,2,16,512]{3,2,1,0:T(8,128)(2,1)S(1)}, u32[]{:S(2)}, u32[]{:S(2)}) collective-permute-start(bf16[16,2,16,512]{3,2,1,0:T(8,128)(2,1)S(1)} %get-tuple-element.41), channel_id=1, source_target_pairs={{0,48},{1,13},{2,50},{3,15},{4,52},{5,1},{6,54},{7,3},{8,56},{9,5}... | collective-permute-start | bytes 1572872 | tf_op jit(solution)/shard_map/ppermute | solution.py:270
  96.5 5.9 %collective-permute-done.5.first = bf16[16,2,16,512]{3,2,1,0:T(8,128)(2,1)S(1)} collective-permute-done((bf16[16,2,16,512]{3,2,1,0:T(8,128)(2,1)S(1)}, bf16[16,2,16,512]{3,2,1,0:T(8,128)(2,1)S(1)}, u32[]{:S(2)}, u32[]{:S(2)}) %collective-permute-start.5) | collective-permute-done | bytes 524320 | tf_op jit(solution)/shard_map/ppermute | solution.py:270
  102.3 5.5 %collective-permute-done.6.second = bf16[16,2,16,512]{3,2,1,0:T(8,128)(2,1)S(1)} collective-permute-done((bf16[16,2,16,512]{3,2,1,0:T(8,128)(2,1)S(1)}, bf16[16,2,16,512]{3,2,1,0:T(8,128)(2,1)S(1)}, u32[]{:S(2)}, u32[]{:S(2)}) %collective-permute-start.6) | collective-permute-done | bytes 524320 | tf_op jit(solution)/shard_map/ppermute | solution.py:270
  107.9 0.0 collective-permute-done.7.third
  107.9 0.2 meet.3
  108.1 13.9 %all_to_all.23.pieces = bf16[16,2,16,512]{3,2,1,0:T(8,128)(2,1)S(1)} all-to-all(bf16[16,2,16,512]{3,2,1,0:T(8,128)(2,1)S(1)} %meet.3), channel_id=1, replica_groups={{8,70,68,74,72,6,12,0,2,78,76,10,4,64,66,14},{24,86,84,90,88,22,28,16,1..., dimensions={0} | all-to-all | bytes 1048576 | tf_op jit(solution)/shard_map/all_to_all | solution.py:44
  122.0 0.7 last.1
Async XLA Ops:
  0.6 6.1 %copy-start = (bf16[2,512,512]{2,1,0:T(8,128)(2,1)S(1)}, bf16[2,512,512]{2,1,0:T(8,128)(2,1)}, u32[]{:S(2)}) copy-start(bf16[2,512,512]{2,1,0:T(8,128)(2,1)} %wave.3) | copy-start | bytes 3145732
  0.7 6.1 %copy-start.2 = (s32[4,2]{0,1:T(2,128)S(1)}, s32[4,2]{0,1:T(2,128)}, u32[]{:S(2)}) copy-start(s32[4,2]{0,1:T(2,128)} %param.8) | copy-start | bytes 100
  6.6 4.2 %collective-permute-start = (bf16[4,512,512]{2,1,0:T(8,128)(2,1)S(1)}, bf16[4,512,512]{2,1,0:T(8,128)(2,1)S(1)}, u32[]{:S(2)}, u32[]{:S(2)}) collective-permute-start(bf16[4,512,512]{2,1,0:T(8,128)(2,1)S(1)} %get-tuple-element.28), channel_id=1, source_target_pairs={{0,1},{1,0},{2,3},{3,2},{4,5},{5,4},{6,7},{7,6},{8,9},{9,8},{10,11... | collective-permute-start | bytes 6291464 | tf_op jit(solution)/shard_map/ppermute | solution.py:408
  10.3 35.7 %copy-start.1 = (f32[2,16,512]{2,1,0:T(8,128)S(1)}, f32[2,16,512]{2,1,0:T(8,128)}, u32[]{:S(2)}) copy-start(f32[2,16,512]{2,1,0:T(8,128)} %precond.3) | copy-start | bytes 196612
  11.3 10.9 %collective-permute-start.1 = (bf16[16,2,16,512]{3,2,1,0:T(8,128)(2,1)S(1)}, bf16[16,2,16,512]{3,2,1,0:T(8,128)(2,1)S(1)}, u32[]{:S(2)}, u32[]{:S(2)}) collective-permute-start(bf16[16,2,16,512]{3,2,1,0:T(8,128)(2,1)S(1)} %get-tuple-element.30), channel_id=1, source_target_pairs={{0,32},{1,9},{2,34},{3,11},{4,36},{5,13},{6,38},{7,15},{8,40},{9,1... | collective-permute-start | bytes 1572872 | tf_op jit(solution)/shard_map/ppermute | solution.py:270
  14.6 13.1 %collective-permute-start.2 = (bf16[16,2,16,512]{3,2,1,0:T(8,128)(2,1)S(1)}, bf16[16,2,16,512]{3,2,1,0:T(8,128)(2,1)S(1)}, u32[]{:S(2)}, u32[]{:S(2)}) collective-permute-start(bf16[16,2,16,512]{3,2,1,0:T(8,128)(2,1)S(1)} %get-tuple-element.31), channel_id=1, source_target_pairs={{0,16},{1,5},{2,18},{3,7},{4,20},{5,9},{6,22},{7,11},{8,24},{9,13}... | collective-permute-start | bytes 1572872 | tf_op jit(solution)/shard_map/ppermute | solution.py:270
  15.0 12.8 %collective-permute-start.3 = (bf16[16,2,16,512]{3,2,1,0:T(8,128)(2,1)S(1)}, bf16[16,2,16,512]{3,2,1,0:T(8,128)(2,1)S(1)}, u32[]{:S(2)}, u32[]{:S(2)}) collective-permute-start(bf16[16,2,16,512]{3,2,1,0:T(8,128)(2,1)S(1)} %get-tuple-element.32), channel_id=1, source_target_pairs={{0,48},{1,13},{2,50},{3,15},{4,52},{5,1},{6,54},{7,3},{8,56},{9,5}... | collective-permute-start | bytes 1572872 | tf_op jit(solution)/shard_map/ppermute | solution.py:270
  86.6 4.4 %collective-permute-start.4 = (bf16[4,512,512]{2,1,0:T(8,128)(2,1)S(1)}, bf16[4,512,512]{2,1,0:T(8,128)(2,1)S(1)}, u32[]{:S(2)}, u32[]{:S(2)}) collective-permute-start(bf16[4,512,512]{2,1,0:T(8,128)(2,1)S(1)} %get-tuple-element.37), channel_id=1, source_target_pairs={{0,1},{1,0},{2,3},{3,2},{4,5},{5,4},{6,7},{7,6},{8,9},{9,8},{10,11... | collective-permute-start | bytes 6291464 | tf_op jit(solution)/shard_map/ppermute | solution.py:408
  91.5 10.9 %collective-permute-start.5 = (bf16[16,2,16,512]{3,2,1,0:T(8,128)(2,1)S(1)}, bf16[16,2,16,512]{3,2,1,0:T(8,128)(2,1)S(1)}, u32[]{:S(2)}, u32[]{:S(2)}) collective-permute-start(bf16[16,2,16,512]{3,2,1,0:T(8,128)(2,1)S(1)} %get-tuple-element.39), channel_id=1, source_target_pairs={{0,32},{1,9},{2,34},{3,11},{4,36},{5,13},{6,38},{7,15},{8,40},{9,1... | collective-permute-start | bytes 1572872 | tf_op jit(solution)/shard_map/ppermute | solution.py:270
  93.2 14.6 %collective-permute-start.6 = (bf16[16,2,16,512]{3,2,1,0:T(8,128)(2,1)S(1)}, bf16[16,2,16,512]{3,2,1,0:T(8,128)(2,1)S(1)}, u32[]{:S(2)}, u32[]{:S(2)}) collective-permute-start(bf16[16,2,16,512]{3,2,1,0:T(8,128)(2,1)S(1)} %get-tuple-element.40), channel_id=1, source_target_pairs={{0,16},{1,5},{2,18},{3,7},{4,20},{5,9},{6,22},{7,11},{8,24},{9,13}... | collective-permute-start | bytes 1572872 | tf_op jit(solution)/shard_map/ppermute | solution.py:270
  94.7 13.1 %collective-permute-start.7 = (bf16[16,2,16,512]{3,2,1,0:T(8,128)(2,1)S(1)}, bf16[16,2,16,512]{3,2,1,0:T(8,128)(2,1)S(1)}, u32[]{:S(2)}, u32[]{:S(2)}) collective-permute-start(bf16[16,2,16,512]{3,2,1,0:T(8,128)(2,1)S(1)} %get-tuple-element.41), channel_id=1, source_target_pairs={{0,48},{1,13},{2,50},{3,15},{4,52},{5,1},{6,54},{7,3},{8,56},{9,5}... | collective-permute-start | bytes 1572872 | tf_op jit(solution)/shard_map/ppermute | solution.py:270

commit v11 on v10

--- a/solution.py
+++ b/solution.py
@@ -47,7 +47,7 @@
 
 
 def with_everyone(pieces):
-    return exchange(pieces, [list(range(lax.axis_size(EVERY)))])
+    return exchange(pieces, [mixed(range(lax.axis_size(EVERY)), 0)])
 
 
 def over_terms(pieces):

time: 124 us -> 124 us (level)
  no operation moved by 1% of the time
where the time goes in v11:
time: 124 us
  blocking collectives  68 us (55%)
  waiting for transfers between devices  22.8 us (18%)
  Pallas kernels  20.4 us (16%)
  starting transfers between devices  11.6 us (9%)
    all_to_all x4, blocking collectives, exchange(): lax.all_to_all(pieces, EVERY, split_axis=0, concat_axis=0, axis_index_gro...  68 us
    ppermute x6, waiting for transfers between devices, along_ring(): return lax.ppermute(value, EVERY, pairs)  21.8 us
    ppermute x6, starting transfers between devices, along_ring(): return lax.ppermute(value, EVERY, pairs)  11.2 us
    pallas_call x2, Pallas kernels, apply_early(): pl.pallas_call(functools.partial(early_kernel, first), out_shape=out, in_...  9.89 us
    pallas_call x2, Pallas kernels, apply_late(): pl.pallas_call(late_kernel, out_shape=jax.ShapeDtypeStruct(begun.shape, F...  7.18 us
  transfers between devices with their start and end apart: 8, of which 7 were waited for; matrix products, arithmetic and copies ran while one was open for 0% of the time, Pallas kernels for 6%

profile of v11, /device:TPU:0, one launch (start us, length us, event | category | flops | bytes accessed | tf_op | source)
XLA Modules:
  0.0 123.5 jit_solution(7173958825807870123)
XLA Ops:
  0.6 0.0 copy-start
  0.7 0.0 copy-start.2
  0.7 5.9 %early_first.1 = (bf16[4,512,512]{2,1,0:T(8,128)(2,1)S(1)}, f32[4,512,512]{2,1,0:T(8,128)S(1)}, bf16[8,512,512]{2,1,0:T(8,128)(2,1)S(1)}, bf16[8,512,512]{2,1,0:T(8,128)(2,1)S(1)}) custom-call(s32[2,4]{1,0:T(2,128)} %bitcast.7, s32[1]{0:T(128)} %bitcast.1.core, bf16[2,512,512]{2,1,0:T(8,128)(2,1)} %wave.3, bf16[8,512,512]{2,1,0:T(8,128)(2,1)} %bitcast.11, ...), custom_call_target="tpu_custom_call" | custom-call | flops 2147483648 | bytes 4194304 | tf_op jit(solution)/shard_map/early_first/pallas_call | solution.py:228
  6.6 0.1 collective-permute-start
  6.7 0.0 copy-done
  6.7 0.0 copy-done.2
  6.7 3.6 %late.2.kept = f32[4,512,512]{2,1,0:T(8,128)S(1)} custom-call(s32[2,4]{1,0:T(2,128)S(1)} %bitcast.8, s32[1]{0:T(128)} %bitcast.1.core, bf16[2,512,512]{2,1,0:T(8,128)(2,1)S(1)} %copy-done, bf16[8,512,512]{2,1,0:T(8,128)(2,1)S(1)} %get-tuple-element.25.lefts.left, ...), custom_call_target="tpu_custom_call", output_to_operand_aliasing={{}: (5, {})} | custom-call | flops 2147483648 | bytes 4194304 | tf_op jit(solution)/shard_map/late/pallas_call | solution.py:242
  10.3 0.0 copy-start.1
  10.3 0.5 collective-permute-done.arrived
  10.8 0.4 pack.2
  11.2 3.2 %collective-permute-start.1 = (bf16[16,2,16,512]{3,2,1,0:T(8,128)(2,1)S(1)}, bf16[16,2,16,512]{3,2,1,0:T(8,128)(2,1)S(1)}, u32[]{:S(2)}, u32[]{:S(2)}) collective-permute-start(bf16[16,2,16,512]{3,2,1,0:T(8,128)(2,1)S(1)} %get-tuple-element.30), channel_id=1, source_target_pairs={{0,32},{1,9},{2,34},{3,11},{4,36},{5,13},{6,38},{7,15},{8,40},{9,1... | collective-permute-start | bytes 1572872 | tf_op jit(solution)/shard_map/ppermute | solution.py:270
  14.5 0.5 collective-permute-start.2
  15.0 2.7 %collective-permute-start.3 = (bf16[16,2,16,512]{3,2,1,0:T(8,128)(2,1)S(1)}, bf16[16,2,16,512]{3,2,1,0:T(8,128)(2,1)S(1)}, u32[]{:S(2)}, u32[]{:S(2)}) collective-permute-start(bf16[16,2,16,512]{3,2,1,0:T(8,128)(2,1)S(1)} %get-tuple-element.32), channel_id=1, source_target_pairs={{0,48},{1,13},{2,50},{3,15},{4,52},{5,1},{6,54},{7,3},{8,56},{9,5}... | collective-permute-start | bytes 1572872 | tf_op jit(solution)/shard_map/ppermute | solution.py:270
  17.7 4.4 %collective-permute-done.1.first = bf16[16,2,16,512]{3,2,1,0:T(8,128)(2,1)S(1)} collective-permute-done((bf16[16,2,16,512]{3,2,1,0:T(8,128)(2,1)S(1)}, bf16[16,2,16,512]{3,2,1,0:T(8,128)(2,1)S(1)}, u32[]{:S(2)}, u32[]{:S(2)}) %collective-permute-start.1) | collective-permute-done | bytes 524320 | tf_op jit(solution)/shard_map/ppermute | solution.py:270
  22.1 5.5 %collective-permute-done.2.second = bf16[16,2,16,512]{3,2,1,0:T(8,128)(2,1)S(1)} collective-permute-done((bf16[16,2,16,512]{3,2,1,0:T(8,128)(2,1)S(1)}, bf16[16,2,16,512]{3,2,1,0:T(8,128)(2,1)S(1)}, u32[]{:S(2)}, u32[]{:S(2)}) %collective-permute-start.2) | collective-permute-done | bytes 524320 | tf_op jit(solution)/shard_map/ppermute | solution.py:270
  27.6 0.2 collective-permute-done.3.third
  27.8 0.2 meet.2
  28.1 17.6 %all_to_all.20.pieces = bf16[16,2,16,512]{3,2,1,0:T(8,128)(2,1)S(1)} all-to-all(bf16[16,2,16,512]{3,2,1,0:T(8,128)(2,1)S(1)} %meet.2), channel_id=1, replica_groups={{8,70,68,74,72,6,12,0,2,78,76,10,4,64,66,14},{24,86,84,90,88,22,28,16,1..., dimensions={0} | all-to-all | bytes 1048576 | tf_op jit(solution)/shard_map/all_to_all | solution.py:44
  45.7 0.0 copy-done.1
  45.7 0.7 first.1
  46.4 15.2 %all_to_all.21.sums = f32[128,1,128]{2,1,0:T(1,128)S(1)} all-to-all(f32[128,1,128]{2,1,0:T(1,128)S(1)} %get-tuple-element.34), channel_id=1, replica_groups={{48,43,108,72,29,14,54,23,124,94,10,44,3,49,83,111,16,95,107,101,110,22..., dimensions={0} | all-to-all | bytes 131072 | tf_op jit(solution)/shard_map/all_to_all | solution.py:44
  61.6 0.6 second.1
  62.2 20.6 %all_to_all.22.vector = bf16[32,2,16,512]{3,2,1,0:T(8,128)(2,1)S(1)} all-to-all(bf16[32,2,16,512]{3,2,1,0:T(8,128)(2,1)S(1)} %second.1), channel_id=1, replica_groups={{0,4,8,12,16,20,24,28,32,36,40,44,48,52,56,60,64,68,72,76,80,84,88,92,9..., dimensions={0} | all-to-all | bytes 2097152 | tf_op jit(solution)/shard_map/all_to_all | solution.py:44
  82.8 4.0 %early.1 = (bf16[4,512,512]{2,1,0:T(8,128)(2,1)S(1)}, f32[4,512,512]{2,1,0:T(8,128)S(1)}) custom-call(s32[2,4]{1,0:T(2,128)S(1)} %bitcast.9, s32[1]{0:T(128)} %bitcast.1.core, bf16[32,2,16,512]{3,2,1,0:T(8,128)(2,1)S(1)} %all_to_all.22.vector, bf16[8,512,512]{2,1,0:T(8,128)(2,1)S(1)} %get-tuple-element.25.lefts.left, ...), custom_call_target="tpu_custom_call" | custom-call | flops 2147483648 | bytes 4194304 | tf_op jit(solution)/shard_map/early/pallas_call | solution.py:228
  86.8 0.3 collective-permute-start.4
  87.0 3.6 %late.3.kept = f32[4,512,512]{2,1,0:T(8,128)S(1)} custom-call(s32[2,4]{1,0:T(2,128)S(1)} %bitcast.10, s32[1]{0:T(128)} %bitcast.1.core, bf16[32,2,16,512]{3,2,1,0:T(8,128)(2,1)S(1)} %all_to_all.22.vector, bf16[8,512,512]{2,1,0:T(8,128)(2,1)S(1)} %get-tuple-element.25.lefts.left, ...), custom_call_target="tpu_custom_call", output_to_operand_aliasing={{}: (5, {})} | custom-call | flops 2147483648 | bytes 4194304 | tf_op jit(solution)/shard_map/late/pallas_call | solution.py:242
  90.6 0.5 collective-permute-done.4.arrived
  91.2 0.4 pack.3
  91.6 1.5 %collective-permute-start.5 = (bf16[16,2,16,512]{3,2,1,0:T(8,128)(2,1)S(1)}, bf16[16,2,16,512]{3,2,1,0:T(8,128)(2,1)S(1)}, u32[]{:S(2)}, u32[]{:S(2)}) collective-permute-start(bf16[16,2,16,512]{3,2,1,0:T(8,128)(2,1)S(1)} %get-tuple-element.39), channel_id=1, source_target_pairs={{0,32},{1,9},{2,34},{3,11},{4,36},{5,13},{6,38},{7,15},{8,40},{9,1... | collective-permute-start | bytes 1572872 | tf_op jit(solution)/shard_map/ppermute | solution.py:270
  93.1 1.4 %collective-permute-start.6 = (bf16[16,2,16,512]{3,2,1,0:T(8,128)(2,1)S(1)}, bf16[16,2,16,512]{3,2,1,0:T(8,128)(2,1)S(1)}, u32[]{:S(2)}, u32[]{:S(2)}) collective-permute-start(bf16[16,2,16,512]{3,2,1,0:T(8,128)(2,1)S(1)} %get-tuple-element.40), channel_id=1, source_target_pairs={{0,16},{1,5},{2,18},{3,7},{4,20},{5,9},{6,22},{7,11},{8,24},{9,13}... | collective-permute-start | bytes 1572872 | tf_op jit(solution)/shard_map/ppermute | solution.py:270
  94.5 1.8 %collective-permute-start.7 = (bf16[16,2,16,512]{3,2,1,0:T(8,128)(2,1)S(1)}, bf16[16,2,16,512]{3,2,1,0:T(8,128)(2,1)S(1)}, u32[]{:S(2)}, u32[]{:S(2)}) collective-permute-start(bf16[16,2,16,512]{3,2,1,0:T(8,128)(2,1)S(1)} %get-tuple-element.41), channel_id=1, source_target_pairs={{0,48},{1,13},{2,50},{3,15},{4,52},{5,1},{6,54},{7,3},{8,56},{9,5}... | collective-permute-start | bytes 1572872 | tf_op jit(solution)/shard_map/ppermute | solution.py:270
  96.3 6.1 %collective-permute-done.5.first = bf16[16,2,16,512]{3,2,1,0:T(8,128)(2,1)S(1)} collective-permute-done((bf16[16,2,16,512]{3,2,1,0:T(8,128)(2,1)S(1)}, bf16[16,2,16,512]{3,2,1,0:T(8,128)(2,1)S(1)}, u32[]{:S(2)}, u32[]{:S(2)}) %collective-permute-start.5) | collective-permute-done | bytes 524320 | tf_op jit(solution)/shard_map/ppermute | solution.py:270
  102.5 5.5 %collective-permute-done.6.second = bf16[16,2,16,512]{3,2,1,0:T(8,128)(2,1)S(1)} collective-permute-done((bf16[16,2,16,512]{3,2,1,0:T(8,128)(2,1)S(1)}, bf16[16,2,16,512]{3,2,1,0:T(8,128)(2,1)S(1)}, u32[]{:S(2)}, u32[]{:S(2)}) %collective-permute-start.6) | collective-permute-done | bytes 524320 | tf_op jit(solution)/shard_map/ppermute | solution.py:270
  108.0 0.0 collective-permute-done.7.third
  108.0 0.2 meet.3
  108.2 14.6 %all_to_all.23.pieces = bf16[16,2,16,512]{3,2,1,0:T(8,128)(2,1)S(1)} all-to-all(bf16[16,2,16,512]{3,2,1,0:T(8,128)(2,1)S(1)} %meet.3), channel_id=1, replica_groups={{8,70,68,74,72,6,12,0,2,78,76,10,4,64,66,14},{24,86,84,90,88,22,28,16,1..., dimensions={0} | all-to-all | bytes 1048576 | tf_op jit(solution)/shard_map/all_to_all | solution.py:44
  122.8 0.7 last.1
Async XLA Ops:
  0.6 6.0 %copy-start = (bf16[2,512,512]{2,1,0:T(8,128)(2,1)S(1)}, bf16[2,512,512]{2,1,0:T(8,128)(2,1)}, u32[]{:S(2)}) copy-start(bf16[2,512,512]{2,1,0:T(8,128)(2,1)} %wave.3) | copy-start | bytes 3145732
  0.7 6.0 %copy-start.2 = (s32[4,2]{0,1:T(2,128)S(1)}, s32[4,2]{0,1:T(2,128)}, u32[]{:S(2)}) copy-start(s32[4,2]{0,1:T(2,128)} %param.8) | copy-start | bytes 100
  6.6 4.2 %collective-permute-start = (bf16[4,512,512]{2,1,0:T(8,128)(2,1)S(1)}, bf16[4,512,512]{2,1,0:T(8,128)(2,1)S(1)}, u32[]{:S(2)}, u32[]{:S(2)}) collective-permute-start(bf16[4,512,512]{2,1,0:T(8,128)(2,1)S(1)} %get-tuple-element.28), channel_id=1, source_target_pairs={{0,1},{1,0},{2,3},{3,2},{4,5},{5,4},{6,7},{7,6},{8,9},{9,8},{10,11... | collective-permute-start | bytes 6291464 | tf_op jit(solution)/shard_map/ppermute | solution.py:408
  10.3 35.4 %copy-start.1 = (f32[2,16,512]{2,1,0:T(8,128)S(1)}, f32[2,16,512]{2,1,0:T(8,128)}, u32[]{:S(2)}) copy-start(f32[2,16,512]{2,1,0:T(8,128)} %precond.3) | copy-start | bytes 196612
  11.2 10.9 %collective-permute-start.1 = (bf16[16,2,16,512]{3,2,1,0:T(8,128)(2,1)S(1)}, bf16[16,2,16,512]{3,2,1,0:T(8,128)(2,1)S(1)}, u32[]{:S(2)}, u32[]{:S(2)}) collective-permute-start(bf16[16,2,16,512]{3,2,1,0:T(8,128)(2,1)S(1)} %get-tuple-element.30), channel_id=1, source_target_pairs={{0,32},{1,9},{2,34},{3,11},{4,36},{5,13},{6,38},{7,15},{8,40},{9,1... | collective-permute-start | bytes 1572872 | tf_op jit(solution)/shard_map/ppermute | solution.py:270
  14.5 13.1 %collective-permute-start.2 = (bf16[16,2,16,512]{3,2,1,0:T(8,128)(2,1)S(1)}, bf16[16,2,16,512]{3,2,1,0:T(8,128)(2,1)S(1)}, u32[]{:S(2)}, u32[]{:S(2)}) collective-permute-start(bf16[16,2,16,512]{3,2,1,0:T(8,128)(2,1)S(1)} %get-tuple-element.31), channel_id=1, source_target_pairs={{0,16},{1,5},{2,18},{3,7},{4,20},{5,9},{6,22},{7,11},{8,24},{9,13}... | collective-permute-start | bytes 1572872 | tf_op jit(solution)/shard_map/ppermute | solution.py:270
  15.0 12.8 %collective-permute-start.3 = (bf16[16,2,16,512]{3,2,1,0:T(8,128)(2,1)S(1)}, bf16[16,2,16,512]{3,2,1,0:T(8,128)(2,1)S(1)}, u32[]{:S(2)}, u32[]{:S(2)}) collective-permute-start(bf16[16,2,16,512]{3,2,1,0:T(8,128)(2,1)S(1)} %get-tuple-element.32), channel_id=1, source_target_pairs={{0,48},{1,13},{2,50},{3,15},{4,52},{5,1},{6,54},{7,3},{8,56},{9,5}... | collective-permute-start | bytes 1572872 | tf_op jit(solution)/shard_map/ppermute | solution.py:270
  86.8 4.4 %collective-permute-start.4 = (bf16[4,512,512]{2,1,0:T(8,128)(2,1)S(1)}, bf16[4,512,512]{2,1,0:T(8,128)(2,1)S(1)}, u32[]{:S(2)}, u32[]{:S(2)}) collective-permute-start(bf16[4,512,512]{2,1,0:T(8,128)(2,1)S(1)} %get-tuple-element.37), channel_id=1, source_target_pairs={{0,1},{1,0},{2,3},{3,2},{4,5},{5,4},{6,7},{7,6},{8,9},{9,8},{10,11... | collective-permute-start | bytes 6291464 | tf_op jit(solution)/shard_map/ppermute | solution.py:408
  91.6 10.9 %collective-permute-start.5 = (bf16[16,2,16,512]{3,2,1,0:T(8,128)(2,1)S(1)}, bf16[16,2,16,512]{3,2,1,0:T(8,128)(2,1)S(1)}, u32[]{:S(2)}, u32[]{:S(2)}) collective-permute-start(bf16[16,2,16,512]{3,2,1,0:T(8,128)(2,1)S(1)} %get-tuple-element.39), channel_id=1, source_target_pairs={{0,32},{1,9},{2,34},{3,11},{4,36},{5,13},{6,38},{7,15},{8,40},{9,1... | collective-permute-start | bytes 1572872 | tf_op jit(solution)/shard_map/ppermute | solution.py:270
  93.1 14.9 %collective-permute-start.6 = (bf16[16,2,16,512]{3,2,1,0:T(8,128)(2,1)S(1)}, bf16[16,2,16,512]{3,2,1,0:T(8,128)(2,1)S(1)}, u32[]{:S(2)}, u32[]{:S(2)}) collective-permute-start(bf16[16,2,16,512]{3,2,1,0:T(8,128)(2,1)S(1)} %get-tuple-element.40), channel_id=1, source_target_pairs={{0,16},{1,5},{2,18},{3,7},{4,20},{5,9},{6,22},{7,11},{8,24},{9,13}... | collective-permute-start | bytes 1572872 | tf_op jit(solution)/shard_map/ppermute | solution.py:270
  94.5 13.5 %collective-permute-start.7 = (bf16[16,2,16,512]{3,2,1,0:T(8,128)(2,1)S(1)}, bf16[16,2,16,512]{3,2,1,0:T(8,128)(2,1)S(1)}, u32[]{:S(2)}, u32[]{:S(2)}) collective-permute-start(bf16[16,2,16,512]{3,2,1,0:T(8,128)(2,1)S(1)} %get-tuple-element.41), channel_id=1, source_target_pairs={{0,48},{1,13},{2,50},{3,15},{4,52},{5,1},{6,54},{7,3},{8,56},{9,5}... | collective-permute-start | bytes 1572872 | tf_op jit(solution)/shard_map/ppermute | solution.py:270

commit v12 on v11

--- a/solution.py
+++ b/solution.py
@@ -121,7 +121,7 @@
 
         @pl.when(touched[slot] == 0)
         def _(slot=slot):
-            totals[slot] = jnp.zeros(totals.shape[1:], F32)
+            totals[slot] = jnp.zeros(totals.shape[1:], totals.dtype)
 
 
 def early_kernel(first, targets, core, vector, left, right, out, kept, *refs):
@@ -170,8 +170,13 @@
     end = jnp.maximum(count, tasks // 2)
     clear(touched)
     run_tasks(targets, order, 0, count, source, lefts, rights, totals, touched, arrive)
-    fill(totals, touched)
-    out[...] = totals[...].astype(BF16)
+    for slot in range(out.shape[0]):
+
+        @pl.when(touched[slot] == 1)
+        def _(slot=slot):
+            out[slot] = totals[slot].astype(BF16)
+
+    fill(out, touched)
     clear(touched)
     run_tasks(targets, order, count, end, source, lefts, rights, kept, touched, arrive)
     if first:

time: 124 us -> 124 us (level)
  blocking collectives: 68 us -> 66.5 us
  waiting for transfers between devices: 22.8 us -> 24.1 us
    all_to_all x4, blocking collectives: 68 us -> 66.5 us  [exchange(): lax.all_to_all(pieces, EVERY, split_axis=0, concat_axis=0, axis_index_gro...]
  transfers between devices with their start and end apart: 8 -> 8, of which waited for: 7 -> 7; matrix products, arithmetic and copies ran while one was open for 0% -> 0% of each run, Pallas kernels for 6% -> 5%
where the time goes in v12:
time: 124 us; the launch traced here: 123 us
  blocking collectives  66.5 us (54%)
  waiting for transfers between devices  24.1 us (19%)
  Pallas kernels  20.6 us (17%)
  starting transfers between devices  11 us (9%)
    all_to_all x4, blocking collectives, exchange(): lax.all_to_all(pieces, EVERY, split_axis=0, concat_axis=0, axis_index_gro...  66.5 us
    ppermute x6, waiting for transfers between devices, along_ring(): return lax.ppermute(value, EVERY, pairs)  22.2 us
    pallas_call x2, Pallas kernels, apply_early(): pl.pallas_call(functools.partial(early_kernel, first), out_shape=out, in_...  11 us
    ppermute x6, starting transfers between devices, along_ring(): return lax.ppermute(value, EVERY, pairs)  10.8 us
    pallas_call x2, Pallas kernels, apply_late(): pl.pallas_call(late_kernel, out_shape=jax.ShapeDtypeStruct(begun.shape, F...  6.35 us
  transfers between devices with their start and end apart: 8, of which 7 were waited for; matrix products, arithmetic and copies ran while one was open for 0% of the time, Pallas kernels for 5%

profile of v12, /device:TPU:0, one launch (start us, length us, event | category | flops | bytes accessed | tf_op | source)
XLA Modules:
  0.0 122.9 jit_solution(5709585825626056724)
XLA Ops:
  0.6 0.0 copy-start
  0.7 0.0 copy-start.2
  0.7 6.5 %early_first.1 = (bf16[4,512,512]{2,1,0:T(8,128)(2,1)S(1)}, f32[4,512,512]{2,1,0:T(8,128)S(1)}, bf16[8,512,512]{2,1,0:T(8,128)(2,1)S(1)}, bf16[8,512,512]{2,1,0:T(8,128)(2,1)S(1)}) custom-call(s32[2,4]{1,0:T(2,128)} %bitcast.7, s32[1]{0:T(128)} %bitcast.1.core, bf16[2,512,512]{2,1,0:T(8,128)(2,1)} %wave.3, bf16[8,512,512]{2,1,0:T(8,128)(2,1)} %bitcast.11, ...), custom_call_target="tpu_custom_call" | custom-call | flops 2147483648 | bytes 4194304 | tf_op jit(solution)/shard_map/early_first/pallas_call | solution.py:233
  7.2 0.1 collective-permute-start
  7.3 0.0 copy-done
  7.3 0.0 copy-done.2
  7.3 3.1 %late.2.kept = f32[4,512,512]{2,1,0:T(8,128)S(1)} custom-call(s32[2,4]{1,0:T(2,128)S(1)} %bitcast.8, s32[1]{0:T(128)} %bitcast.1.core, bf16[2,512,512]{2,1,0:T(8,128)(2,1)S(1)} %copy-done, bf16[8,512,512]{2,1,0:T(8,128)(2,1)S(1)} %get-tuple-element.25.lefts.left, ...), custom_call_target="tpu_custom_call", output_to_operand_aliasing={{}: (5, {})} | custom-call | flops 2147483648 | bytes 4194304 | tf_op jit(solution)/shard_map/late/pallas_call | solution.py:247
  10.4 0.0 copy-start.1
  10.4 1.0 collective-permute-done.arrived
  11.4 0.4 pack.2
  11.9 3.4 %collective-permute-start.1 = (bf16[16,2,16,512]{3,2,1,0:T(8,128)(2,1)S(1)}, bf16[16,2,16,512]{3,2,1,0:T(8,128)(2,1)S(1)}, u32[]{:S(2)}, u32[]{:S(2)}) collective-permute-start(bf16[16,2,16,512]{3,2,1,0:T(8,128)(2,1)S(1)} %get-tuple-element.30), channel_id=1, source_target_pairs={{0,32},{1,9},{2,34},{3,11},{4,36},{5,13},{6,38},{7,15},{8,40},{9,1... | collective-permute-start | bytes 1572872 | tf_op jit(solution)/shard_map/ppermute | solution.py:275
  15.3 0.4 collective-permute-start.2
  15.7 2.8 %collective-permute-start.3 = (bf16[16,2,16,512]{3,2,1,0:T(8,128)(2,1)S(1)}, bf16[16,2,16,512]{3,2,1,0:T(8,128)(2,1)S(1)}, u32[]{:S(2)}, u32[]{:S(2)}) collective-permute-start(bf16[16,2,16,512]{3,2,1,0:T(8,128)(2,1)S(1)} %get-tuple-element.32), channel_id=1, source_target_pairs={{0,48},{1,13},{2,50},{3,15},{4,52},{5,1},{6,54},{7,3},{8,56},{9,5}... | collective-permute-start | bytes 1572872 | tf_op jit(solution)/shard_map/ppermute | solution.py:275
  18.5 4.2 %collective-permute-done.1.first = bf16[16,2,16,512]{3,2,1,0:T(8,128)(2,1)S(1)} collective-permute-done((bf16[16,2,16,512]{3,2,1,0:T(8,128)(2,1)S(1)}, bf16[16,2,16,512]{3,2,1,0:T(8,128)(2,1)S(1)}, u32[]{:S(2)}, u32[]{:S(2)}) %collective-permute-start.1) | collective-permute-done | bytes 524320 | tf_op jit(solution)/shard_map/ppermute | solution.py:275
  22.7 5.5 %collective-permute-done.2.second = bf16[16,2,16,512]{3,2,1,0:T(8,128)(2,1)S(1)} collective-permute-done((bf16[16,2,16,512]{3,2,1,0:T(8,128)(2,1)S(1)}, bf16[16,2,16,512]{3,2,1,0:T(8,128)(2,1)S(1)}, u32[]{:S(2)}, u32[]{:S(2)}) %collective-permute-start.2) | collective-permute-done | bytes 524320 | tf_op jit(solution)/shard_map/ppermute | solution.py:275
  28.3 0.2 collective-permute-done.3.third
  28.5 0.2 meet.2
  28.7 16.9 %all_to_all.20.pieces = bf16[16,2,16,512]{3,2,1,0:T(8,128)(2,1)S(1)} all-to-all(bf16[16,2,16,512]{3,2,1,0:T(8,128)(2,1)S(1)} %meet.2), channel_id=1, replica_groups={{8,70,68,74,72,6,12,0,2,78,76,10,4,64,66,14},{24,86,84,90,88,22,28,16,1..., dimensions={0} | all-to-all | bytes 1048576 | tf_op jit(solution)/shard_map/all_to_all | solution.py:44
  45.6 0.0 copy-done.1
  45.6 0.7 first.1
  46.3 15.5 %all_to_all.21.sums = f32[128,1,128]{2,1,0:T(1,128)S(1)} all-to-all(f32[128,1,128]{2,1,0:T(1,128)S(1)} %get-tuple-element.34), channel_id=1, replica_groups={{48,43,108,72,29,14,54,23,124,94,10,44,3,49,83,111,16,95,107,101,110,22..., dimensions={0} | all-to-all | bytes 131072 | tf_op jit(solution)/shard_map/all_to_all | solution.py:44
  61.9 0.6 second.1
  62.5 20.6 %all_to_all.22.vector = bf16[32,2,16,512]{3,2,1,0:T(8,128)(2,1)S(1)} all-to-all(bf16[32,2,16,512]{3,2,1,0:T(8,128)(2,1)S(1)} %second.1), channel_id=1, replica_groups={{0,4,8,12,16,20,24,28,32,36,40,44,48,52,56,60,64,68,72,76,80,84,88,92,9..., dimensions={0} | all-to-all | bytes 2097152 | tf_op jit(solution)/shard_map/all_to_all | solution.py:44
  83.0 4.4 %early.1 = (bf16[4,512,512]{2,1,0:T(8,128)(2,1)S(1)}, f32[4,512,512]{2,1,0:T(8,128)S(1)}) custom-call(s32[2,4]{1,0:T(2,128)S(1)} %bitcast.9, s32[1]{0:T(128)} %bitcast.1.core, bf16[32,2,16,512]{3,2,1,0:T(8,128)(2,1)S(1)} %all_to_all.22.vector, bf16[8,512,512]{2,1,0:T(8,128)(2,1)S(1)} %get-tuple-element.25.lefts.left, ...), custom_call_target="tpu_custom_call" | custom-call | flops 2147483648 | bytes 4194304 | tf_op jit(solution)/shard_map/early/pallas_call | solution.py:233
  87.5 0.1 collective-permute-start.4
  87.6 3.3 %late.3.kept = f32[4,512,512]{2,1,0:T(8,128)S(1)} custom-call(s32[2,4]{1,0:T(2,128)S(1)} %bitcast.10, s32[1]{0:T(128)} %bitcast.1.core, bf16[32,2,16,512]{3,2,1,0:T(8,128)(2,1)S(1)} %all_to_all.22.vector, bf16[8,512,512]{2,1,0:T(8,128)(2,1)S(1)} %get-tuple-element.25.lefts.left, ...), custom_call_target="tpu_custom_call", output_to_operand_aliasing={{}: (5, {})} | custom-call | flops 2147483648 | bytes 4194304 | tf_op jit(solution)/shard_map/late/pallas_call | solution.py:247
  90.9 0.9 collective-permute-done.4.arrived
  91.7 0.4 pack.3
  92.2 0.9 collective-permute-start.5
  93.1 2.2 %collective-permute-start.6 = (bf16[16,2,16,512]{3,2,1,0:T(8,128)(2,1)S(1)}, bf16[16,2,16,512]{3,2,1,0:T(8,128)(2,1)S(1)}, u32[]{:S(2)}, u32[]{:S(2)}) collective-permute-start(bf16[16,2,16,512]{3,2,1,0:T(8,128)(2,1)S(1)} %get-tuple-element.40), channel_id=1, source_target_pairs={{0,16},{1,5},{2,18},{3,7},{4,20},{5,9},{6,22},{7,11},{8,24},{9,13}... | collective-permute-start | bytes 1572872 | tf_op jit(solution)/shard_map/ppermute | solution.py:275
  95.3 1.0 collective-permute-start.7
  96.3 6.7 %collective-permute-done.5.first = bf16[16,2,16,512]{3,2,1,0:T(8,128)(2,1)S(1)} collective-permute-done((bf16[16,2,16,512]{3,2,1,0:T(8,128)(2,1)S(1)}, bf16[16,2,16,512]{3,2,1,0:T(8,128)(2,1)S(1)}, u32[]{:S(2)}, u32[]{:S(2)}) %collective-permute-start.5) | collective-permute-done | bytes 524320 | tf_op jit(solution)/shard_map/ppermute | solution.py:275
  103.0 5.5 %collective-permute-done.6.second = bf16[16,2,16,512]{3,2,1,0:T(8,128)(2,1)S(1)} collective-permute-done((bf16[16,2,16,512]{3,2,1,0:T(8,128)(2,1)S(1)}, bf16[16,2,16,512]{3,2,1,0:T(8,128)(2,1)S(1)}, u32[]{:S(2)}, u32[]{:S(2)}) %collective-permute-start.6) | collective-permute-done | bytes 524320 | tf_op jit(solution)/shard_map/ppermute | solution.py:275
  108.5 0.0 collective-permute-done.7.third
  108.5 0.2 meet.3
  108.8 13.5 %all_to_all.23.pieces = bf16[16,2,16,512]{3,2,1,0:T(8,128)(2,1)S(1)} all-to-all(bf16[16,2,16,512]{3,2,1,0:T(8,128)(2,1)S(1)} %meet.3), channel_id=1, replica_groups={{8,70,68,74,72,6,12,0,2,78,76,10,4,64,66,14},{24,86,84,90,88,22,28,16,1..., dimensions={0} | all-to-all | bytes 1048576 | tf_op jit(solution)/shard_map/all_to_all | solution.py:44
  122.2 0.7 last.1
Async XLA Ops:
  0.6 6.7 %copy-start = (bf16[2,512,512]{2,1,0:T(8,128)(2,1)S(1)}, bf16[2,512,512]{2,1,0:T(8,128)(2,1)}, u32[]{:S(2)}) copy-start(bf16[2,512,512]{2,1,0:T(8,128)(2,1)} %wave.3) | copy-start | bytes 3145732
  0.7 6.7 %copy-start.2 = (s32[4,2]{0,1:T(2,128)S(1)}, s32[4,2]{0,1:T(2,128)}, u32[]{:S(2)}) copy-start(s32[4,2]{0,1:T(2,128)} %param.8) | copy-start | bytes 100
  7.2 4.2 %collective-permute-start = (bf16[4,512,512]{2,1,0:T(8,128)(2,1)S(1)}, bf16[4,512,512]{2,1,0:T(8,128)(2,1)S(1)}, u32[]{:S(2)}, u32[]{:S(2)}) collective-permute-start(bf16[4,512,512]{2,1,0:T(8,128)(2,1)S(1)} %get-tuple-element.28), channel_id=1, source_target_pairs={{0,1},{1,0},{2,3},{3,2},{4,5},{5,4},{6,7},{7,6},{8,9},{9,8},{10,11... | collective-permute-start | bytes 6291464 | tf_op jit(solution)/shard_map/ppermute | solution.py:413
  10.4 35.2 %copy-start.1 = (f32[2,16,512]{2,1,0:T(8,128)S(1)}, f32[2,16,512]{2,1,0:T(8,128)}, u32[]{:S(2)}) copy-start(f32[2,16,512]{2,1,0:T(8,128)} %precond.3) | copy-start | bytes 196612
  11.9 10.9 %collective-permute-start.1 = (bf16[16,2,16,512]{3,2,1,0:T(8,128)(2,1)S(1)}, bf16[16,2,16,512]{3,2,1,0:T(8,128)(2,1)S(1)}, u32[]{:S(2)}, u32[]{:S(2)}) collective-permute-start(bf16[16,2,16,512]{3,2,1,0:T(8,128)(2,1)S(1)} %get-tuple-element.30), channel_id=1, source_target_pairs={{0,32},{1,9},{2,34},{3,11},{4,36},{5,13},{6,38},{7,15},{8,40},{9,1... | collective-permute-start | bytes 1572872 | tf_op jit(solution)/shard_map/ppermute | solution.py:275
  15.3 13.0 %collective-permute-start.2 = (bf16[16,2,16,512]{3,2,1,0:T(8,128)(2,1)S(1)}, bf16[16,2,16,512]{3,2,1,0:T(8,128)(2,1)S(1)}, u32[]{:S(2)}, u32[]{:S(2)}) collective-permute-start(bf16[16,2,16,512]{3,2,1,0:T(8,128)(2,1)S(1)} %get-tuple-element.31), channel_id=1, source_target_pairs={{0,16},{1,5},{2,18},{3,7},{4,20},{5,9},{6,22},{7,11},{8,24},{9,13}... | collective-permute-start | bytes 1572872 | tf_op jit(solution)/shard_map/ppermute | solution.py:275
  15.7 12.8 %collective-permute-start.3 = (bf16[16,2,16,512]{3,2,1,0:T(8,128)(2,1)S(1)}, bf16[16,2,16,512]{3,2,1,0:T(8,128)(2,1)S(1)}, u32[]{:S(2)}, u32[]{:S(2)}) collective-permute-start(bf16[16,2,16,512]{3,2,1,0:T(8,128)(2,1)S(1)} %get-tuple-element.32), channel_id=1, source_target_pairs={{0,48},{1,13},{2,50},{3,15},{4,52},{5,1},{6,54},{7,3},{8,56},{9,5}... | collective-permute-start | bytes 1572872 | tf_op jit(solution)/shard_map/ppermute | solution.py:275
  87.5 4.2 %collective-permute-start.4 = (bf16[4,512,512]{2,1,0:T(8,128)(2,1)S(1)}, bf16[4,512,512]{2,1,0:T(8,128)(2,1)S(1)}, u32[]{:S(2)}, u32[]{:S(2)}) collective-permute-start(bf16[4,512,512]{2,1,0:T(8,128)(2,1)S(1)} %get-tuple-element.37), channel_id=1, source_target_pairs={{0,1},{1,0},{2,3},{3,2},{4,5},{5,4},{6,7},{7,6},{8,9},{9,8},{10,11... | collective-permute-start | bytes 6291464 | tf_op jit(solution)/shard_map/ppermute | solution.py:413
  92.2 10.9 %collective-permute-start.5 = (bf16[16,2,16,512]{3,2,1,0:T(8,128)(2,1)S(1)}, bf16[16,2,16,512]{3,2,1,0:T(8,128)(2,1)S(1)}, u32[]{:S(2)}, u32[]{:S(2)}) collective-permute-start(bf16[16,2,16,512]{3,2,1,0:T(8,128)(2,1)S(1)} %get-tuple-element.39), channel_id=1, source_target_pairs={{0,32},{1,9},{2,34},{3,11},{4,36},{5,13},{6,38},{7,15},{8,40},{9,1... | collective-permute-start | bytes 1572872 | tf_op jit(solution)/shard_map/ppermute | solution.py:275
  93.1 15.5 %collective-permute-start.6 = (bf16[16,2,16,512]{3,2,1,0:T(8,128)(2,1)S(1)}, bf16[16,2,16,512]{3,2,1,0:T(8,128)(2,1)S(1)}, u32[]{:S(2)}, u32[]{:S(2)}) collective-permute-start(bf16[16,2,16,512]{3,2,1,0:T(8,128)(2,1)S(1)} %get-tuple-element.40), channel_id=1, source_target_pairs={{0,16},{1,5},{2,18},{3,7},{4,20},{5,9},{6,22},{7,11},{8,24},{9,13}... | collective-permute-start | bytes 1572872 | tf_op jit(solution)/shard_map/ppermute | solution.py:275
  95.3 13.2 %collective-permute-start.7 = (bf16[16,2,16,512]{3,2,1,0:T(8,128)(2,1)S(1)}, bf16[16,2,16,512]{3,2,1,0:T(8,128)(2,1)S(1)}, u32[]{:S(2)}, u32[]{:S(2)}) collective-permute-start(bf16[16,2,16,512]{3,2,1,0:T(8,128)(2,1)S(1)} %get-tuple-element.41), channel_id=1, source_target_pairs={{0,48},{1,13},{2,50},{3,15},{4,52},{5,1},{6,54},{7,3},{8,56},{9,5}... | collective-permute-start | bytes 1572872 | tf_op jit(solution)/shard_map/ppermute | solution.py:275
